TPU v7x, 32 devices: a whole 2x2x4 slice. The times are simulated.
32 devices in a mesh: dp: 4 (over z), sh: 8 (over y, x, core).
Axes of the slice: x: 2, y: 2, z: 4, core: 2. Of those that a mesh axis runs over, the one named last changes fastest.
Arguments:
- k_prefill: bfloat16 [32, 4352, 8, 128], P('dp', None, 'sh'), parts along dimension 0
- v_prefill: bfloat16 [32, 4352, 8, 128], P('dp', None, 'sh'), parts along dimension 0
- lengths: int32 [32], P('dp'), parts along dimension 0
- residual: bfloat16 [32, 4096], P(('dp', 'sh')), parts along dimension 0
- norm_gain: bfloat16 [4096], replicated
- w_query: bfloat16 [4096, 4096], replicated
- w_key: bfloat16 [4096, 1024], replicated
- w_value: bfloat16 [4096, 1024], replicated
- w_out: bfloat16 [4096, 4096], replicated
Outputs:
- output 1: bfloat16 [32, 4096], P(('dp', 'sh')), parts along dimension 0
- output 2: bfloat16 [32, 4096, 8, 128], P(('dp', 'sh')), parts along dimension 0
- output 3: bfloat16 [32, 4096, 8, 128], P(('dp', 'sh')), parts along dimension 0
There are 4 independent parts. A program takes and returns all parts, laid end to end along the dimension named above; an argument that names none is the same for every part.
All inputs are finite; a program needn't handle non-finite values.
Results may differ from a plain program's by a relative error of at most 0.00421.
Values are sent between devices in bfloat16 or wider.
A program may use at most 1 GiB of HBM per device.

v0:
```python
import jax
import jax.numpy as jnp
from jax import lax
from jax.sharding import PartitionSpec as P

WINDOW = 4096
THETA = 10000.0
EPS = 1e-5


def rolling_rows(prefill, lengths):
    def one_row(row_vals, row_len):
        first_pos = jnp.maximum(row_len - WINDOW, 0)
        win_vals = lax.dynamic_slice_in_dim(row_vals, first_pos, WINDOW, axis=0)
        positions = first_pos + jnp.arange(WINDOW, dtype=jnp.int32)
        win_vals = jnp.where((positions < row_len)[:, None, None], win_vals, jnp.zeros((), win_vals.dtype))
        doubled = jnp.concatenate([win_vals, win_vals], axis=0)
        return lax.dynamic_slice_in_dim(doubled, WINDOW - first_pos % WINDOW, WINDOW, axis=0)
    return jax.vmap(one_row)(prefill, lengths)


def rotate(heads, positions):
    head_dim = heads.shape[-1]
    half_dim = head_dim // 2
    inv_freq = THETA ** (-2.0 * jnp.arange(half_dim, dtype=jnp.float32) / head_dim)
    angles = positions.astype(jnp.float32).reshape(positions.shape + (1,) * (heads.ndim - 1)) * inv_freq
    cos_part = jnp.cos(angles)
    sin_part = jnp.sin(angles)
    first_half = heads[..., :half_dim].astype(jnp.float32)
    second_half = heads[..., half_dim:].astype(jnp.float32)
    return jnp.concatenate([first_half * cos_part - second_half * sin_part, second_half * cos_part + first_half * sin_part], axis=-1).astype(jnp.bfloat16)


def decode_rows(residual, lengths, k_cache, v_cache, norm_gain, w_query, w_key, w_value, w_out):
    num_rows = residual.shape[0]
    kv_heads = k_cache.shape[2]
    head_dim = k_cache.shape[3]
    q_group = w_query.shape[1] // (kv_heads * head_dim)
    resid_f32 = residual.astype(jnp.float32)
    inv_rms = lax.rsqrt(jnp.mean(resid_f32 * resid_f32, axis=-1, keepdims=True) + EPS)
    normed = (resid_f32 * inv_rms * norm_gain.astype(jnp.float32)).astype(jnp.bfloat16)
    q_heads = jnp.dot(normed, w_query, preferred_element_type=jnp.float32).astype(jnp.bfloat16).reshape(num_rows, kv_heads, q_group, head_dim)
    k_new = jnp.dot(normed, w_key, preferred_element_type=jnp.float32).astype(jnp.bfloat16).reshape(num_rows, kv_heads, head_dim)
    v_new = jnp.dot(normed, w_value, preferred_element_type=jnp.float32).astype(jnp.bfloat16).reshape(num_rows, kv_heads, head_dim)
    q_heads = rotate(q_heads, lengths)
    k_new = rotate(k_new, lengths)
    slot_ids = jnp.arange(WINDOW, dtype=jnp.int32)
    new_slot = (slot_ids[None, :] == (lengths % WINDOW)[:, None])[:, :, None, None]
    k_cache = jnp.where(new_slot, k_new[:, None], k_cache)
    v_cache = jnp.where(new_slot, v_new[:, None], v_cache)
    live_slot = (lengths[:, None] - jnp.remainder(lengths[:, None] - slot_ids[None, :], WINDOW)) >= 0
    scores = jnp.einsum('rkgd,rwkd->rkgw', q_heads, k_cache, preferred_element_type=jnp.float32) / head_dim ** 0.5
    scores = jnp.where(live_slot[:, None, None, :], scores, -jnp.inf)
    exp_scores = jnp.exp(scores - jnp.max(scores, axis=-1, keepdims=True))
    weights = (exp_scores / jnp.sum(exp_scores, axis=-1, keepdims=True)).astype(jnp.bfloat16)
    attn_out = jnp.einsum('rkgw,rwkd->rkgd', weights, v_cache, preferred_element_type=jnp.float32).astype(jnp.bfloat16).reshape(num_rows, kv_heads * q_group * head_dim)
    resid_out = (resid_f32 + jnp.dot(attn_out, w_out, preferred_element_type=jnp.float32)).astype(jnp.bfloat16)
    return resid_out, k_cache, v_cache


def solution(mesh):
    head_spec = P('dp', None, 'sh', None)
    row_spec = P(('dp', 'sh'))
    full_spec = P(None, None)

    def per_device(k_prefill, v_prefill, lengths, residual, norm_gain, w_query, w_key, w_value, w_out):
        num_rows = residual.shape[0]
        my_lengths = lax.dynamic_slice_in_dim(lengths, lax.axis_index('sh') * num_rows, num_rows)
        k_rows = lax.all_to_all(k_prefill, 'sh', 0, 2, tiled=True)
        v_rows = lax.all_to_all(v_prefill, 'sh', 0, 2, tiled=True)
        k_cache = rolling_rows(k_rows, my_lengths)
        v_cache = rolling_rows(v_rows, my_lengths)
        return decode_rows(residual, my_lengths, k_cache, v_cache, norm_gain, w_query, w_key, w_value, w_out)
    return jax.shard_map(per_device, mesh=mesh, in_specs=(head_spec, head_spec, P('dp'), P(('dp', 'sh'), None), P(None), full_spec, full_spec, full_spec, full_spec), out_specs=(P(('dp', 'sh'), None), row_spec, row_spec), check_vma=False)
```

profile of v0, /device:TPU:0, one launch (start us, length us, event | category | flops | bytes accessed | tf_op | source)
XLA Modules:
  0.0 376.2 jit_solution(14820132361320436251)
XLA Ops:
  0.6 106.0 %all_to_all.36 = bf16[8,4352,1,128]{3,1,2,0:T(8,128)(2,1)} all-to-all(bf16[8,4352,1,128]{3,1,2,0:T(8,128)(2,1)} %param.9), channel_id=1, replica_groups=mesh['dp'=4,'sh'=8] {'sh'}, dimensions={0} | all-to-all | bytes 17825792 | tf_op jit(solution)/shard_map/all_to_all | solution.py:69
  106.6 5.1 %all-to-all-start.1 = ((bf16[8,4352,1,128]{3,1,2,0:T(8,128)(2,1)}), bf16[8,4352,1,128]{3,1,2,0:T(8,128)(2,1)}, u32[]{:S(2)}, u32[]{:S(2)}) async-start(bf16[8,4352,1,128]{3,1,2,0:T(8,128)(2,1)} %param.10), calls=%async_computation.1 | async-start | bytes 17825792 | tf_op jit(solution)/shard_map/all_to_all | solution.py:70
  111.8 0.6 dynamic_slice.3
  115.6 0.6 multiply_reduce_fusion
  117.0 12.8 %fusion.31 = f32[1,4096]{1,0:T(1,128)S(1)} fusion(bf16[4096,4096]{1,0:T(8,128)(2,1)} %param.14, f32[1,4096]{1,0:T(1,128)S(1)} %bitcast.54, bf16[1,4096]{1,0:T(2,128)(2,1)S(1)} %copy-done, f32[]{:T(128)S(6)} %rsqrt.4), kind=kOutput, calls=%fused_computation.44 | convolution fusion | flops 33570816 | bytes 33595396 | tf_op jit(solution)/shard_map/dot_general | solution.py:42
  129.8 0.1 fusion.50
  129.9 0.0 slice-start.1
  129.9 4.7 %fusion.29 = f32[1,1024]{1,0:T(1,128)S(1)} fusion(bf16[4096,1024]{1,0:T(8,128)(2,1)} %param.15, f32[1,4096]{1,0:T(1,128)S(1)} %bitcast.55, bf16[1,4096]{1,0:T(2,128)(2,1)S(1)} %copy-done, f32[]{:T(128)S(6)} %rsqrt.4), kind=kOutput, calls=%fused_computation.42 | convolution fusion | flops 8404992 | bytes 8417284 | tf_op jit(solution)/shard_map/dot_general | solution.py:43
  134.6 0.1 fusion.49
  134.7 0.1 pad_maximum_fusion
  134.8 0.7 fusion.26
  135.5 0.7 add_compare_fusion
  136.1 0.0 slice-done
  136.2 1.2 fusion.27
  137.4 0.1 fusion.40
  137.5 9.0 %constant_dynamic-slice_fusion.1 = bf16[8,4096,1,128]{3,1,2,0:T(8,128)(2,1)} fusion(bf16[8,4352,1,128]{3,1,2,0:T(8,128)(2,1)} %all_to_all.36, s32[]{:T(128)} %bitcast.12), kind=kLoop, calls=%fused_computation.75 | loop fusion | bytes 16777220
  146.4 65.0 %all-to-all-done.1 = bf16[8,4352,1,128]{3,1,2,0:T(8,128)(2,1)} async-done(((bf16[8,4352,1,128]{3,1,2,0:T(8,128)(2,1)}), bf16[8,4352,1,128]{3,1,2,0:T(8,128)(2,1)}, u32[]{:S(2)}, u32[]{:S(2)}) %all-to-all-start.1) | async-done | bytes 8912928 | tf_op jit(solution)/shard_map/all_to_all | solution.py:70
  211.4 8.9 %constant_dynamic-slice_fusion = bf16[8,4096,1,128]{3,1,2,0:T(8,128)(2,1)} fusion(bf16[8,4352,1,128]{3,1,2,0:T(8,128)(2,1)} %all-to-all-done.1, s32[]{:T(128)} %bitcast.12), kind=kLoop, calls=%fused_computation.74 | loop fusion | bytes 16777220
  220.3 35.0 %bitcast_select_fusion.1 = (bf16[1,4096,8,128]{3,2,1,0:T(8,128)(2,1)S(1)}, bf16[1,4096,8,128]{3,2,1,0:T(8,128)(2,1)S(1)}) fusion(bf16[8,4096,1,128]{3,1,2,0:T(8,128)(2,1)} %constant_dynamic-slice_fusion.1, pred[4096]{0:T(1024)(128)(4,1)S(1)} %add_compare_fusion, bf16[8,4096,1,128]{3,1,2,0:T(8,128)(2,1)} %constant_dynamic-slice_fusion), kind=kLoop, calls=%fused_computation.8 | loop fusion | flops 8388608 | bytes 33558528 | tf_op jit(solution)/shard_map/vmap(jit(_where))/select_n | solution.py:16
  255.4 48.0 %bitcast_select_fusion.3 = (bf16[4096,8,128]{2,1,0:T(8,128)(2,1)}, bf16[4096,8,128]{2,1,0:T(8,128)(2,1)}) fusion(pred[4096]{0:T(1024)(128)(4,1)S(1)} %iota_compare_fusion, bf16[8,128]{1,0:T(8,128)(2,1)S(1)} %pad_maximum_fusion, s32[]{:T(128)} %bitcast.16, bf16[1,4096,8,128]{3,2,1,0:T(8,128)(2,1)S(1)} %get-tuple-element.53, ...), kind=kLoop, calls=%fused_computation.10 | loop fusion | flops 16777216 | bytes 33562628 | tf_op jit(solution)/shard_map/jit(_where)/select_n | solution.py:49
  303.3 47.8 %broadcast_select_fusion = (bf16[1,4096,8,128]{3,2,1,0:T(8,128)(2,1)}, bf16[1,4096,8,128]{3,2,1,0:T(8,128)(2,1)}) fusion(pred[4096]{0:T(1024)(128)(4,1)S(1)} %iota_compare_fusion, bf16[8,128]{1,0:T(8,128)(2,1)S(1)} %convert_bitcast_fusion, s32[]{:T(128)} %bitcast.16, bf16[1,4096,8,128]{3,2,1,0:T(8,128)(2,1)S(1)} %get-tuple-element.54, ...), kind=kLoop, calls=%fused_computation.15 | loop fusion | flops 16777216 | bytes 33562628 | tf_op jit(solution)/shard_map/jit(_where)/select_n | solution.py:50
  351.1 5.9 %fusion.53 = (f32[8,4]{1,0:T(8,128)S(1)}, f32[8,4,4096]{2,1,0:T(4,128)S(1)}) fusion(bf16[4096,8,128]{2,1,0:T(8,128)(2,1)} %get-tuple-element.51, pred[4096]{0:T(1024)(128)(4,1)S(1)} %fusion.26, bf16[8,4,64]{2,1,0:T(4,128)(2,1)S(1)} %get-tuple-element.48, bf16[8,4,64]{2,1,0:T(4,128)(2,1)S(1)} %get-tuple-element.47), kind=kOutput, calls=%fused_computation.80 | convolution fusion | flops 34099200 | bytes 8925312 | tf_op jit(solution)/shard_map/sub | solution.py:54
  357.0 5.7 %fusion.16 = bf16[8,4,128]{2,1,0:T(4,128)(2,1)S(1)} fusion(bf16[4096,8,128]{2,1,0:T(8,128)(2,1)} %get-tuple-element.52, f32[8,4,4096]{2,1,0:T(4,128)S(1)} %get-tuple-element.58, f32[8,4]{1,0:T(8,128)S(1)} %get-tuple-element.57), kind=kOutput, calls=%fused_computation.23 | convolution fusion | flops 33820672 | bytes 8921216 | tf_op jit(solution)/shard_map/rkgw,rwkd->rkgd/dot_general | solution.py:56
  362.7 13.4 %fusion.15 = bf16[1,4096]{1,0:T(2,128)(2,1)} fusion(bf16[4096,1]{0,1:T(2,128)(2,1)S(1)} %reshape.377, bf16[4096,4096]{1,0:T(8,128)(2,1)} %param.17, bf16[1,4096]{1,0:T(2,128)(2,1)S(1)} %copy-done), kind=kOutput, calls=%fused_computation.22 | convolution fusion | flops 33566720 | bytes 33579008 | tf_op jit(solution)/shard_map/dot_general | solution.py:57
  (15 shorter events, 0.1 us)
Async XLA Ops:
  106.6 5.1 %copy-start.2 = (s32[8]{0:T(128)S(1)}, s32[8]{0:T(128)}, u32[]{:S(2)}) copy-start(s32[8]{0:T(128)} %param.11) | copy-start | bytes 100
  106.6 9.0 %copy-start.1 = (bf16[4096]{0:T(1024)(128)(2,1)S(1)}, bf16[4096]{0:T(1024)(128)(2,1)}, u32[]{:S(2)}) copy-start(bf16[4096]{0:T(1024)(128)(2,1)} %param.13) | copy-start | bytes 24580
  106.6 9.0 %copy-start = (bf16[1,4096]{1,0:T(2,128)(2,1)S(1)}, bf16[1,4096]{1,0:T(2,128)(2,1)}, u32[]{:S(2)}) copy-start(bf16[1,4096]{1,0:T(2,128)(2,1)} %param.12) | copy-start | bytes 24580
  106.6 104.7 %all-to-all-start.1 = ((bf16[8,4352,1,128]{3,1,2,0:T(8,128)(2,1)}), bf16[8,4352,1,128]{3,1,2,0:T(8,128)(2,1)}, u32[]{:S(2)}, u32[]{:S(2)}) async-start(bf16[8,4352,1,128]{3,1,2,0:T(8,128)(2,1)} %param.10), calls=%async_computation.1 | async-start | bytes 17825792 | tf_op jit(solution)/shard_map/all_to_all | solution.py:70
  129.8 6.3 %slice-start = ((s8[8388608]{0:T(1024)(128)(4,1)}), s8[4194304]{0:T(1024)(128)(4,1)S(1)}, s32[]{:S(2)}) async-start(s8[8388608]{0:T(1024)(128)(4,1)} %bitcast.52), calls=%async_computation.2 | async-start | bytes 8388608
  129.9 6.3 %slice-start.1 = ((s8[8388608]{0:T(1024)(128)(4,1)}), s8[4194304]{0:T(1024)(128)(4,1)S(1)}, s32[]{:S(2)}) async-start(s8[8388608]{0:T(1024)(128)(4,1)} %bitcast.52), calls=%async_computation.3 | async-start | bytes 8388608
where the time goes:
time: 377 us; the launch traced here: 376 us
  other arithmetic  133 us (35%)
  blocking collectives  106 us (28%)
  waiting for transfers between devices  65 us (17%)
  matrix products  43.8 us (12%)
  local copies, waits for them, and re-layouts  18.5 us (5%)
  starting transfers between devices  5.12 us (1%)
  between operations  4.73 us (1%)
    all_to_all x1, blocking collectives, per_device(): k_rows = lax.all_to_all(k_prefill, 'sh', 0, 2, tiled=True)  106 us
    all_to_all x1, waiting for transfers between devices, per_device(): v_rows = lax.all_to_all(v_prefill, 'sh', 0, 2, tiled=True)  65 us
    select_n x1, other arithmetic, decode_rows(): k_cache = jnp.where(new_slot, k_new[:, None], k_cache)  48 us
    select_n x1, other arithmetic, decode_rows(): v_cache = jnp.where(new_slot, v_new[:, None], v_cache)  47.8 us
    select_n x1, other arithmetic, one_row(): jnp.where((positions < row_len)[:, None, None], win_vals, jnp.zeros((), w...  35 us
    unnamed x12, local copies, waits for them, and re-layouts  17.9 us
    dot_general x1, matrix products, decode_rows(): jnp.dot(attn_out, w_out, preferred_element_type=jnp.float32)  13.4 us
    dot_general x1, matrix products, decode_rows(): jnp.dot(normed, w_query, preferred_element_type=jnp.float32)  12.8 us
  transfers between devices with their start and end apart: 1, of which 1 were waited for; matrix products, arithmetic and copies ran while one was open for 8% of the time, Pallas kernels for 0%

commit v1 on v0

v1 whole, which is shorter than its diff:
```python
import functools

import jax
import jax.numpy as jnp
from jax import lax
from jax.experimental import pallas as pl
from jax.experimental.pallas import tpu as pltpu
from jax.sharding import PartitionSpec as P


WINDOW = 4096
THETA = 10000.0
EPS = 1e-5
PEERS = 8
GROUP = 32
WRAP = 256
CHUNKS = ((256, 512), (768, 1280), (2048, 1280), (3328, 512), (3840, 256))
BLOCK = 256
ORDER = (6, 4, 2, 7, 5, 3, 1)
MIB = 1024 * 1024


def rotate(heads, positions):
    head_dim = heads.shape[-1]
    half_dim = head_dim // 2
    inv_freq = THETA ** (-2.0 * jnp.arange(half_dim, dtype=jnp.float32) / head_dim)
    angles = positions.astype(jnp.float32).reshape(positions.shape + (1,) * (heads.ndim - 1)) * inv_freq
    cos_part = jnp.cos(angles)
    sin_part = jnp.sin(angles)
    first_half = heads[..., :half_dim].astype(jnp.float32)
    second_half = heads[..., half_dim:].astype(jnp.float32)
    return jnp.concatenate([first_half * cos_part - second_half * sin_part, second_half * cos_part + first_half * sin_part], axis=-1).astype(jnp.bfloat16)


def pack_kernel(first, count, me_ref, k_ref, v_ref, *refs):
    outs = refs[:len(ORDER)]
    held, in_sems, out_sems = refs[len(ORDER):]
    me = me_ref[0]
    reads = []
    for at, offset in enumerate(ORDER):
        for kv, src in enumerate((k_ref, v_ref)):
            reads.append(pltpu.make_async_copy(src.at[me ^ offset, pl.ds(first, count)], held.at[at, kv], in_sems.at[at, kv]))
            reads[-1].start()
    writes = []
    for at, out in enumerate(outs):
        reads[2 * at].wait()
        reads[2 * at + 1].wait()
        writes.append(pltpu.make_async_copy(held.at[at], out, out_sems.at[at]))
        writes[-1].start()
    for write in writes:
        write.wait()


def pack(first, count, me, k_mine, v_mine):
    dim = k_mine.shape[2]
    piece = jax.ShapeDtypeStruct((2, count, dim), jnp.bfloat16)
    return pl.pallas_call(
        functools.partial(pack_kernel, first, count),
        out_shape=[piece] * len(ORDER),
        in_specs=[pl.BlockSpec(memory_space=pltpu.SMEM)] + [pl.BlockSpec(memory_space=pltpu.HBM)] * 2,
        out_specs=[pl.BlockSpec(memory_space=pltpu.HBM)] * len(ORDER),
        scratch_shapes=[pltpu.VMEM((len(ORDER), 2, count, dim), jnp.bfloat16), pltpu.SemaphoreType.DMA((len(ORDER), 2)), pltpu.SemaphoreType.DMA((len(ORDER),))],
        compiler_params=pltpu.CompilerParams(vmem_limit_bytes=12 * MIB),
        cost_estimate=pl.CostEstimate(flops=0, bytes_accessed=len(ORDER) * 4 * count * dim * 2, transcendentals=0),
    )(me, k_mine, v_mine)


def wrap_kernel(me_ref, len_ref, k_ref, k_late_ref, v_ref, v_late_ref, *outs):
    me = me_ref[0]
    slots = lax.broadcasted_iota(jnp.int32, (WRAP, 128), 0)
    for out, offset in zip(outs, ORDER + (0,)):
        row = me ^ offset
        late = slots + WINDOW < len_ref[row]
        for kv, (base_ref, late_ref) in enumerate(((k_ref, k_late_ref), (v_ref, v_late_ref))):
            out[kv] = jnp.where(late, late_ref[row].astype(jnp.float32), base_ref[row].astype(jnp.float32)).astype(jnp.bfloat16)


def wrap_pack(me, lengths, k_mine, v_mine):
    rows, _, dim = k_mine.shape
    base = pl.BlockSpec((rows, WRAP, dim), lambda i: (0, 0, 0))
    late = pl.BlockSpec((rows, WRAP, dim), lambda i: (0, WINDOW // WRAP, 0))
    piece = jax.ShapeDtypeStruct((2, WRAP, dim), jnp.bfloat16)
    return pl.pallas_call(
        wrap_kernel,
        grid=(1,),
        out_shape=[piece] * (len(ORDER) + 1),
        out_specs=[pl.BlockSpec((2, WRAP, dim), lambda i: (0, 0, 0))] * (len(ORDER) + 1),
        in_specs=[pl.BlockSpec(memory_space=pltpu.SMEM)] * 2 + [base, late, base, late],
        compiler_params=pltpu.CompilerParams(vmem_limit_bytes=16 * MIB),
        cost_estimate=pl.CostEstimate(flops=rows * 8 * WRAP * dim, bytes_accessed=rows * 6 * WRAP * dim * 2, transcendentals=0),
    )(me, lengths, k_mine, k_mine, v_mine, v_mine)


def interleave_kernel(first, count, block, has_own, num_alias, me_ref, len_ref, new_ref, *refs):
    num_own = 2 if has_own else 1
    own = refs[:num_own]
    pieces = refs[num_own:num_own + len(ORDER)]
    k_out, v_out, held, mixed, in_sems, out_sems = refs[num_own + len(ORDER) + num_alias:]
    tiles = count // block
    me = me_ref[0]
    row_len = len_ref[0]
    new_slot = lax.rem(row_len, WINDOW)
    outs = (k_out, v_out)

    def read(tile, kv, offset):
        at = pl.multiple_of(tile * block, block)
        if offset:
            src = pieces[ORDER.index(offset)].at[kv, pl.ds(at, block)]
        elif has_own:
            src = own[kv].at[me, pl.ds(first + at, block)]
        else:
            src = own[0].at[kv, pl.ds(at, block)]
        return pltpu.make_async_copy(src, held.at[tile, kv, me ^ offset], in_sems.at[tile, kv, offset])

    def write(tile, kv):
        at = pl.multiple_of((first + tile * block) * PEERS, block * PEERS)
        return pltpu.make_async_copy(mixed.at[tile, kv], outs[kv].at[pl.ds(at, block * PEERS)], out_sems.at[tile, kv])

    @pl.loop(0, tiles)
    def _(tile):
        for kv in range(2):
            for offset in range(PEERS):
                read(tile, kv, offset).start()

    @pl.loop(0, tiles)
    def _(tile):
        start = first + tile * block
        plain = (start + block <= row_len) & ((new_slot < start) | (new_slot >= start + block))
        for kv in range(2):
            for offset in range(PEERS):
                read(tile, kv, offset).wait()

            def group(at):
                return jnp.swapaxes(held[tile, kv, :, at:at + GROUP, :], 0, 1).reshape(GROUP * PEERS, -1)

            @pl.when(plain)
            def _():
                for at in range(0, block, GROUP):
                    mixed[tile, kv, at * PEERS:(at + GROUP) * PEERS, :] = group(at)

            @pl.when(jnp.logical_not(plain))
            def _():
                new = jnp.concatenate([new_ref[kv]] * GROUP, axis=0)
                slot_of_row = lax.broadcasted_iota(jnp.int32, new.shape, 0) // PEERS
                for at in range(0, block, GROUP):
                    slots = slot_of_row + (start + at)
                    rows = jnp.where(slots < row_len, group(at).astype(jnp.float32), 0.0)
                    rows = jnp.where(slots == new_slot, new, rows)
                    mixed[tile, kv, at * PEERS:(at + GROUP) * PEERS, :] = rows.astype(jnp.bfloat16)

            write(tile, kv).start()

    @pl.loop(0, tiles)
    def _(tile):
        for kv in range(2):
            write(tile, kv).wait()


def interleave(first, me, row_len, new, own, pieces, caches):
    count, dim = pieces[0].shape[1:]
    block = min(count, BLOCK)
    tiles = count // block
    cache = jax.ShapeDtypeStruct((WINDOW * PEERS, dim), jnp.bfloat16)
    any_spec = pl.BlockSpec(memory_space=pltpu.HBM)
    args = [me, row_len, new, *own, *pieces]
    in_specs = [pl.BlockSpec(memory_space=pltpu.SMEM)] * 2 + [pl.BlockSpec(memory_space=pltpu.VMEM)] + [any_spec] * (len(own) + len(pieces))
    aliases = {}
    if caches is not None:
        aliases = {len(args): 0, len(args) + 1: 1}
        args += caches
        in_specs += [any_spec] * 2
    return pl.pallas_call(
        functools.partial(interleave_kernel, first, count, block, len(own) == 2, len(aliases)),
        out_shape=[cache, cache],
        in_specs=in_specs,
        out_specs=[any_spec] * 2,
        input_output_aliases=aliases,
        scratch_shapes=[
            pltpu.VMEM((tiles, 2, PEERS, block, dim), jnp.bfloat16),
            pltpu.VMEM((tiles, 2, block * PEERS, dim), jnp.bfloat16),
            pltpu.SemaphoreType.DMA((tiles, 2, PEERS)),
            pltpu.SemaphoreType.DMA((tiles, 2)),
        ],
        compiler_params=pltpu.CompilerParams(vmem_limit_bytes=16 * MIB),
        cost_estimate=pl.CostEstimate(flops=count * 64 * dim, bytes_accessed=count * PEERS * dim * 8, transcendentals=0),
    )(*args)


def solution(mesh):
    head_spec = P('dp', None, 'sh', None)
    row_spec = P(('dp', 'sh'))
    full_spec = P(None, None)

    def swap(value, offset):
        return lax.ppermute(value, 'sh', [(i, i ^ offset) for i in range(PEERS)])

    def exchange(table, me):
        got = [lax.dynamic_slice_in_dim(table, me ^ offset, 1) for offset in range(PEERS)]
        return [got[0]] + [swap(got[offset], offset) for offset in range(1, PEERS)]

    def by_device(got, me):
        return jnp.take(jnp.concatenate(got, axis=0), me ^ jnp.arange(PEERS), axis=0)

    def per_device(k_prefill, v_prefill, lengths, residual, norm_gain, w_query, w_key, w_value, w_out):
        me = lax.axis_index('sh')
        me_vec = me.reshape(1).astype(jnp.int32)
        seq_len = k_prefill.shape[1]
        head_dim = k_prefill.shape[3]
        k_mine = k_prefill.reshape(PEERS, seq_len, head_dim)
        v_mine = v_prefill.reshape(PEERS, seq_len, head_dim)
        my_len = lax.dynamic_slice_in_dim(lengths, me, 1)
        received = {}

        def send(first, pieces):
            received[first] = [swap(piece, offset) for piece, offset in zip(pieces, ORDER)]

        def start(chunk, after=None, before=None):
            place = me_vec
            if after is not None:
                place, after = lax.optimization_barrier((place, after))
            pieces = pack(*chunk, place, k_mine, v_mine)
            pieces, before = lax.optimization_barrier((pieces, before))
            send(chunk[0], pieces)
            return after, before

        _, residual = start(CHUNKS[0], before=residual)
        _, residual = start(CHUNKS[1], after=residual, before=residual)

        resid_f32 = residual.astype(jnp.float32)
        inv_rms = lax.rsqrt(jnp.mean(resid_f32 * resid_f32, axis=-1, keepdims=True) + EPS)
        normed = (resid_f32 * inv_rms * norm_gain.astype(jnp.float32)).astype(jnp.bfloat16)
        q_heads = jnp.dot(normed, w_query, preferred_element_type=jnp.float32).astype(jnp.bfloat16).reshape(1, -1, head_dim)
        k_new = jnp.dot(normed, w_key, preferred_element_type=jnp.float32).astype(jnp.bfloat16).reshape(1, PEERS, head_dim)
        v_new = jnp.dot(normed, w_value, preferred_element_type=jnp.float32).astype(jnp.bfloat16).reshape(1, PEERS, head_dim)
        q_heads = rotate(q_heads, my_len)
        k_new = rotate(k_new, my_len)
        q_group = q_heads.shape[1] // PEERS
        new = jnp.concatenate([k_new, v_new], axis=0).astype(jnp.float32)

        table = jnp.concatenate([q_heads.reshape(PEERS, q_group, head_dim), k_new.reshape(PEERS, 1, head_dim), v_new.reshape(PEERS, 1, head_dim)], axis=1).reshape(PEERS, -1)
        qkv_parts = exchange(table, me)
        _, table = start(CHUNKS[2], after=table, before=table)
        wrap_place, _ = lax.optimization_barrier((me_vec, table))
        wrapped = wrap_pack(wrap_place, lengths, k_mine, v_mine)
        send(0, wrapped[:-1])
        qkv = by_device(qkv_parts, me).reshape(PEERS, q_group + 2, head_dim)
        q_all, k_all, v_all = qkv[:, :q_group], qkv[:, q_group:q_group + 1], qkv[:, q_group + 1:]
        positions = jnp.arange(seq_len, dtype=jnp.int32)[None, :]
        live = (positions < lengths[:, None]) & (positions > lengths[:, None] - WINDOW)
        scores = jnp.einsum('bgd,bsd->bgs', q_all, k_mine, preferred_element_type=jnp.float32) / head_dim ** 0.5
        scores = jnp.where(live[:, None, :], scores, -jnp.inf)
        top_old = jnp.max(scores, axis=-1, keepdims=True)
        new_score = jnp.sum(q_all.astype(jnp.float32) * k_all.astype(jnp.float32), axis=-1, keepdims=True) / head_dim ** 0.5
        top = jnp.maximum(top_old, new_score)
        exp_scores = jnp.exp(scores - top)
        exp_new = jnp.exp(new_score - top)
        total = jnp.sum(exp_scores, axis=-1, keepdims=True) + exp_new
        weights = (exp_scores / total).astype(jnp.bfloat16)
        new_weight = lax.reduce_precision(exp_new / total, 8, 7)
        mixed = jnp.einsum('bgs,bsd->bgd', weights, v_mine, preferred_element_type=jnp.float32)
        mixed = (mixed + new_weight * v_all.astype(jnp.float32)).astype(jnp.bfloat16).reshape(PEERS, -1)
        attn_parts = exchange(mixed, me)

        place, _ = lax.optimization_barrier((me_vec, mixed))
        caches = None

        def store(first, caches):
            own = [wrapped[-1]] if first == 0 else [k_mine, v_mine]
            return interleave(first, place, my_len, new, own, received[first], caches)

        caches = store(CHUNKS[0][0], caches)
        caches = store(CHUNKS[1][0], caches)
        caches, caches = start(CHUNKS[3], after=caches, before=caches)
        caches, caches = start(CHUNKS[4], after=caches, before=caches)
        caches = store(CHUNKS[2][0], caches)
        attn_parts, caches = lax.optimization_barrier((attn_parts, caches))
        attn_out = by_device(attn_parts, me).reshape(1, -1)
        resid_out = (resid_f32 + jnp.dot(attn_out, w_out, preferred_element_type=jnp.float32)).astype(jnp.bfloat16)
        for first in (0, CHUNKS[3][0], CHUNKS[4][0]):
            caches = store(first, caches)
        shape = (1, WINDOW, PEERS, head_dim)
        return resid_out, caches[0].reshape(shape), caches[1].reshape(shape)

    return jax.shard_map(per_device, mesh=mesh, in_specs=(head_spec, head_spec, P('dp'), P(('dp', 'sh'), None), P(None), full_spec, full_spec, full_spec, full_spec), out_specs=(P(('dp', 'sh'), None), row_spec, row_spec), check_vma=False)
```

time: 377 us -> 316 us (0.84)
  other arithmetic: 133 us -> 3.22 us
  blocking collectives: 106 us -> 0 us
  Pallas kernels: 0 us -> 57.3 us
  starting transfers between devices: 5.12 us -> 59 us
  waiting for transfers between devices: 65 us -> 104 us
  local copies, waits for them, and re-layouts: 18.5 us -> 41.3 us
    select_n x3 -> x2, other arithmetic: 131 us -> 0.08 us  [by_device(): jnp.take(jnp.concatenate(got, axis=0), me ^ jnp.arange(PEERS), axis=0)]
    all_to_all x1 -> x0, blocking collectives: 106 us -> none  [per_device(): k_rows = lax.all_to_all(k_prefill, 'sh', 0, 2, tiled=True)]
    ppermute x0 -> x56, waiting for transfers between devices: none -> 104 us  [swap(): return lax.ppermute(value, 'sh', [(i, i ^ offset) for i in range(PEERS)])]
    all_to_all x1 -> x0, waiting for transfers between devices: 65 us -> none  [per_device(): v_rows = lax.all_to_all(v_prefill, 'sh', 0, 2, tiled=True)]
    ppermute x0 -> x56, starting transfers between devices: none -> 59 us  [swap(): return lax.ppermute(value, 'sh', [(i, i ^ offset) for i in range(PEERS)])]
    pallas_call x0 -> x12, Pallas kernels: none -> 57.3 us  [the longest x6 40.6 us: interleave(): pl.pallas_call(functools.partial(interleave_kernel, first, count, block,...]
    unnamed x12 -> x113, local copies, waits for them, and re-layouts: 17.9 us -> 37.3 us
    dot_general x5 -> x6, matrix products: 37.9 us -> 46.8 us  [the longest x1 13.4 us: per_device(): jnp.dot(attn_out, w_out, preferred_element_type=jnp.float32)]
  transfers between devices with their start and end apart: 1 -> 56, of which waited for: 1 -> 19; matrix products, arithmetic and copies ran while one was open for 8% -> 9% of each run, Pallas kernels for 0% -> 15%
where the time goes in v1:
time: 316 us; the launch traced here: 314 us
  waiting for transfers between devices  104 us (33%)
  starting transfers between devices  59 us (19%)
  Pallas kernels  57.3 us (18%)
  matrix products  46.8 us (15%)
  local copies, waits for them, and re-layouts  41.3 us (13%)
  other arithmetic  3.22 us (1%)
    ppermute x56, waiting for transfers between devices, swap(): return lax.ppermute(value, 'sh', [(i, i ^ offset) for i in range(PEERS)])  104 us
    ppermute x56, starting transfers between devices, swap(): return lax.ppermute(value, 'sh', [(i, i ^ offset) for i in range(PEERS)])  59 us
    pallas_call x6, Pallas kernels, interleave(): pl.pallas_call(functools.partial(interleave_kernel, first, count, block,...  40.6 us
    unnamed x113, local copies, waits for them, and re-layouts  37.3 us
    pallas_call x5, Pallas kernels, pack(): pl.pallas_call(functools.partial(pack_kernel, first, count), out_shape=[p...  15.2 us
    dot_general x1, matrix products, per_device(): jnp.dot(attn_out, w_out, preferred_element_type=jnp.float32)  13.4 us
    dot_general x1, matrix products, per_device(): jnp.dot(normed, w_query, preferred_element_type=jnp.float32)  12.9 us
  transfers between devices with their start and end apart: 56, of which 19 were waited for; matrix products, arithmetic and copies ran while one was open for 9% of the time, Pallas kernels for 15%

profile of v1, /device:TPU:0, one launch (start us, length us, event | category | flops | bytes accessed | tf_op | source)
XLA Modules:
  0.0 314.4 jit_solution(16792642873666241622)
XLA Ops:
  4.2 3.5 %copy-done.3 = bf16[8,4352,1,128]{3,1,2,0:T(8,128)(2,1)S(1)} copy-done((bf16[8,4352,1,128]{3,1,2,0:T(8,128)(2,1)S(1)}, bf16[8,4352,1,128]{3,1,2,0:T(8,128)(2,1)}, u32[]{:S(2)}) %copy-start.3) | copy-done | bytes 8912920
  20.3 4.6 %fusion.14 = f32[1,1024]{1,0:T(1,128)S(1)} fusion(bf16[4096,1024]{1,0:T(8,128)(2,1)} %param.15, f32[1,4096]{1,0:T(1,128)S(1)} %bitcast.91, bf16[1,4096]{1,0:T(2,128)(2,1)S(1)} %copy-done.37, f32[]{:T(128)S(6)} %rsqrt.4), kind=kOutput, calls=%fused_computation.28 | convolution fusion | flops 8404992 | bytes 8417284 | tf_op jit(solution)/shard_map/dot_general | solution.py:233
  26.2 4.6 %fusion.12 = f32[1,1024]{1,0:T(1,128)S(1)} fusion(bf16[4096,1024]{1,0:T(8,128)(2,1)} %param.16, f32[1,4096]{1,0:T(1,128)S(1)} %bitcast.92, bf16[1,4096]{1,0:T(2,128)(2,1)S(1)} %copy-done.37, f32[]{:T(128)S(6)} %rsqrt.4), kind=kOutput, calls=%fused_computation.26 | convolution fusion | flops 8404992 | bytes 8417284 | tf_op jit(solution)/shard_map/dot_general | solution.py:234
  31.4 12.9 %fusion.16 = f32[1,4096]{1,0:T(1,128)S(1)} fusion(bf16[4096,4096]{1,0:T(8,128)(2,1)} %param.14, f32[1,4096]{1,0:T(1,128)S(1)} %bitcast.93, bf16[1,4096]{1,0:T(2,128)(2,1)S(1)} %copy-done.37, f32[]{:T(128)S(6)} %rsqrt.4), kind=kOutput, calls=%fused_computation.30 | convolution fusion | flops 33570816 | bytes 33595396 | tf_op jit(solution)/shard_map/dot_general | solution.py:232
  56.2 3.5 %copy-done.4 = bf16[8,4352,1,128]{3,1,2,0:T(8,128)(2,1)S(1)} copy-done((bf16[8,4352,1,128]{3,1,2,0:T(8,128)(2,1)S(1)}, bf16[8,4352,1,128]{3,1,2,0:T(8,128)(2,1)}, u32[]{:S(2)}) %copy-start.4) | copy-done | bytes 8912920
  65.7 6.2 %fusion.32 = (f32[8,4]{1,0:T(8,128)S(1)}, f32[8,4,4352]{2,1,0:T(4,128)S(1)}) fusion(bf16[8,4352,1,128]{3,1,2,0:T(8,128)(2,1)} %param.9, bf16[8,6,128]{2,1,0:T(8,128)(2,1)S(1)} %copy_select_fusion, pred[8,4352]{1,0:T(8,128)(4,1)S(1)} %fusion.7), kind=kOutput, calls=%fused_computation.90 | convolution fusion | flops 36069344 | bytes 9513088 | tf_op jit(solution)/shard_map/bgd,bsd->bgs/dot_general | solution.py:250
  72.4 5.1 %fusion.3 = bf16[1,8,4,128]{3,2,1,0:T(4,128)(2,1)S(1)} fusion(f32[8,4,4352]{2,1,0:T(4,128)S(1)} %get-tuple-element.252, f32[8,4]{1,0:T(8,128)S(1)} %get-tuple-element.228, f32[8,4]{1,0:T(8,128)S(1)} %multiply_maximum_fusion, f32[8,128]{1,0:T(8,128)S(1)} %bitcast.95, f32[8,4]{1,0:T(8,128)S(1)} %get-tuple-element.227, bf16[8,4352,1,128]{3,1,2,0:T(8,128)(2,1)} %param.10), kind=kOutput, calls=%fused_computation.8 | convolution fusion | flops 36081664 | bytes 9482624 | tf_op jit(solution)/shard_map/bgs,bsd->bgd/dot_general | solution.py:260
  101.6 3.7 %collective-permute-done.28.refs_2_ = bf16[2,512,128]{2,1,0:T(8,128)(2,1)S(1)} collective-permute-done((bf16[2,512,128]{2,1,0:T(8,128)(2,1)S(1)}, bf16[2,512,128]{2,1,0:T(8,128)(2,1)S(1)}, u32[]{:S(2)}, u32[]{:S(2)}) %collective-permute-start.28) | collective-permute-done | bytes 262176 | tf_op jit(solution)/shard_map/ppermute | solution.py:195
  106.3 3.6 %collective-permute-done.29.refs_3_ = bf16[2,512,128]{2,1,0:T(8,128)(2,1)S(1)} collective-permute-done((bf16[2,512,128]{2,1,0:T(8,128)(2,1)S(1)}, bf16[2,512,128]{2,1,0:T(8,128)(2,1)S(1)}, u32[]{:S(2)}, u32[]{:S(2)}) %collective-permute-start.29) | collective-permute-done | bytes 262176 | tf_op jit(solution)/shard_map/ppermute | solution.py:195
  116.9 18.3 %collective-permute-done.32.refs_6_ = bf16[2,512,128]{2,1,0:T(8,128)(2,1)S(1)} collective-permute-done((bf16[2,512,128]{2,1,0:T(8,128)(2,1)S(1)}, bf16[2,512,128]{2,1,0:T(8,128)(2,1)S(1)}, u32[]{:S(2)}, u32[]{:S(2)}) %collective-permute-start.32) | collective-permute-done | bytes 262176 | tf_op jit(solution)/shard_map/ppermute | solution.py:195
  136.7 11.5 %collective-permute-done.33.refs_7_ = bf16[2,512,128]{2,1,0:T(8,128)(2,1)S(1)} collective-permute-done((bf16[2,512,128]{2,1,0:T(8,128)(2,1)S(1)}, bf16[2,512,128]{2,1,0:T(8,128)(2,1)S(1)}, u32[]{:S(2)}, u32[]{:S(2)}) %collective-permute-start.33) | collective-permute-done | bytes 262176 | tf_op jit(solution)/shard_map/ppermute | solution.py:195
  163.8 14.5 %collective-permute-done.25.refs_6_ = bf16[2,1280,128]{2,1,0:T(8,128)(2,1)S(1)} collective-permute-done((bf16[2,1280,128]{2,1,0:T(8,128)(2,1)S(1)}, bf16[2,1280,128]{2,1,0:T(8,128)(2,1)S(1)}, u32[]{:S(2)}, u32[]{:S(2)}) %collective-permute-start.25) | collective-permute-done | bytes 655392 | tf_op jit(solution)/shard_map/ppermute | solution.py:195
  181.5 11.1 %collective-permute-done.14.refs_2_ = bf16[2,1280,128]{2,1,0:T(8,128)(2,1)S(1)} collective-permute-done((bf16[2,1280,128]{2,1,0:T(8,128)(2,1)S(1)}, bf16[2,1280,128]{2,1,0:T(8,128)(2,1)S(1)}, u32[]{:S(2)}, u32[]{:S(2)}) %collective-permute-start.14) | collective-permute-done | bytes 655392 | tf_op jit(solution)/shard_map/ppermute | solution.py:195
  192.8 13.7 %collective-permute-done.15.refs_3_ = bf16[2,1280,128]{2,1,0:T(8,128)(2,1)S(1)} collective-permute-done((bf16[2,1280,128]{2,1,0:T(8,128)(2,1)S(1)}, bf16[2,1280,128]{2,1,0:T(8,128)(2,1)S(1)}, u32[]{:S(2)}, u32[]{:S(2)}) %collective-permute-start.15) | collective-permute-done | bytes 655392 | tf_op jit(solution)/shard_map/ppermute | solution.py:195
  206.6 3.5 %copy-done.6 = bf16[8,4352,1,128]{3,1,2,0:T(8,128)(2,1)S(1)} copy-done((bf16[8,4352,1,128]{3,1,2,0:T(8,128)(2,1)S(1)}, bf16[8,4352,1,128]{3,1,2,0:T(8,128)(2,1)}, u32[]{:S(2)}) %copy-start.6) | copy-done | bytes 8912920
  210.1 6.0 %shard_map.115 = (bf16[32768,128]{1,0:T(8,128)(2,1)}, bf16[32768,128]{1,0:T(8,128)(2,1)}) custom-call(s32[1]{0:T(128)} %bitcast.me_ref, s32[1]{0:T(128)} %dynamic_slice.51.len_ref, f32[2,8,128]{2,1,0:T(8,128)S(1)} %maximum_convert_fusion.new_ref, bf16[8,4352,128]{2,1,0:T(8,128)(2,1)S(1)} %bitcast.80, bf16[8,4352,128]{2,1,0:T(8,128)(2,1)S(1)} %bitcast.68, ...), custom_call_target="tpu_custom_call" | custom-call | flops 4194304 | bytes 4194304 | tf_op jit(solution)/shard_map/pallas_call | solution.py:172
  216.1 11.4 %shard_map.116 = (bf16[32768,128]{1,0:T(8,128)(2,1)}, bf16[32768,128]{1,0:T(8,128)(2,1)}) custom-call(s32[1]{0:T(128)} %bitcast.me_ref, s32[1]{0:T(128)} %dynamic_slice.51.len_ref, f32[2,8,128]{2,1,0:T(8,128)S(1)} %maximum_convert_fusion.new_ref, bf16[8,4352,128]{2,1,0:T(8,128)(2,1)S(1)} %bitcast.81, ...), custom_call_target="tpu_custom_call", output_to_operand_aliasing={{0}: (12, {}), {1}: (13, {})} | custom-call | flops 10485760 | bytes 10485760 | tf_op jit(solution)/shard_map/pallas_call | solution.py:172
  227.5 3.6 %shard_map.117 = (bf16[2,512,128]{2,1,0:T(8,128)(2,1)S(1)}, bf16[2,512,128]{2,1,0:T(8,128)(2,1)S(1)}, bf16[2,512,128]{2,1,0:T(8,128)(2,1)}, bf16[2,512,128]{2,1,...) custom-call(s32[1]{0:T(128)} %bitcast.me_ref, ...), custom_call_target="tpu_custom_call" | custom-call | bytes 3670016 | tf_op jit(solution)/shard_map/pallas_call | solution.py:57
  231.7 3.6 %collective-permute-start.43 = (bf16[2,512,128]{2,1,0:T(8,128)(2,1)S(1)}, bf16[2,512,128]{2,1,0:T(8,128)(2,1)S(1)}, u32[]{:S(2)}, u32[]{:S(2)}) collective-permute-start(bf16[2,512,128]{2,1,0:T(8,128)(2,1)S(1)} %get-tuple-element.203), channel_id=1, source_target_pairs={{0,4},{1,5},{2,6},{3,7},{4,0},{5,1},{6,2},{7,3},{8,12},{9,13},{10,... | collective-permute-start | bytes 786440 | tf_op jit(solution)/shard_map/ppermute | solution.py:195
  242.8 3.8 %collective-permute-done.35.refs_2_ = bf16[2,256,128]{2,1,0:T(8,128)(2,1)S(1)} collective-permute-done((bf16[2,256,128]{2,1,0:T(8,128)(2,1)S(1)}, bf16[2,256,128]{2,1,0:T(8,128)(2,1)S(1)}, u32[]{:S(2)}, u32[]{:S(2)}) %collective-permute-start.35) | collective-permute-done | bytes 131104 | tf_op jit(solution)/shard_map/ppermute | solution.py:195
  246.8 11.4 %collective-permute-done.36.refs_3_ = bf16[2,256,128]{2,1,0:T(8,128)(2,1)S(1)} collective-permute-done((bf16[2,256,128]{2,1,0:T(8,128)(2,1)S(1)}, bf16[2,256,128]{2,1,0:T(8,128)(2,1)S(1)}, u32[]{:S(2)}, u32[]{:S(2)}) %collective-permute-start.36) | collective-permute-done | bytes 131104 | tf_op jit(solution)/shard_map/ppermute | solution.py:195
  260.9 11.3 %shard_map.119 = (bf16[32768,128]{1,0:T(8,128)(2,1)}, bf16[32768,128]{1,0:T(8,128)(2,1)}) custom-call(s32[1]{0:T(128)} %bitcast.me_ref, s32[1]{0:T(128)} %dynamic_slice.51.len_ref, f32[2,8,128]{2,1,0:T(8,128)S(1)} %maximum_convert_fusion.new_ref, bf16[8,4352,128]{2,1,0:T(8,128)(2,1)S(1)} %bitcast.86, ...), custom_call_target="tpu_custom_call", output_to_operand_aliasing={{0}: (12, {}), {1}: (13, {})} | custom-call | flops 10485760 | bytes 10485760 | tf_op jit(solution)/shard_map/pallas_call | solution.py:172
  281.7 13.4 %fusion.1 = bf16[1,4096]{1,0:T(2,128)(2,1)} fusion(bf16[4096,1]{0,1:T(2,128)(2,1)S(1)} %bitcast.96, bf16[4096,4096]{1,0:T(8,128)(2,1)} %param.17, bf16[1,4096]{1,0:T(2,128)(2,1)} %param.12), kind=kOutput, calls=%fused_computation.5 | convolution fusion | flops 33566720 | bytes 33579008 | tf_op jit(solution)/shard_map/dot_general | solution.py:278
  305.5 5.4 %shard_map.122 = (bf16[32768,128]{1,0:T(8,128)(2,1)}, bf16[32768,128]{1,0:T(8,128)(2,1)}) custom-call(s32[1]{0:T(128)} %bitcast.me_ref, s32[1]{0:T(128)} %dynamic_slice.51.len_ref, f32[2,8,128]{2,1,0:T(8,128)S(1)} %maximum_convert_fusion.new_ref, bf16[8,4352,128]{2,1,0:T(8,128)(2,1)S(1)} %bitcast.87, ...), custom_call_target="tpu_custom_call", output_to_operand_aliasing={{0}: (12, {}), {1}: (13, {})} | custom-call | flops 4194304 | bytes 4194304 | tf_op jit(solution)/shard_map/pallas_call | solution.py:172
  (253 shorter events, 121.5 us)
Async XLA Ops:
  61.8 29.7 %collective-permute-start.49 = (bf16[2,256,128]{2,1,0:T(8,128)(2,1)S(1)}, bf16[2,256,128]{2,1,0:T(8,128)(2,1)S(1)}, u32[]{:S(2)}, u32[]{:S(2)}) collective-permute-start(bf16[2,256,128]{2,1,0:T(8,128)(2,1)S(1)} %get-tuple-element.210), channel_id=1, source_target_pairs={{0,6},{1,7},{2,4},{3,5},{4,2},{5,3},{6,0},{7,1},{8,14},{9,15},{10,... | collective-permute-start | bytes 393224 | tf_op jit(solution)/shard_map/ppermute | solution.py:195
  64.4 27.8 %collective-permute-start.50 = (bf16[2,256,128]{2,1,0:T(8,128)(2,1)}, bf16[2,256,128]{2,1,0:T(8,128)(2,1)S(1)}, u32[]{:S(2)}, u32[]{:S(2)}) collective-permute-start(bf16[2,256,128]{2,1,0:T(8,128)(2,1)} %get-tuple-element.211), channel_id=1, source_target_pairs={{0,4},{1,5},{2,6},{3,7},{4,0},{5,1},{6,2},{7,3},{8,12},{9,13},{10,... | collective-permute-start | bytes 393224 | tf_op jit(solution)/shard_map/ppermute | solution.py:195
  100.9 34.4 %collective-permute-start.32 = (bf16[2,512,128]{2,1,0:T(8,128)(2,1)S(1)}, bf16[2,512,128]{2,1,0:T(8,128)(2,1)S(1)}, u32[]{:S(2)}, u32[]{:S(2)}) collective-permute-start(bf16[2,512,128]{2,1,0:T(8,128)(2,1)S(1)} %copy-done.22), channel_id=1, source_target_pairs={{0,5},{1,4},{2,7},{3,6},{4,1},{5,0},{6,3},{7,2},{8,13},{9,12},{10,... | collective-permute-start | bytes 786440 | tf_op jit(solution)/shard_map/ppermute | solution.py:195
  105.3 46.8 %collective-permute-start.21 = (bf16[2,1280,128]{2,1,0:T(8,128)(2,1)S(1)}, bf16[2,1280,128]{2,1,0:T(8,128)(2,1)S(1)}, u32[]{:S(2)}, u32[]{:S(2)}) collective-permute-start(bf16[2,1280,128]{2,1,0:T(8,128)(2,1)S(1)} %copy-done.16), channel_id=1, source_target_pairs={{0,6},{1,7},{2,4},{3,5},{4,2},{5,3},{6,0},{7,1},{8,14},{9,15},{10,... | collective-permute-start | bytes 1966088 | tf_op jit(solution)/shard_map/ppermute | solution.py:195
  109.9 49.6 %collective-permute-start.22 = (bf16[2,1280,128]{2,1,0:T(8,128)(2,1)S(1)}, bf16[2,1280,128]{2,1,0:T(8,128)(2,1)S(1)}, u32[]{:S(2)}, u32[]{:S(2)}) collective-permute-start(bf16[2,1280,128]{2,1,0:T(8,128)(2,1)S(1)} %copy-done.14), channel_id=1, source_target_pairs={{0,4},{1,5},{2,6},{3,7},{4,0},{5,1},{6,2},{7,3},{8,12},{9,13},{10,... | collective-permute-start | bytes 1966088 | tf_op jit(solution)/shard_map/ppermute | solution.py:195
  111.2 48.5 %collective-permute-start.23 = (bf16[2,1280,128]{2,1,0:T(8,128)(2,1)S(1)}, bf16[2,1280,128]{2,1,0:T(8,128)(2,1)S(1)}, u32[]{:S(2)}, u32[]{:S(2)}) collective-permute-start(bf16[2,1280,128]{2,1,0:T(8,128)(2,1)S(1)} %copy-done.12), channel_id=1, source_target_pairs={{0,2},{1,3},{2,0},{3,1},{4,6},{5,7},{6,4},{7,5},{8,10},{9,11},{10,... | collective-permute-start | bytes 1966088 | tf_op jit(solution)/shard_map/ppermute | solution.py:195
  115.2 33.0 %collective-permute-start.33 = (bf16[2,512,128]{2,1,0:T(8,128)(2,1)S(1)}, bf16[2,512,128]{2,1,0:T(8,128)(2,1)S(1)}, u32[]{:S(2)}, u32[]{:S(2)}) collective-permute-start(bf16[2,512,128]{2,1,0:T(8,128)(2,1)S(1)} %copy-done.20), channel_id=1, source_target_pairs={{0,3},{1,2},{2,1},{3,0},{4,7},{5,6},{6,5},{7,4},{8,11},{9,10},{10,... | collective-permute-start | bytes 786440 | tf_op jit(solution)/shard_map/ppermute | solution.py:195
  150.4 27.9 %collective-permute-start.25 = (bf16[2,1280,128]{2,1,0:T(8,128)(2,1)S(1)}, bf16[2,1280,128]{2,1,0:T(8,128)(2,1)S(1)}, u32[]{:S(2)}, u32[]{:S(2)}) collective-permute-start(bf16[2,1280,128]{2,1,0:T(8,128)(2,1)S(1)} %get-tuple-element.151), channel_id=1, source_target_pairs={{0,5},{1,4},{2,7},{3,6},{4,1},{5,0},{6,3},{7,2},{8,13},{9,12},{10,... | collective-permute-start | bytes 1966088 | tf_op jit(solution)/shard_map/ppermute | solution.py:195
  159.7 32.8 %collective-permute-start.14 = (bf16[2,1280,128]{2,1,0:T(8,128)(2,1)S(1)}, bf16[2,1280,128]{2,1,0:T(8,128)(2,1)S(1)}, u32[]{:S(2)}, u32[]{:S(2)}) collective-permute-start(bf16[2,1280,128]{2,1,0:T(8,128)(2,1)S(1)} %get-tuple-element.140), channel_id=1, source_target_pairs={{0,6},{1,7},{2,4},{3,5},{4,2},{5,3},{6,0},{7,1},{8,14},{9,15},{10,... | collective-permute-start | bytes 1966088 | tf_op jit(solution)/shard_map/ppermute | solution.py:195
  163.0 43.5 %collective-permute-start.15 = (bf16[2,1280,128]{2,1,0:T(8,128)(2,1)S(1)}, bf16[2,1280,128]{2,1,0:T(8,128)(2,1)S(1)}, u32[]{:S(2)}, u32[]{:S(2)}) collective-permute-start(bf16[2,1280,128]{2,1,0:T(8,128)(2,1)S(1)} %get-tuple-element.141), channel_id=1, source_target_pairs={{0,4},{1,5},{2,6},{3,7},{4,0},{5,1},{6,2},{7,3},{8,12},{9,13},{10,... | collective-permute-start | bytes 1966088 | tf_op jit(solution)/shard_map/ppermute | solution.py:195
  178.3 52.9 %collective-permute-start.16 = (bf16[2,1280,128]{2,1,0:T(8,128)(2,1)S(1)}, bf16[2,1280,128]{2,1,0:T(8,128)(2,1)S(1)}, u32[]{:S(2)}, u32[]{:S(2)}) collective-permute-start(bf16[2,1280,128]{2,1,0:T(8,128)(2,1)S(1)} %get-tuple-element.142), channel_id=1, source_target_pairs={{0,2},{1,3},{2,0},{3,1},{4,6},{5,7},{6,4},{7,5},{8,10},{9,11},{10,... | collective-permute-start | bytes 1966088 | tf_op jit(solution)/shard_map/ppermute | solution.py:195
  179.0 52.6 %collective-permute-start.17 = (bf16[2,1280,128]{2,1,0:T(8,128)(2,1)S(1)}, bf16[2,1280,128]{2,1,0:T(8,128)(2,1)S(1)}, u32[]{:S(2)}, u32[]{:S(2)}) collective-permute-start(bf16[2,1280,128]{2,1,0:T(8,128)(2,1)S(1)} %get-tuple-element.143), channel_id=1, source_target_pairs={{0,7},{1,6},{2,5},{3,4},{4,3},{5,2},{6,1},{7,0},{8,15},{9,14},{10,... | collective-permute-start | bytes 1966088 | tf_op jit(solution)/shard_map/ppermute | solution.py:195
  179.4 59.9 %collective-permute-start.18 = (bf16[2,1280,128]{2,1,0:T(8,128)(2,1)S(1)}, bf16[2,1280,128]{2,1,0:T(8,128)(2,1)S(1)}, u32[]{:S(2)}, u32[]{:S(2)}) collective-permute-start(bf16[2,1280,128]{2,1,0:T(8,128)(2,1)S(1)} %get-tuple-element.144), channel_id=1, source_target_pairs={{0,5},{1,4},{2,7},{3,6},{4,1},{5,0},{6,3},{7,2},{8,13},{9,12},{10,... | collective-permute-start | bytes 1966088 | tf_op jit(solution)/shard_map/ppermute | solution.py:195
  192.5 48.2 %collective-permute-start.19 = (bf16[2,1280,128]{2,1,0:T(8,128)(2,1)S(1)}, bf16[2,1280,128]{2,1,0:T(8,128)(2,1)S(1)}, u32[]{:S(2)}, u32[]{:S(2)}) collective-permute-start(bf16[2,1280,128]{2,1,0:T(8,128)(2,1)S(1)} %get-tuple-element.145), channel_id=1, source_target_pairs={{0,3},{1,2},{2,1},{3,0},{4,7},{5,6},{6,5},{7,4},{8,11},{9,10},{10,... | collective-permute-start | bytes 1966088 | tf_op jit(solution)/shard_map/ppermute | solution.py:195
  206.5 34.2 %collective-permute-start.20 = (bf16[2,1280,128]{2,1,0:T(8,128)(2,1)S(1)}, bf16[2,1280,128]{2,1,0:T(8,128)(2,1)S(1)}, u32[]{:S(2)}, u32[]{:S(2)}) collective-permute-start(bf16[2,1280,128]{2,1,0:T(8,128)(2,1)S(1)} %get-tuple-element.146), channel_id=1, source_target_pairs={{0,1},{1,0},{2,3},{3,2},{4,5},{5,4},{6,7},{7,6},{8,9},{9,8},{10,11... | collective-permute-start | bytes 1966088 | tf_op jit(solution)/shard_map/ppermute | solution.py:195
  231.2 28.5 %collective-permute-start.42 = (bf16[2,512,128]{2,1,0:T(8,128)(2,1)S(1)}, bf16[2,512,128]{2,1,0:T(8,128)(2,1)S(1)}, u32[]{:S(2)}, u32[]{:S(2)}) collective-permute-start(bf16[2,512,128]{2,1,0:T(8,128)(2,1)S(1)} %get-tuple-element.202), channel_id=1, source_target_pairs={{0,6},{1,7},{2,4},{3,5},{4,2},{5,3},{6,0},{7,1},{8,14},{9,15},{10,... | collective-permute-start | bytes 786440 | tf_op jit(solution)/shard_map/ppermute | solution.py:195
  231.7 28.7 %collective-permute-start.43 = (bf16[2,512,128]{2,1,0:T(8,128)(2,1)S(1)}, bf16[2,512,128]{2,1,0:T(8,128)(2,1)S(1)}, u32[]{:S(2)}, u32[]{:S(2)}) collective-permute-start(bf16[2,512,128]{2,1,0:T(8,128)(2,1)S(1)} %get-tuple-element.203), channel_id=1, source_target_pairs={{0,4},{1,5},{2,6},{3,7},{4,0},{5,1},{6,2},{7,3},{8,12},{9,13},{10,... | collective-permute-start | bytes 786440 | tf_op jit(solution)/shard_map/ppermute | solution.py:195
  240.7 34.3 %collective-permute-start.44 = (bf16[2,512,128]{2,1,0:T(8,128)(2,1)}, bf16[2,512,128]{2,1,0:T(8,128)(2,1)S(1)}, u32[]{:S(2)}, u32[]{:S(2)}) collective-permute-start(bf16[2,512,128]{2,1,0:T(8,128)(2,1)} %get-tuple-element.204), channel_id=1, source_target_pairs={{0,2},{1,3},{2,0},{3,1},{4,6},{5,7},{6,4},{7,5},{8,10},{9,11},{10,... | collective-permute-start | bytes 786440 | tf_op jit(solution)/shard_map/ppermute | solution.py:195
  246.6 31.7 %collective-permute-start.45 = (bf16[2,512,128]{2,1,0:T(8,128)(2,1)}, bf16[2,512,128]{2,1,0:T(8,128)(2,1)S(1)}, u32[]{:S(2)}, u32[]{:S(2)}) collective-permute-start(bf16[2,512,128]{2,1,0:T(8,128)(2,1)} %get-tuple-element.205), channel_id=1, source_target_pairs={{0,7},{1,6},{2,5},{3,4},{4,3},{5,2},{6,1},{7,0},{8,15},{9,14},{10,... | collective-permute-start | bytes 786440 | tf_op jit(solution)/shard_map/ppermute | solution.py:195
  275.0 35.8 %collective-permute-start.37 = (bf16[2,256,128]{2,1,0:T(8,128)(2,1)}, bf16[2,256,128]{2,1,0:T(8,128)(2,1)S(1)}, u32[]{:S(2)}, u32[]{:S(2)}) collective-permute-start(bf16[2,256,128]{2,1,0:T(8,128)(2,1)} %copy-done.36), channel_id=1, source_target_pairs={{0,2},{1,3},{2,0},{3,1},{4,6},{5,7},{6,4},{7,5},{8,10},{9,11},{10,... | collective-permute-start | bytes 393224 | tf_op jit(solution)/shard_map/ppermute | solution.py:195
  278.3 32.6 %collective-permute-start.38 = (bf16[2,256,128]{2,1,0:T(8,128)(2,1)}, bf16[2,256,128]{2,1,0:T(8,128)(2,1)S(1)}, u32[]{:S(2)}, u32[]{:S(2)}) collective-permute-start(bf16[2,256,128]{2,1,0:T(8,128)(2,1)} %copy-done.35), channel_id=1, source_target_pairs={{0,7},{1,6},{2,5},{3,4},{4,3},{5,2},{6,1},{7,0},{8,15},{9,14},{10,... | collective-permute-start | bytes 393224 | tf_op jit(solution)/shard_map/ppermute | solution.py:195
  280.3 30.6 %collective-permute-start.39 = (bf16[2,256,128]{2,1,0:T(8,128)(2,1)}, bf16[2,256,128]{2,1,0:T(8,128)(2,1)S(1)}, u32[]{:S(2)}, u32[]{:S(2)}) collective-permute-start(bf16[2,256,128]{2,1,0:T(8,128)(2,1)} %copy-done.34), channel_id=1, source_target_pairs={{0,5},{1,4},{2,7},{3,6},{4,1},{5,0},{6,3},{7,2},{8,13},{9,12},{10,... | collective-permute-start | bytes 393224 | tf_op jit(solution)/shard_map/ppermute | solution.py:195
  280.3 30.6 %collective-permute-start.40 = (bf16[2,256,128]{2,1,0:T(8,128)(2,1)}, bf16[2,256,128]{2,1,0:T(8,128)(2,1)S(1)}, u32[]{:S(2)}, u32[]{:S(2)}) collective-permute-start(bf16[2,256,128]{2,1,0:T(8,128)(2,1)} %copy-done.33), channel_id=1, source_target_pairs={{0,3},{1,2},{2,1},{3,0},{4,7},{5,6},{6,5},{7,4},{8,11},{9,10},{10,... | collective-permute-start | bytes 393224 | tf_op jit(solution)/shard_map/ppermute | solution.py:195
  281.3 29.7 %collective-permute-start.41 = (bf16[2,256,128]{2,1,0:T(8,128)(2,1)S(1)}, bf16[2,256,128]{2,1,0:T(8,128)(2,1)S(1)}, u32[]{:S(2)}, u32[]{:S(2)}) collective-permute-start(bf16[2,256,128]{2,1,0:T(8,128)(2,1)S(1)} %get-tuple-element.201), channel_id=1, source_target_pairs={{0,1},{1,0},{2,3},{3,2},{4,5},{5,4},{6,7},{7,6},{8,9},{9,8},{10,11... | collective-permute-start | bytes 393224 | tf_op jit(solution)/shard_map/ppermute | solution.py:195
  (87 other events, 1392.9 us)

commit v2 on v1

--- a/solution.py
+++ b/solution.py
@@ -17,7 +17,7 @@
 CHUNKS = ((256, 512), (768, 1280), (2048, 1280), (3328, 512), (3840, 256))
 BLOCK = 256
 ORDER = (6, 4, 2, 7, 5, 3, 1)
-MIB = 1024 * 1024
+VMEM_LIMIT = 60 * 1024 * 1024
 
 
 def rotate(heads, positions):
@@ -60,7 +60,7 @@
         in_specs=[pl.BlockSpec(memory_space=pltpu.SMEM)] + [pl.BlockSpec(memory_space=pltpu.HBM)] * 2,
         out_specs=[pl.BlockSpec(memory_space=pltpu.HBM)] * len(ORDER),
         scratch_shapes=[pltpu.VMEM((len(ORDER), 2, count, dim), jnp.bfloat16), pltpu.SemaphoreType.DMA((len(ORDER), 2)), pltpu.SemaphoreType.DMA((len(ORDER),))],
-        compiler_params=pltpu.CompilerParams(vmem_limit_bytes=12 * MIB),
+        compiler_params=pltpu.CompilerParams(vmem_limit_bytes=VMEM_LIMIT),
         cost_estimate=pl.CostEstimate(flops=0, bytes_accessed=len(ORDER) * 4 * count * dim * 2, transcendentals=0),
     )(me, k_mine, v_mine)
 
@@ -86,7 +86,7 @@
         out_shape=[piece] * (len(ORDER) + 1),
         out_specs=[pl.BlockSpec((2, WRAP, dim), lambda i: (0, 0, 0))] * (len(ORDER) + 1),
         in_specs=[pl.BlockSpec(memory_space=pltpu.SMEM)] * 2 + [base, late, base, late],
-        compiler_params=pltpu.CompilerParams(vmem_limit_bytes=16 * MIB),
+        compiler_params=pltpu.CompilerParams(vmem_limit_bytes=VMEM_LIMIT),
         cost_estimate=pl.CostEstimate(flops=rows * 8 * WRAP * dim, bytes_accessed=rows * 6 * WRAP * dim * 2, transcendentals=0),
     )(me, lengths, k_mine, k_mine, v_mine, v_mine)
 
@@ -181,7 +181,7 @@
             pltpu.SemaphoreType.DMA((tiles, 2, PEERS)),
             pltpu.SemaphoreType.DMA((tiles, 2)),
         ],
-        compiler_params=pltpu.CompilerParams(vmem_limit_bytes=16 * MIB),
+        compiler_params=pltpu.CompilerParams(vmem_limit_bytes=VMEM_LIMIT),
         cost_estimate=pl.CostEstimate(flops=count * 64 * dim, bytes_accessed=count * PEERS * dim * 8, transcendentals=0),
     )(*args)
 

time: 316 us -> 280 us (0.89)
  local copies, waits for them, and re-layouts: 41.3 us -> 5.04 us
  waiting for transfers between devices: 104 us -> 119 us
  Pallas kernels: 57.3 us -> 47.1 us
  starting transfers between devices: 59 us -> 53.8 us
    unnamed x113 -> x115, local copies, waits for them, and re-layouts: 37.3 us -> 3.09 us
    ppermute x56, waiting for transfers between devices: 104 us -> 119 us  [swap(): return lax.ppermute(value, 'sh', [(i, i ^ offset) for i in range(PEERS)])]
    pallas_call x6, Pallas kernels: 40.6 us -> 29.4 us  [interleave(): pl.pallas_call(functools.partial(interleave_kernel, first, count, block,...]
    ppermute x56, starting transfers between devices: 59 us -> 53.8 us  [swap(): return lax.ppermute(value, 'sh', [(i, i ^ offset) for i in range(PEERS)])]
  transfers between devices with their start and end apart: 56 -> 56, of which waited for: 19 -> 21; matrix products, arithmetic and copies ran while one was open for 9% -> 10% of each run, Pallas kernels for 15% -> 13%
where the time goes in v2:
time: 280 us; the launch traced here: 277 us
  waiting for transfers between devices  119 us (42%)
  starting transfers between devices  53.8 us (19%)
  Pallas kernels  47.1 us (17%)
  matrix products  46.7 us (17%)
  local copies, waits for them, and re-layouts  5.04 us (2%)
  between operations  2.91 us (1%)
    ppermute x56, waiting for transfers between devices, swap(): return lax.ppermute(value, 'sh', [(i, i ^ offset) for i in range(PEERS)])  119 us
    ppermute x56, starting transfers between devices, swap(): return lax.ppermute(value, 'sh', [(i, i ^ offset) for i in range(PEERS)])  53.8 us
    pallas_call x6, Pallas kernels, interleave(): pl.pallas_call(functools.partial(interleave_kernel, first, count, block,...  29.4 us
    pallas_call x5, Pallas kernels, pack(): pl.pallas_call(functools.partial(pack_kernel, first, count), out_shape=[p...  15 us
    dot_general x1, matrix products, per_device(): jnp.dot(attn_out, w_out, preferred_element_type=jnp.float32)  13.4 us
    dot_general x1, matrix products, per_device(): jnp.dot(normed, w_query, preferred_element_type=jnp.float32)  12.9 us
    dot_general x1, matrix products, per_device(): jnp.einsum('bgd,bsd->bgs', q_all, k_mine, preferred_element_type=jnp.floa...  6.02 us
  transfers between devices with their start and end apart: 56, of which 21 were waited for; matrix products, arithmetic and copies ran while one was open for 10% of the time, Pallas kernels for 13%

profile of v2, /device:TPU:0, one launch (start us, length us, event | category | flops | bytes accessed | tf_op | source)
XLA Modules:
  0.0 277.2 jit_solution(4083499090530177337)
XLA Ops:
  3.1 4.0 %shard_map.113 = (bf16[2,1280,128]{2,1,0:T(8,128)(2,1)}, bf16[2,1280,128]{2,1,0:T(8,128)(2,1)}, bf16[2,1280,128]{2,1,0:T(8,128)(2,1)}, bf16[2,1280,128]{2,1,0:T(...) custom-call(s32[1]{0:T(128)} %bitcast.me_ref, ...), custom_call_target="tpu_custom_call" | custom-call | bytes 9175040 | tf_op jit(solution)/shard_map/pallas_call | solution.py:57
  8.5 4.6 %fusion.14 = f32[1,1024]{1,0:T(1,128)S(1)} fusion(bf16[4096,1024]{1,0:T(8,128)(2,1)} %param.15, f32[1,4096]{1,0:T(1,128)S(1)} %bitcast.87, bf16[1,4096]{1,0:T(2,128)(2,1)S(1)} %copy-done, f32[]{:T(128)S(6)} %rsqrt.4), kind=kOutput, calls=%fused_computation.28 | convolution fusion | flops 8404992 | bytes 8417284 | tf_op jit(solution)/shard_map/dot_general | solution.py:233
  14.4 4.6 %fusion.12 = f32[1,1024]{1,0:T(1,128)S(1)} fusion(bf16[4096,1024]{1,0:T(8,128)(2,1)} %param.16, f32[1,4096]{1,0:T(1,128)S(1)} %bitcast.88, bf16[1,4096]{1,0:T(2,128)(2,1)S(1)} %copy-done, f32[]{:T(128)S(6)} %rsqrt.4), kind=kOutput, calls=%fused_computation.26 | convolution fusion | flops 8404992 | bytes 8417284 | tf_op jit(solution)/shard_map/dot_general | solution.py:234
  19.0 12.9 %fusion.16 = f32[1,4096]{1,0:T(1,128)S(1)} fusion(bf16[4096,4096]{1,0:T(8,128)(2,1)} %param.14, f32[1,4096]{1,0:T(1,128)S(1)} %bitcast.89, bf16[1,4096]{1,0:T(2,128)(2,1)S(1)} %copy-done, f32[]{:T(128)S(6)} %rsqrt.4), kind=kOutput, calls=%fused_computation.30 | convolution fusion | flops 33570816 | bytes 33595396 | tf_op jit(solution)/shard_map/dot_general | solution.py:232
  46.9 6.0 %fusion.32 = (f32[8,4]{1,0:T(8,128)S(1)}, f32[8,4,4352]{2,1,0:T(4,128)S(1)}) fusion(bf16[8,4352,1,128]{3,1,2,0:T(8,128)(2,1)} %param.9, bf16[8,6,128]{2,1,0:T(8,128)(2,1)S(1)} %copy_select_fusion, pred[8,4352]{1,0:T(8,128)(4,1)S(1)} %fusion.7), kind=kOutput, calls=%fused_computation.90 | convolution fusion | flops 36069344 | bytes 9513088 | tf_op jit(solution)/shard_map/bgd,bsd->bgs/dot_general | solution.py:250
  53.4 5.2 %fusion.3 = bf16[1,8,4,128]{3,2,1,0:T(4,128)(2,1)S(1)} fusion(f32[8,4,4352]{2,1,0:T(4,128)S(1)} %get-tuple-element.252, f32[8,4]{1,0:T(8,128)S(1)} %get-tuple-element.228, f32[8,4]{1,0:T(8,128)S(1)} %multiply_maximum_fusion, f32[8,128]{1,0:T(8,128)S(1)} %bitcast.91, f32[8,4]{1,0:T(8,128)S(1)} %get-tuple-element.227, bf16[8,4352,1,128]{3,1,2,0:T(8,128)(2,1)} %param.10), kind=kOutput, calls=%fused_computation.8 | convolution fusion | flops 36081664 | bytes 9482624 | tf_op jit(solution)/shard_map/bgs,bsd->bgd/dot_general | solution.py:260
  80.7 4.3 %collective-permute-done.28.refs_2_ = bf16[2,512,128]{2,1,0:T(8,128)(2,1)S(1)} collective-permute-done((bf16[2,512,128]{2,1,0:T(8,128)(2,1)S(1)}, bf16[2,512,128]{2,1,0:T(8,128)(2,1)S(1)}, u32[]{:S(2)}, u32[]{:S(2)}) %collective-permute-start.28) | collective-permute-done | bytes 262176 | tf_op jit(solution)/shard_map/ppermute | solution.py:195
  86.3 4.4 %collective-permute-done.29.refs_3_ = bf16[2,512,128]{2,1,0:T(8,128)(2,1)S(1)} collective-permute-done((bf16[2,512,128]{2,1,0:T(8,128)(2,1)S(1)}, bf16[2,512,128]{2,1,0:T(8,128)(2,1)S(1)}, u32[]{:S(2)}, u32[]{:S(2)}) %collective-permute-start.29) | collective-permute-done | bytes 262176 | tf_op jit(solution)/shard_map/ppermute | solution.py:195
  96.2 18.9 %collective-permute-done.32.refs_6_ = bf16[2,512,128]{2,1,0:T(8,128)(2,1)} collective-permute-done((bf16[2,512,128]{2,1,0:T(8,128)(2,1)S(1)}, bf16[2,512,128]{2,1,0:T(8,128)(2,1)}, u32[]{:S(2)}, u32[]{:S(2)}) %collective-permute-start.32) | collective-permute-done | bytes 262176 | tf_op jit(solution)/shard_map/ppermute | solution.py:195
  116.7 11.5 %collective-permute-done.33.refs_7_ = bf16[2,512,128]{2,1,0:T(8,128)(2,1)S(1)} collective-permute-done((bf16[2,512,128]{2,1,0:T(8,128)(2,1)S(1)}, bf16[2,512,128]{2,1,0:T(8,128)(2,1)S(1)}, u32[]{:S(2)}, u32[]{:S(2)}) %collective-permute-start.33) | collective-permute-done | bytes 262176 | tf_op jit(solution)/shard_map/ppermute | solution.py:195
  133.0 4.0 %shard_map.114 = (bf16[2,1280,128]{2,1,0:T(8,128)(2,1)}, bf16[2,1280,128]{2,1,0:T(8,128)(2,1)}, bf16[2,1280,128]{2,1,0:T(8,128)(2,1)}, bf16[2,1280,128]{2,1,0:T(...) custom-call(s32[1]{0:T(128)} %bitcast.me_ref, ...), custom_call_target="tpu_custom_call" | custom-call | bytes 9175040 | tf_op jit(solution)/shard_map/pallas_call | solution.py:57
  138.7 4.6 %collective-permute-done.24.refs_5_ = bf16[2,1280,128]{2,1,0:T(8,128)(2,1)S(1)} collective-permute-done((bf16[2,1280,128]{2,1,0:T(8,128)(2,1)}, bf16[2,1280,128]{2,1,0:T(8,128)(2,1)S(1)}, u32[]{:S(2)}, u32[]{:S(2)}) %collective-permute-start.24) | collective-permute-done | bytes 655392 | tf_op jit(solution)/shard_map/ppermute | solution.py:195
  144.2 13.7 %collective-permute-done.25.refs_6_ = bf16[2,1280,128]{2,1,0:T(8,128)(2,1)S(1)} collective-permute-done((bf16[2,1280,128]{2,1,0:T(8,128)(2,1)}, bf16[2,1280,128]{2,1,0:T(8,128)(2,1)S(1)}, u32[]{:S(2)}, u32[]{:S(2)}) %collective-permute-start.25) | collective-permute-done | bytes 655392 | tf_op jit(solution)/shard_map/ppermute | solution.py:195
  161.1 11.1 %collective-permute-done.14.refs_2_ = bf16[2,1280,128]{2,1,0:T(8,128)(2,1)S(1)} collective-permute-done((bf16[2,1280,128]{2,1,0:T(8,128)(2,1)}, bf16[2,1280,128]{2,1,0:T(8,128)(2,1)S(1)}, u32[]{:S(2)}, u32[]{:S(2)}) %collective-permute-start.14) | collective-permute-done | bytes 655392 | tf_op jit(solution)/shard_map/ppermute | solution.py:195
  172.7 13.4 %collective-permute-done.15.refs_3_ = bf16[2,1280,128]{2,1,0:T(8,128)(2,1)S(1)} collective-permute-done((bf16[2,1280,128]{2,1,0:T(8,128)(2,1)}, bf16[2,1280,128]{2,1,0:T(8,128)(2,1)S(1)}, u32[]{:S(2)}, u32[]{:S(2)}) %collective-permute-start.15) | collective-permute-done | bytes 655392 | tf_op jit(solution)/shard_map/ppermute | solution.py:195
  186.9 4.6 %shard_map.115 = (bf16[32768,128]{1,0:T(8,128)(2,1)}, bf16[32768,128]{1,0:T(8,128)(2,1)}) custom-call(s32[1]{0:T(128)} %bitcast.me_ref, s32[1]{0:T(128)} %dynamic_slice.51.len_ref, f32[2,8,128]{2,1,0:T(8,128)} %maximum_convert_fusion.new_ref, bf16[8,4352,128]{2,1,0:T(8,128)(2,1)} %bitcast.78, bf16[8,4352,128]{2,1,0:T(8,128)(2,1)} %bitcast.66, ...), custom_call_target="tpu_custom_call" | custom-call | flops 4194304 | bytes 4194304 | tf_op jit(solution)/shard_map/pallas_call | solution.py:172
  191.6 6.6 %shard_map.116 = (bf16[32768,128]{1,0:T(8,128)(2,1)}, bf16[32768,128]{1,0:T(8,128)(2,1)}) custom-call(s32[1]{0:T(128)} %bitcast.me_ref, s32[1]{0:T(128)} %dynamic_slice.51.len_ref, f32[2,8,128]{2,1,0:T(8,128)} %maximum_convert_fusion.new_ref, bf16[8,4352,128]{2,1,0:T(8,128)(2,1)} %bitcast.79, ...), custom_call_target="tpu_custom_call", output_to_operand_aliasing={{0}: (12, {}), {1}: (13, {})} | custom-call | flops 10485760 | bytes 10485760 | tf_op jit(solution)/shard_map/pallas_call | solution.py:172
  206.4 7.5 %collective-permute-done.18.refs_6_ = bf16[2,1280,128]{2,1,0:T(8,128)(2,1)S(1)} collective-permute-done((bf16[2,1280,128]{2,1,0:T(8,128)(2,1)}, bf16[2,1280,128]{2,1,0:T(8,128)(2,1)S(1)}, u32[]{:S(2)}, u32[]{:S(2)}) %collective-permute-start.18) | collective-permute-done | bytes 655392 | tf_op jit(solution)/shard_map/ppermute | solution.py:195
  217.5 5.3 %collective-permute-done.35.refs_2_ = bf16[2,256,128]{2,1,0:T(8,128)(2,1)S(1)} collective-permute-done((bf16[2,256,128]{2,1,0:T(8,128)(2,1)}, bf16[2,256,128]{2,1,0:T(8,128)(2,1)S(1)}, u32[]{:S(2)}, u32[]{:S(2)}) %collective-permute-start.35) | collective-permute-done | bytes 131104 | tf_op jit(solution)/shard_map/ppermute | solution.py:195
  223.3 12.9 %collective-permute-done.36.refs_3_ = bf16[2,256,128]{2,1,0:T(8,128)(2,1)S(1)} collective-permute-done((bf16[2,256,128]{2,1,0:T(8,128)(2,1)}, bf16[2,256,128]{2,1,0:T(8,128)(2,1)S(1)}, u32[]{:S(2)}, u32[]{:S(2)}) %collective-permute-start.36) | collective-permute-done | bytes 131104 | tf_op jit(solution)/shard_map/ppermute | solution.py:195
  238.1 6.6 %shard_map.119 = (bf16[32768,128]{1,0:T(8,128)(2,1)}, bf16[32768,128]{1,0:T(8,128)(2,1)}) custom-call(s32[1]{0:T(128)} %bitcast.me_ref, s32[1]{0:T(128)} %dynamic_slice.51.len_ref, f32[2,8,128]{2,1,0:T(8,128)} %maximum_convert_fusion.new_ref, bf16[8,4352,128]{2,1,0:T(8,128)(2,1)} %bitcast.82, ...), custom_call_target="tpu_custom_call", output_to_operand_aliasing={{0}: (12, {}), {1}: (13, {})} | custom-call | flops 10485760 | bytes 10485760 | tf_op jit(solution)/shard_map/pallas_call | solution.py:172
  251.1 13.4 %fusion.1 = bf16[1,4096]{1,0:T(2,128)(2,1)} fusion(bf16[4096,1]{0,1:T(2,128)(2,1)S(1)} %bitcast.92, bf16[4096,4096]{1,0:T(8,128)(2,1)} %param.17, bf16[1,4096]{1,0:T(2,128)(2,1)S(1)} %copy-done), kind=kOutput, calls=%fused_computation.5 | convolution fusion | flops 33566720 | bytes 33579008 | tf_op jit(solution)/shard_map/dot_general | solution.py:278
  264.6 3.7 %shard_map.121 = (bf16[32768,128]{1,0:T(8,128)(2,1)}, bf16[32768,128]{1,0:T(8,128)(2,1)}) custom-call(s32[1]{0:T(128)} %bitcast.me_ref, s32[1]{0:T(128)} %dynamic_slice.51.len_ref, f32[2,8,128]{2,1,0:T(8,128)} %maximum_convert_fusion.new_ref, bf16[2,256,128]{2,1,0:T(8,128)(2,1)} %get-tuple-element.209.refs_0_, ...), custom_call_target="tpu_custom_call", output_to_operand_aliasing={{0}: (11, {}), {1}: (12, {})} | custom-call | flops 2097152 | bytes 2097152 | tf_op jit(solution)/shard_map/pallas_call | solution.py:172
  268.3 4.2 %shard_map.122 = (bf16[32768,128]{1,0:T(8,128)(2,1)}, bf16[32768,128]{1,0:T(8,128)(2,1)}) custom-call(s32[1]{0:T(128)} %bitcast.me_ref, s32[1]{0:T(128)} %dynamic_slice.51.len_ref, f32[2,8,128]{2,1,0:T(8,128)} %maximum_convert_fusion.new_ref, bf16[8,4352,128]{2,1,0:T(8,128)(2,1)} %bitcast.83, ...), custom_call_target="tpu_custom_call", output_to_operand_aliasing={{0}: (12, {}), {1}: (13, {})} | custom-call | flops 4194304 | bytes 4194304 | tf_op jit(solution)/shard_map/pallas_call | solution.py:172
  (253 shorter events, 86.1 us)
Async XLA Ops:
  43.0 27.4 %collective-permute-start.49 = (bf16[2,256,128]{2,1,0:T(8,128)(2,1)}, bf16[2,256,128]{2,1,0:T(8,128)(2,1)S(1)}, u32[]{:S(2)}, u32[]{:S(2)}) collective-permute-start(bf16[2,256,128]{2,1,0:T(8,128)(2,1)} %get-tuple-element.210), channel_id=1, source_target_pairs={{0,6},{1,7},{2,4},{3,5},{4,2},{5,3},{6,0},{7,1},{8,14},{9,15},{10,... | collective-permute-start | bytes 393224 | tf_op jit(solution)/shard_map/ppermute | solution.py:195
  45.6 25.5 %collective-permute-start.50 = (bf16[2,256,128]{2,1,0:T(8,128)(2,1)}, bf16[2,256,128]{2,1,0:T(8,128)(2,1)S(1)}, u32[]{:S(2)}, u32[]{:S(2)}) collective-permute-start(bf16[2,256,128]{2,1,0:T(8,128)(2,1)} %get-tuple-element.211), channel_id=1, source_target_pairs={{0,4},{1,5},{2,6},{3,7},{4,0},{5,1},{6,2},{7,3},{8,12},{9,13},{10,... | collective-permute-start | bytes 393224 | tf_op jit(solution)/shard_map/ppermute | solution.py:195
  80.2 35.0 %collective-permute-start.32 = (bf16[2,512,128]{2,1,0:T(8,128)(2,1)S(1)}, bf16[2,512,128]{2,1,0:T(8,128)(2,1)}, u32[]{:S(2)}, u32[]{:S(2)}) collective-permute-start(bf16[2,512,128]{2,1,0:T(8,128)(2,1)S(1)} %copy-done.41), channel_id=1, source_target_pairs={{0,5},{1,4},{2,7},{3,6},{4,1},{5,0},{6,3},{7,2},{8,13},{9,12},{10,... | collective-permute-start | bytes 786440 | tf_op jit(solution)/shard_map/ppermute | solution.py:195
  85.0 46.9 %collective-permute-start.21 = (bf16[2,1280,128]{2,1,0:T(8,128)(2,1)S(1)}, bf16[2,1280,128]{2,1,0:T(8,128)(2,1)S(1)}, u32[]{:S(2)}, u32[]{:S(2)}) collective-permute-start(bf16[2,1280,128]{2,1,0:T(8,128)(2,1)S(1)} %copy-done.38), channel_id=1, source_target_pairs={{0,6},{1,7},{2,4},{3,5},{4,2},{5,3},{6,0},{7,1},{8,14},{9,15},{10,... | collective-permute-start | bytes 1966088 | tf_op jit(solution)/shard_map/ppermute | solution.py:195
  90.6 46.4 %collective-permute-start.22 = (bf16[2,1280,128]{2,1,0:T(8,128)(2,1)}, bf16[2,1280,128]{2,1,0:T(8,128)(2,1)S(1)}, u32[]{:S(2)}, u32[]{:S(2)}) collective-permute-start(bf16[2,1280,128]{2,1,0:T(8,128)(2,1)} %get-tuple-element.148), channel_id=1, source_target_pairs={{0,4},{1,5},{2,6},{3,7},{4,0},{5,1},{6,2},{7,3},{8,12},{9,13},{10,... | collective-permute-start | bytes 1966088 | tf_op jit(solution)/shard_map/ppermute | solution.py:195
  91.2 46.7 %collective-permute-start.23 = (bf16[2,1280,128]{2,1,0:T(8,128)(2,1)}, bf16[2,1280,128]{2,1,0:T(8,128)(2,1)S(1)}, u32[]{:S(2)}, u32[]{:S(2)}) collective-permute-start(bf16[2,1280,128]{2,1,0:T(8,128)(2,1)} %get-tuple-element.149), channel_id=1, source_target_pairs={{0,2},{1,3},{2,0},{3,1},{4,6},{5,7},{6,4},{7,5},{8,10},{9,11},{10,... | collective-permute-start | bytes 1966088 | tf_op jit(solution)/shard_map/ppermute | solution.py:195
  95.5 32.7 %collective-permute-start.33 = (bf16[2,512,128]{2,1,0:T(8,128)(2,1)S(1)}, bf16[2,512,128]{2,1,0:T(8,128)(2,1)S(1)}, u32[]{:S(2)}, u32[]{:S(2)}) collective-permute-start(bf16[2,512,128]{2,1,0:T(8,128)(2,1)S(1)} %copy-done.40), channel_id=1, source_target_pairs={{0,3},{1,2},{2,1},{3,0},{4,7},{5,6},{6,5},{7,4},{8,11},{9,10},{10,... | collective-permute-start | bytes 786440 | tf_op jit(solution)/shard_map/ppermute | solution.py:195
  115.1 28.2 %collective-permute-start.24 = (bf16[2,1280,128]{2,1,0:T(8,128)(2,1)}, bf16[2,1280,128]{2,1,0:T(8,128)(2,1)S(1)}, u32[]{:S(2)}, u32[]{:S(2)}) collective-permute-start(bf16[2,1280,128]{2,1,0:T(8,128)(2,1)} %get-tuple-element.150), channel_id=1, source_target_pairs={{0,7},{1,6},{2,5},{3,4},{4,3},{5,2},{6,1},{7,0},{8,15},{9,14},{10,... | collective-permute-start | bytes 1966088 | tf_op jit(solution)/shard_map/ppermute | solution.py:195
  130.4 27.4 %collective-permute-start.25 = (bf16[2,1280,128]{2,1,0:T(8,128)(2,1)}, bf16[2,1280,128]{2,1,0:T(8,128)(2,1)S(1)}, u32[]{:S(2)}, u32[]{:S(2)}) collective-permute-start(bf16[2,1280,128]{2,1,0:T(8,128)(2,1)} %get-tuple-element.151), channel_id=1, source_target_pairs={{0,5},{1,4},{2,7},{3,6},{4,1},{5,0},{6,3},{7,2},{8,13},{9,12},{10,... | collective-permute-start | bytes 1966088 | tf_op jit(solution)/shard_map/ppermute | solution.py:195
  131.9 27.1 %collective-permute-start.26 = (bf16[2,1280,128]{2,1,0:T(8,128)(2,1)}, bf16[2,1280,128]{2,1,0:T(8,128)(2,1)}, u32[]{:S(2)}, u32[]{:S(2)}) collective-permute-start(bf16[2,1280,128]{2,1,0:T(8,128)(2,1)} %get-tuple-element.152), channel_id=1, source_target_pairs={{0,3},{1,2},{2,1},{3,0},{4,7},{5,6},{6,5},{7,4},{8,11},{9,10},{10,... | collective-permute-start | bytes 1966088 | tf_op jit(solution)/shard_map/ppermute | solution.py:195
  137.9 34.3 %collective-permute-start.14 = (bf16[2,1280,128]{2,1,0:T(8,128)(2,1)}, bf16[2,1280,128]{2,1,0:T(8,128)(2,1)S(1)}, u32[]{:S(2)}, u32[]{:S(2)}) collective-permute-start(bf16[2,1280,128]{2,1,0:T(8,128)(2,1)} %get-tuple-element.140), channel_id=1, source_target_pairs={{0,6},{1,7},{2,4},{3,5},{4,2},{5,3},{6,0},{7,1},{8,14},{9,15},{10,... | collective-permute-start | bytes 1966088 | tf_op jit(solution)/shard_map/ppermute | solution.py:195
  143.3 42.8 %collective-permute-start.15 = (bf16[2,1280,128]{2,1,0:T(8,128)(2,1)}, bf16[2,1280,128]{2,1,0:T(8,128)(2,1)S(1)}, u32[]{:S(2)}, u32[]{:S(2)}) collective-permute-start(bf16[2,1280,128]{2,1,0:T(8,128)(2,1)} %get-tuple-element.141), channel_id=1, source_target_pairs={{0,4},{1,5},{2,6},{3,7},{4,0},{5,1},{6,2},{7,3},{8,12},{9,13},{10,... | collective-permute-start | bytes 1966088 | tf_op jit(solution)/shard_map/ppermute | solution.py:195
  157.9 42.8 %collective-permute-start.16 = (bf16[2,1280,128]{2,1,0:T(8,128)(2,1)}, bf16[2,1280,128]{2,1,0:T(8,128)(2,1)S(1)}, u32[]{:S(2)}, u32[]{:S(2)}) collective-permute-start(bf16[2,1280,128]{2,1,0:T(8,128)(2,1)} %get-tuple-element.142), channel_id=1, source_target_pairs={{0,2},{1,3},{2,0},{3,1},{4,6},{5,7},{6,4},{7,5},{8,10},{9,11},{10,... | collective-permute-start | bytes 1966088 | tf_op jit(solution)/shard_map/ppermute | solution.py:195
  159.0 42.6 %collective-permute-start.17 = (bf16[2,1280,128]{2,1,0:T(8,128)(2,1)}, bf16[2,1280,128]{2,1,0:T(8,128)(2,1)S(1)}, u32[]{:S(2)}, u32[]{:S(2)}) collective-permute-start(bf16[2,1280,128]{2,1,0:T(8,128)(2,1)} %get-tuple-element.143), channel_id=1, source_target_pairs={{0,7},{1,6},{2,5},{3,4},{4,3},{5,2},{6,1},{7,0},{8,15},{9,14},{10,... | collective-permute-start | bytes 1966088 | tf_op jit(solution)/shard_map/ppermute | solution.py:195
  159.9 54.1 %collective-permute-start.18 = (bf16[2,1280,128]{2,1,0:T(8,128)(2,1)}, bf16[2,1280,128]{2,1,0:T(8,128)(2,1)S(1)}, u32[]{:S(2)}, u32[]{:S(2)}) collective-permute-start(bf16[2,1280,128]{2,1,0:T(8,128)(2,1)} %get-tuple-element.144), channel_id=1, source_target_pairs={{0,5},{1,4},{2,7},{3,6},{4,1},{5,0},{6,3},{7,2},{8,13},{9,12},{10,... | collective-permute-start | bytes 1966088 | tf_op jit(solution)/shard_map/ppermute | solution.py:195
  172.2 43.1 %collective-permute-start.19 = (bf16[2,1280,128]{2,1,0:T(8,128)(2,1)}, bf16[2,1280,128]{2,1,0:T(8,128)(2,1)}, u32[]{:S(2)}, u32[]{:S(2)}) collective-permute-start(bf16[2,1280,128]{2,1,0:T(8,128)(2,1)} %get-tuple-element.145), channel_id=1, source_target_pairs={{0,3},{1,2},{2,1},{3,0},{4,7},{5,6},{6,5},{7,4},{8,11},{9,10},{10,... | collective-permute-start | bytes 1966088 | tf_op jit(solution)/shard_map/ppermute | solution.py:195
  186.1 30.4 %collective-permute-start.20 = (bf16[2,1280,128]{2,1,0:T(8,128)(2,1)}, bf16[2,1280,128]{2,1,0:T(8,128)(2,1)}, u32[]{:S(2)}, u32[]{:S(2)}) collective-permute-start(bf16[2,1280,128]{2,1,0:T(8,128)(2,1)} %get-tuple-element.146), channel_id=1, source_target_pairs={{0,1},{1,0},{2,3},{3,2},{4,5},{5,4},{6,7},{7,6},{8,9},{9,8},{10,11... | collective-permute-start | bytes 1966088 | tf_op jit(solution)/shard_map/ppermute | solution.py:195
  200.7 35.8 %collective-permute-start.42 = (bf16[2,512,128]{2,1,0:T(8,128)(2,1)}, bf16[2,512,128]{2,1,0:T(8,128)(2,1)S(1)}, u32[]{:S(2)}, u32[]{:S(2)}) collective-permute-start(bf16[2,512,128]{2,1,0:T(8,128)(2,1)} %get-tuple-element.202), channel_id=1, source_target_pairs={{0,6},{1,7},{2,4},{3,5},{4,2},{5,3},{6,0},{7,1},{8,14},{9,15},{10,... | collective-permute-start | bytes 786440 | tf_op jit(solution)/shard_map/ppermute | solution.py:195
  201.6 36.4 %collective-permute-start.43 = (bf16[2,512,128]{2,1,0:T(8,128)(2,1)}, bf16[2,512,128]{2,1,0:T(8,128)(2,1)S(1)}, u32[]{:S(2)}, u32[]{:S(2)}) collective-permute-start(bf16[2,512,128]{2,1,0:T(8,128)(2,1)} %get-tuple-element.203), channel_id=1, source_target_pairs={{0,4},{1,5},{2,6},{3,7},{4,0},{5,1},{6,2},{7,3},{8,12},{9,13},{10,... | collective-permute-start | bytes 786440 | tf_op jit(solution)/shard_map/ppermute | solution.py:195
  216.6 28.9 %collective-permute-start.44 = (bf16[2,512,128]{2,1,0:T(8,128)(2,1)}, bf16[2,512,128]{2,1,0:T(8,128)(2,1)S(1)}, u32[]{:S(2)}, u32[]{:S(2)}) collective-permute-start(bf16[2,512,128]{2,1,0:T(8,128)(2,1)} %get-tuple-element.204), channel_id=1, source_target_pairs={{0,2},{1,3},{2,0},{3,1},{4,6},{5,7},{6,4},{7,5},{8,10},{9,11},{10,... | collective-permute-start | bytes 786440 | tf_op jit(solution)/shard_map/ppermute | solution.py:195
  222.8 24.7 %collective-permute-start.45 = (bf16[2,512,128]{2,1,0:T(8,128)(2,1)}, bf16[2,512,128]{2,1,0:T(8,128)(2,1)S(1)}, u32[]{:S(2)}, u32[]{:S(2)}) collective-permute-start(bf16[2,512,128]{2,1,0:T(8,128)(2,1)} %get-tuple-element.205), channel_id=1, source_target_pairs={{0,7},{1,6},{2,5},{3,4},{4,3},{5,2},{6,1},{7,0},{8,15},{9,14},{10,... | collective-permute-start | bytes 786440 | tf_op jit(solution)/shard_map/ppermute | solution.py:195
  245.5 26.9 %collective-permute-start.37 = (bf16[2,256,128]{2,1,0:T(8,128)(2,1)S(1)}, bf16[2,256,128]{2,1,0:T(8,128)(2,1)S(1)}, u32[]{:S(2)}, u32[]{:S(2)}) collective-permute-start(bf16[2,256,128]{2,1,0:T(8,128)(2,1)S(1)} %copy-done.55), channel_id=1, source_target_pairs={{0,2},{1,3},{2,0},{3,1},{4,6},{5,7},{6,4},{7,5},{8,10},{9,11},{10,... | collective-permute-start | bytes 393224 | tf_op jit(solution)/shard_map/ppermute | solution.py:195
  247.5 25.0 %collective-permute-start.38 = (bf16[2,256,128]{2,1,0:T(8,128)(2,1)S(1)}, bf16[2,256,128]{2,1,0:T(8,128)(2,1)S(1)}, u32[]{:S(2)}, u32[]{:S(2)}) collective-permute-start(bf16[2,256,128]{2,1,0:T(8,128)(2,1)S(1)} %copy-done.54), channel_id=1, source_target_pairs={{0,7},{1,6},{2,5},{3,4},{4,3},{5,2},{6,1},{7,0},{8,15},{9,14},{10,... | collective-permute-start | bytes 393224 | tf_op jit(solution)/shard_map/ppermute | solution.py:195
  249.2 23.3 %collective-permute-start.39 = (bf16[2,256,128]{2,1,0:T(8,128)(2,1)S(1)}, bf16[2,256,128]{2,1,0:T(8,128)(2,1)S(1)}, u32[]{:S(2)}, u32[]{:S(2)}) collective-permute-start(bf16[2,256,128]{2,1,0:T(8,128)(2,1)S(1)} %copy-done.53), channel_id=1, source_target_pairs={{0,5},{1,4},{2,7},{3,6},{4,1},{5,0},{6,3},{7,2},{8,13},{9,12},{10,... | collective-permute-start | bytes 393224 | tf_op jit(solution)/shard_map/ppermute | solution.py:195
  (88 other events, 1380.4 us)

commit v3 on v2

--- a/solution.py
+++ b/solution.py
@@ -14,9 +14,9 @@
 PEERS = 8
 GROUP = 32
 WRAP = 256
-CHUNKS = ((256, 512), (768, 1280), (2048, 1280), (3328, 512), (3840, 256))
+CHUNKS = ((256, 256), (512, 1280), (1792, 1280), (3072, 896), (3968, 128))
 BLOCK = 256
-ORDER = (6, 4, 2, 7, 5, 3, 1)
+ORDER = (4, 2, 6, 5, 3, 7, 1)
 VMEM_LIMIT = 60 * 1024 * 1024
 
 
@@ -158,7 +158,7 @@
 
 def interleave(first, me, row_len, new, own, pieces, caches):
     count, dim = pieces[0].shape[1:]
-    block = min(count, BLOCK)
+    block = BLOCK if count % BLOCK == 0 else BLOCK // 2
     tiles = count // block
     cache = jax.ShapeDtypeStruct((WINDOW * PEERS, dim), jnp.bfloat16)
     any_spec = pl.BlockSpec(memory_space=pltpu.HBM)

time: 280 us -> 294 us (1.050)
  waiting for transfers between devices: 119 us -> 131 us
  starting transfers between devices: 53.8 us -> 57.9 us
    ppermute x56, waiting for transfers between devices: 119 us -> 131 us  [swap(): return lax.ppermute(value, 'sh', [(i, i ^ offset) for i in range(PEERS)])]
    ppermute x56, starting transfers between devices: 53.8 us -> 57.9 us  [swap(): return lax.ppermute(value, 'sh', [(i, i ^ offset) for i in range(PEERS)])]
  transfers between devices with their start and end apart: 56 -> 56, of which waited for: 21 -> 26; matrix products, arithmetic and copies ran while one was open for 10% -> 9% of each run, Pallas kernels for 13% -> 13%
where the time goes in v3:
time: 294 us; the launch traced here: 291 us
  waiting for transfers between devices  131 us (45%)
  starting transfers between devices  57.9 us (20%)
  Pallas kernels  47.2 us (16%)
  matrix products  46.5 us (16%)
  local copies, waits for them, and re-layouts  3.36 us (1%)
    ppermute x56, waiting for transfers between devices, swap(): return lax.ppermute(value, 'sh', [(i, i ^ offset) for i in range(PEERS)])  131 us
    ppermute x56, starting transfers between devices, swap(): return lax.ppermute(value, 'sh', [(i, i ^ offset) for i in range(PEERS)])  57.9 us
    pallas_call x6, Pallas kernels, interleave(): pl.pallas_call(functools.partial(interleave_kernel, first, count, block,...  29.7 us
    pallas_call x5, Pallas kernels, pack(): pl.pallas_call(functools.partial(pack_kernel, first, count), out_shape=[p...  14.9 us
    dot_general x1, matrix products, per_device(): jnp.dot(attn_out, w_out, preferred_element_type=jnp.float32)  13.4 us
    dot_general x1, matrix products, per_device(): jnp.dot(normed, w_query, preferred_element_type=jnp.float32)  13 us
    dot_general x1, matrix products, per_device(): jnp.einsum('bgd,bsd->bgs', q_all, k_mine, preferred_element_type=jnp.floa...  6.02 us
  transfers between devices with their start and end apart: 56, of which 26 were waited for; matrix products, arithmetic and copies ran while one was open for 9% of the time, Pallas kernels for 13%

profile of v3, /device:TPU:0, one launch (start us, length us, event | category | flops | bytes accessed | tf_op | source)
XLA Modules:
  0.0 291.1 jit_solution(12190042600098230690)
XLA Ops:
  2.7 4.0 %shard_map.113 = (bf16[2,1280,128]{2,1,0:T(8,128)(2,1)}, bf16[2,1280,128]{2,1,0:T(8,128)(2,1)}, bf16[2,1280,128]{2,1,0:T(8,128)(2,1)}, bf16[2,1280,128]{2,1,0:T(...) custom-call(s32[1]{0:T(128)} %bitcast.me_ref, ...), custom_call_target="tpu_custom_call" | custom-call | bytes 9175040 | tf_op jit(solution)/shard_map/pallas_call | solution.py:57
  8.1 4.6 %fusion.14 = f32[1,1024]{1,0:T(1,128)S(1)} fusion(bf16[4096,1024]{1,0:T(8,128)(2,1)} %param.15, f32[1,4096]{1,0:T(1,128)S(1)} %bitcast.87, bf16[1,4096]{1,0:T(2,128)(2,1)S(1)} %copy-done, f32[]{:T(128)S(6)} %rsqrt.4), kind=kOutput, calls=%fused_computation.28 | convolution fusion | flops 8404992 | bytes 8417284 | tf_op jit(solution)/shard_map/dot_general | solution.py:233
  13.9 4.6 %fusion.12 = f32[1,1024]{1,0:T(1,128)S(1)} fusion(bf16[4096,1024]{1,0:T(8,128)(2,1)} %param.16, f32[1,4096]{1,0:T(1,128)S(1)} %bitcast.88, bf16[1,4096]{1,0:T(2,128)(2,1)S(1)} %copy-done, f32[]{:T(128)S(6)} %rsqrt.4), kind=kOutput, calls=%fused_computation.26 | convolution fusion | flops 8404992 | bytes 8417284 | tf_op jit(solution)/shard_map/dot_general | solution.py:234
  18.5 13.0 %fusion.16 = f32[1,4096]{1,0:T(1,128)S(1)} fusion(bf16[4096,4096]{1,0:T(8,128)(2,1)} %param.14, f32[1,4096]{1,0:T(1,128)S(1)} %bitcast.89, bf16[1,4096]{1,0:T(2,128)(2,1)S(1)} %copy-done, f32[]{:T(128)S(6)} %rsqrt.4), kind=kOutput, calls=%fused_computation.30 | convolution fusion | flops 33570816 | bytes 33595396 | tf_op jit(solution)/shard_map/dot_general | solution.py:232
  45.9 6.0 %fusion.32 = (f32[8,4]{1,0:T(8,128)S(1)}, f32[8,4,4352]{2,1,0:T(4,128)S(1)}) fusion(bf16[8,4352,1,128]{3,1,2,0:T(8,128)(2,1)} %param.9, bf16[8,6,128]{2,1,0:T(8,128)(2,1)S(1)} %copy_select_fusion, pred[8,4352]{1,0:T(8,128)(4,1)S(1)} %fusion.7), kind=kOutput, calls=%fused_computation.90 | convolution fusion | flops 36069344 | bytes 9513088 | tf_op jit(solution)/shard_map/bgd,bsd->bgs/dot_general | solution.py:250
  52.3 4.9 %fusion.3 = bf16[1,8,4,128]{3,2,1,0:T(4,128)(2,1)S(1)} fusion(f32[8,4,4352]{2,1,0:T(4,128)S(1)} %get-tuple-element.252, f32[8,4]{1,0:T(8,128)S(1)} %get-tuple-element.228, f32[8,4]{1,0:T(8,128)S(1)} %multiply_maximum_fusion, f32[8,128]{1,0:T(8,128)S(1)} %bitcast.91, f32[8,4]{1,0:T(8,128)S(1)} %get-tuple-element.227, bf16[8,4352,1,128]{3,1,2,0:T(8,128)(2,1)} %param.10), kind=kOutput, calls=%fused_computation.8 | convolution fusion | flops 36081664 | bytes 9482624 | tf_op jit(solution)/shard_map/bgs,bsd->bgd/dot_general | solution.py:260
  57.7 5.0 %collective-permute-done.10 = bf16[1,512]{1,0:T(2,128)(2,1)S(1)} collective-permute-done((bf16[1,512]{1,0:T(2,128)(2,1)S(1)}, bf16[1,512]{1,0:T(2,128)(2,1)S(1)}, u32[]{:S(2)}, u32[]{:S(2)}) %collective-permute-start.10) | collective-permute-done | bytes 1056 | tf_op jit(solution)/shard_map/ppermute | solution.py:195
  103.6 28.9 %collective-permute-done.54.refs_6_ = bf16[2,256,128]{2,1,0:T(8,128)(2,1)S(1)} collective-permute-done((bf16[2,256,128]{2,1,0:T(8,128)(2,1)}, bf16[2,256,128]{2,1,0:T(8,128)(2,1)S(1)}, u32[]{:S(2)}, u32[]{:S(2)}) %collective-permute-start.54) | collective-permute-done | bytes 131104 | tf_op jit(solution)/shard_map/ppermute | solution.py:195
  136.0 4.0 %shard_map.114 = (bf16[2,1280,128]{2,1,0:T(8,128)(2,1)}, bf16[2,1280,128]{2,1,0:T(8,128)(2,1)}, bf16[2,1280,128]{2,1,0:T(8,128)(2,1)}, bf16[2,1280,128]{2,1,0:T(...) custom-call(s32[1]{0:T(128)} %bitcast.me_ref, ...), custom_call_target="tpu_custom_call" | custom-call | bytes 9175040 | tf_op jit(solution)/shard_map/pallas_call | solution.py:57
  142.7 8.5 %collective-permute-done.25.refs_6_ = bf16[2,1280,128]{2,1,0:T(8,128)(2,1)S(1)} collective-permute-done((bf16[2,1280,128]{2,1,0:T(8,128)(2,1)}, bf16[2,1280,128]{2,1,0:T(8,128)(2,1)S(1)}, u32[]{:S(2)}, u32[]{:S(2)}) %collective-permute-start.25) | collective-permute-done | bytes 655392 | tf_op jit(solution)/shard_map/ppermute | solution.py:195
  152.3 12.9 %collective-permute-done.26.refs_7_ = bf16[2,1280,128]{2,1,0:T(8,128)(2,1)} collective-permute-done((bf16[2,1280,128]{2,1,0:T(8,128)(2,1)}, bf16[2,1280,128]{2,1,0:T(8,128)(2,1)}, u32[]{:S(2)}, u32[]{:S(2)}) %collective-permute-start.26) | collective-permute-done | bytes 655392 | tf_op jit(solution)/shard_map/ppermute | solution.py:195
  167.5 4.8 %collective-permute-done.14.refs_2_ = bf16[2,1280,128]{2,1,0:T(8,128)(2,1)S(1)} collective-permute-done((bf16[2,1280,128]{2,1,0:T(8,128)(2,1)}, bf16[2,1280,128]{2,1,0:T(8,128)(2,1)S(1)}, u32[]{:S(2)}, u32[]{:S(2)}) %collective-permute-start.14) | collective-permute-done | bytes 655392 | tf_op jit(solution)/shard_map/ppermute | solution.py:195
  172.4 7.6 %collective-permute-done.15.refs_3_ = bf16[2,1280,128]{2,1,0:T(8,128)(2,1)S(1)} collective-permute-done((bf16[2,1280,128]{2,1,0:T(8,128)(2,1)}, bf16[2,1280,128]{2,1,0:T(8,128)(2,1)S(1)}, u32[]{:S(2)}, u32[]{:S(2)}) %collective-permute-start.15) | collective-permute-done | bytes 655392 | tf_op jit(solution)/shard_map/ppermute | solution.py:195
  180.7 4.1 %shard_map.115 = (bf16[32768,128]{1,0:T(8,128)(2,1)}, bf16[32768,128]{1,0:T(8,128)(2,1)}) custom-call(s32[1]{0:T(128)} %bitcast.me_ref, s32[1]{0:T(128)} %dynamic_slice.51.len_ref, f32[2,8,128]{2,1,0:T(8,128)} %maximum_convert_fusion.new_ref, bf16[8,4352,128]{2,1,0:T(8,128)(2,1)} %bitcast.78, bf16[8,4352,128]{2,1,0:T(8,128)(2,1)} %bitcast.66, ...), custom_call_target="tpu_custom_call" | custom-call | flops 2097152 | bytes 2097152 | tf_op jit(solution)/shard_map/pallas_call | solution.py:172
  184.8 6.6 %shard_map.116 = (bf16[32768,128]{1,0:T(8,128)(2,1)}, bf16[32768,128]{1,0:T(8,128)(2,1)}) custom-call(s32[1]{0:T(128)} %bitcast.me_ref, s32[1]{0:T(128)} %dynamic_slice.51.len_ref, f32[2,8,128]{2,1,0:T(8,128)} %maximum_convert_fusion.new_ref, bf16[8,4352,128]{2,1,0:T(8,128)(2,1)} %bitcast.79, ...), custom_call_target="tpu_custom_call", output_to_operand_aliasing={{0}: (12, {}), {1}: (13, {})} | custom-call | flops 10485760 | bytes 10485760 | tf_op jit(solution)/shard_map/pallas_call | solution.py:172
  202.0 5.4 %collective-permute-done.18.refs_6_ = bf16[2,1280,128]{2,1,0:T(8,128)(2,1)S(1)} collective-permute-done((bf16[2,1280,128]{2,1,0:T(8,128)(2,1)}, bf16[2,1280,128]{2,1,0:T(8,128)(2,1)S(1)}, u32[]{:S(2)}, u32[]{:S(2)}) %collective-permute-start.18) | collective-permute-done | bytes 655392 | tf_op jit(solution)/shard_map/ppermute | solution.py:195
  207.8 13.7 %collective-permute-done.19.refs_7_ = bf16[2,1280,128]{2,1,0:T(8,128)(2,1)} collective-permute-done((bf16[2,1280,128]{2,1,0:T(8,128)(2,1)}, bf16[2,1280,128]{2,1,0:T(8,128)(2,1)}, u32[]{:S(2)}, u32[]{:S(2)}) %collective-permute-start.19) | collective-permute-done | bytes 655392 | tf_op jit(solution)/shard_map/ppermute | solution.py:195
  225.5 7.9 %collective-permute-done.36.refs_3_ = bf16[2,128,128]{2,1,0:T(8,128)(2,1)S(1)} collective-permute-done((bf16[2,128,128]{2,1,0:T(8,128)(2,1)}, bf16[2,128,128]{2,1,0:T(8,128)(2,1)S(1)}, u32[]{:S(2)}, u32[]{:S(2)}) %collective-permute-start.36) | collective-permute-done | bytes 65568 | tf_op jit(solution)/shard_map/ppermute | solution.py:195
  235.4 6.6 %shard_map.119 = (bf16[32768,128]{1,0:T(8,128)(2,1)}, bf16[32768,128]{1,0:T(8,128)(2,1)}) custom-call(s32[1]{0:T(128)} %bitcast.me_ref, s32[1]{0:T(128)} %dynamic_slice.51.len_ref, f32[2,8,128]{2,1,0:T(8,128)} %maximum_convert_fusion.new_ref, bf16[8,4352,128]{2,1,0:T(8,128)(2,1)} %bitcast.82, ...), custom_call_target="tpu_custom_call", output_to_operand_aliasing={{0}: (12, {}), {1}: (13, {})} | custom-call | flops 10485760 | bytes 10485760 | tf_op jit(solution)/shard_map/pallas_call | solution.py:172
  248.3 4.1 %collective-permute-done.46.refs_6_ = bf16[2,896,128]{2,1,0:T(8,128)(2,1)S(1)} collective-permute-done((bf16[2,896,128]{2,1,0:T(8,128)(2,1)}, bf16[2,896,128]{2,1,0:T(8,128)(2,1)S(1)}, u32[]{:S(2)}, u32[]{:S(2)}) %collective-permute-start.46) | collective-permute-done | bytes 458784 | tf_op jit(solution)/shard_map/ppermute | solution.py:195
  253.8 8.4 %collective-permute-done.47.refs_7_ = bf16[2,896,128]{2,1,0:T(8,128)(2,1)} collective-permute-done((bf16[2,896,128]{2,1,0:T(8,128)(2,1)}, bf16[2,896,128]{2,1,0:T(8,128)(2,1)}, u32[]{:S(2)}, u32[]{:S(2)}) %collective-permute-start.47) | collective-permute-done | bytes 458784 | tf_op jit(solution)/shard_map/ppermute | solution.py:195
  264.3 13.4 %fusion.1 = bf16[1,4096]{1,0:T(2,128)(2,1)} fusion(bf16[4096,1]{0,1:T(2,128)(2,1)S(1)} %bitcast.92, bf16[4096,4096]{1,0:T(8,128)(2,1)} %param.17, bf16[1,4096]{1,0:T(2,128)(2,1)S(1)} %copy-done), kind=kOutput, calls=%fused_computation.5 | convolution fusion | flops 33566720 | bytes 33579008 | tf_op jit(solution)/shard_map/dot_general | solution.py:278
  277.7 3.6 %shard_map.121 = (bf16[32768,128]{1,0:T(8,128)(2,1)}, bf16[32768,128]{1,0:T(8,128)(2,1)}) custom-call(s32[1]{0:T(128)} %bitcast.me_ref, s32[1]{0:T(128)} %dynamic_slice.51.len_ref, f32[2,8,128]{2,1,0:T(8,128)} %maximum_convert_fusion.new_ref, bf16[2,256,128]{2,1,0:T(8,128)(2,1)} %get-tuple-element.209.refs_0_, ...), custom_call_target="tpu_custom_call", output_to_operand_aliasing={{0}: (11, {}), {1}: (12, {})} | custom-call | flops 2097152 | bytes 2097152 | tf_op jit(solution)/shard_map/pallas_call | solution.py:172
  281.3 5.6 %shard_map.122 = (bf16[32768,128]{1,0:T(8,128)(2,1)}, bf16[32768,128]{1,0:T(8,128)(2,1)}) custom-call(s32[1]{0:T(128)} %bitcast.me_ref, s32[1]{0:T(128)} %dynamic_slice.51.len_ref, f32[2,8,128]{2,1,0:T(8,128)} %maximum_convert_fusion.new_ref, bf16[8,4352,128]{2,1,0:T(8,128)(2,1)} %bitcast.83, ...), custom_call_target="tpu_custom_call", output_to_operand_aliasing={{0}: (12, {}), {1}: (13, {})} | custom-call | flops 7340032 | bytes 7340032 | tf_op jit(solution)/shard_map/pallas_call | solution.py:172
  (237 shorter events, 100.2 us)
Async XLA Ops:
  39.9 43.3 %collective-permute-start.28 = (bf16[2,256,128]{2,1,0:T(8,128)(2,1)S(1)}, bf16[2,256,128]{2,1,0:T(8,128)(2,1)S(1)}, u32[]{:S(2)}, u32[]{:S(2)}) collective-permute-start(bf16[2,256,128]{2,1,0:T(8,128)(2,1)S(1)} %copy-done.42), channel_id=1, source_target_pairs={{0,4},{1,5},{2,6},{3,7},{4,0},{5,1},{6,2},{7,3},{8,12},{9,13},{10,... | collective-permute-start | bytes 393224 | tf_op jit(solution)/shard_map/ppermute | solution.py:195
  41.6 43.2 %collective-permute-start.29 = (bf16[2,256,128]{2,1,0:T(8,128)(2,1)S(1)}, bf16[2,256,128]{2,1,0:T(8,128)(2,1)S(1)}, u32[]{:S(2)}, u32[]{:S(2)}) collective-permute-start(bf16[2,256,128]{2,1,0:T(8,128)(2,1)S(1)} %copy-done.41), channel_id=1, source_target_pairs={{0,2},{1,3},{2,0},{3,1},{4,6},{5,7},{6,4},{7,5},{8,10},{9,11},{10,... | collective-permute-start | bytes 393224 | tf_op jit(solution)/shard_map/ppermute | solution.py:195
  43.1 41.8 %collective-permute-start.30 = (bf16[2,256,128]{2,1,0:T(8,128)(2,1)S(1)}, bf16[2,256,128]{2,1,0:T(8,128)(2,1)S(1)}, u32[]{:S(2)}, u32[]{:S(2)}) collective-permute-start(bf16[2,256,128]{2,1,0:T(8,128)(2,1)S(1)} %copy-done.40), channel_id=1, source_target_pairs={{0,6},{1,7},{2,4},{3,5},{4,2},{5,3},{6,0},{7,1},{8,14},{9,15},{10,... | collective-permute-start | bytes 393224 | tf_op jit(solution)/shard_map/ppermute | solution.py:195
  43.5 91.3 %collective-permute-start.21 = (bf16[2,1280,128]{2,1,0:T(8,128)(2,1)}, bf16[2,1280,128]{2,1,0:T(8,128)(2,1)S(1)}, u32[]{:S(2)}, u32[]{:S(2)}) collective-permute-start(bf16[2,1280,128]{2,1,0:T(8,128)(2,1)} %get-tuple-element.147), channel_id=1, source_target_pairs={{0,4},{1,5},{2,6},{3,7},{4,0},{5,1},{6,2},{7,3},{8,12},{9,13},{10,... | collective-permute-start | bytes 1966088 | tf_op jit(solution)/shard_map/ppermute | solution.py:195
  95.5 44.5 %collective-permute-start.22 = (bf16[2,1280,128]{2,1,0:T(8,128)(2,1)}, bf16[2,1280,128]{2,1,0:T(8,128)(2,1)S(1)}, u32[]{:S(2)}, u32[]{:S(2)}) collective-permute-start(bf16[2,1280,128]{2,1,0:T(8,128)(2,1)} %get-tuple-element.148), channel_id=1, source_target_pairs={{0,2},{1,3},{2,0},{3,1},{4,6},{5,7},{6,4},{7,5},{8,10},{9,11},{10,... | collective-permute-start | bytes 1966088 | tf_op jit(solution)/shard_map/ppermute | solution.py:195
  98.4 42.1 %collective-permute-start.23 = (bf16[2,1280,128]{2,1,0:T(8,128)(2,1)}, bf16[2,1280,128]{2,1,0:T(8,128)(2,1)S(1)}, u32[]{:S(2)}, u32[]{:S(2)}) collective-permute-start(bf16[2,1280,128]{2,1,0:T(8,128)(2,1)} %get-tuple-element.149), channel_id=1, source_target_pairs={{0,6},{1,7},{2,4},{3,5},{4,2},{5,3},{6,0},{7,1},{8,14},{9,15},{10,... | collective-permute-start | bytes 1966088 | tf_op jit(solution)/shard_map/ppermute | solution.py:195
  101.1 31.5 %collective-permute-start.54 = (bf16[2,256,128]{2,1,0:T(8,128)(2,1)}, bf16[2,256,128]{2,1,0:T(8,128)(2,1)S(1)}, u32[]{:S(2)}, u32[]{:S(2)}) collective-permute-start(bf16[2,256,128]{2,1,0:T(8,128)(2,1)} %get-tuple-element.215), channel_id=1, source_target_pairs={{0,7},{1,6},{2,5},{3,4},{4,3},{5,2},{6,1},{7,0},{8,15},{9,14},{10,... | collective-permute-start | bytes 393224 | tf_op jit(solution)/shard_map/ppermute | solution.py:195
  102.6 39.1 %collective-permute-start.24 = (bf16[2,1280,128]{2,1,0:T(8,128)(2,1)}, bf16[2,1280,128]{2,1,0:T(8,128)(2,1)S(1)}, u32[]{:S(2)}, u32[]{:S(2)}) collective-permute-start(bf16[2,1280,128]{2,1,0:T(8,128)(2,1)} %get-tuple-element.150), channel_id=1, source_target_pairs={{0,5},{1,4},{2,7},{3,6},{4,1},{5,0},{6,3},{7,2},{8,13},{9,12},{10,... | collective-permute-start | bytes 1966088 | tf_op jit(solution)/shard_map/ppermute | solution.py:195
  134.8 30.4 %collective-permute-start.26 = (bf16[2,1280,128]{2,1,0:T(8,128)(2,1)}, bf16[2,1280,128]{2,1,0:T(8,128)(2,1)}, u32[]{:S(2)}, u32[]{:S(2)}) collective-permute-start(bf16[2,1280,128]{2,1,0:T(8,128)(2,1)} %get-tuple-element.152), channel_id=1, source_target_pairs={{0,7},{1,6},{2,5},{3,4},{4,3},{5,2},{6,1},{7,0},{8,15},{9,14},{10,... | collective-permute-start | bytes 1966088 | tf_op jit(solution)/shard_map/ppermute | solution.py:195
  140.1 26.8 %collective-permute-start.27 = (bf16[2,1280,128]{2,1,0:T(8,128)(2,1)}, bf16[2,1280,128]{2,1,0:T(8,128)(2,1)S(1)}, u32[]{:S(2)}, u32[]{:S(2)}) collective-permute-start(bf16[2,1280,128]{2,1,0:T(8,128)(2,1)} %get-tuple-element.153), channel_id=1, source_target_pairs={{0,1},{1,0},{2,3},{3,2},{4,5},{5,4},{6,7},{7,6},{8,9},{9,8},{10,11... | collective-permute-start | bytes 1966088 | tf_op jit(solution)/shard_map/ppermute | solution.py:195
  140.5 31.9 %collective-permute-start.14 = (bf16[2,1280,128]{2,1,0:T(8,128)(2,1)}, bf16[2,1280,128]{2,1,0:T(8,128)(2,1)S(1)}, u32[]{:S(2)}, u32[]{:S(2)}) collective-permute-start(bf16[2,1280,128]{2,1,0:T(8,128)(2,1)} %get-tuple-element.140), channel_id=1, source_target_pairs={{0,4},{1,5},{2,6},{3,7},{4,0},{5,1},{6,2},{7,3},{8,12},{9,13},{10,... | collective-permute-start | bytes 1966088 | tf_op jit(solution)/shard_map/ppermute | solution.py:195
  141.7 38.2 %collective-permute-start.15 = (bf16[2,1280,128]{2,1,0:T(8,128)(2,1)}, bf16[2,1280,128]{2,1,0:T(8,128)(2,1)S(1)}, u32[]{:S(2)}, u32[]{:S(2)}) collective-permute-start(bf16[2,1280,128]{2,1,0:T(8,128)(2,1)} %get-tuple-element.141), channel_id=1, source_target_pairs={{0,2},{1,3},{2,0},{3,1},{4,6},{5,7},{6,4},{7,5},{8,10},{9,11},{10,... | collective-permute-start | bytes 1966088 | tf_op jit(solution)/shard_map/ppermute | solution.py:195
  151.1 43.3 %collective-permute-start.16 = (bf16[2,1280,128]{2,1,0:T(8,128)(2,1)}, bf16[2,1280,128]{2,1,0:T(8,128)(2,1)S(1)}, u32[]{:S(2)}, u32[]{:S(2)}) collective-permute-start(bf16[2,1280,128]{2,1,0:T(8,128)(2,1)} %get-tuple-element.142), channel_id=1, source_target_pairs={{0,6},{1,7},{2,4},{3,5},{4,2},{5,3},{6,0},{7,1},{8,14},{9,15},{10,... | collective-permute-start | bytes 1966088 | tf_op jit(solution)/shard_map/ppermute | solution.py:195
  165.2 34.1 %collective-permute-start.17 = (bf16[2,1280,128]{2,1,0:T(8,128)(2,1)}, bf16[2,1280,128]{2,1,0:T(8,128)(2,1)S(1)}, u32[]{:S(2)}, u32[]{:S(2)}) collective-permute-start(bf16[2,1280,128]{2,1,0:T(8,128)(2,1)} %get-tuple-element.143), channel_id=1, source_target_pairs={{0,5},{1,4},{2,7},{3,6},{4,1},{5,0},{6,3},{7,2},{8,13},{9,12},{10,... | collective-permute-start | bytes 1966088 | tf_op jit(solution)/shard_map/ppermute | solution.py:195
  166.9 40.5 %collective-permute-start.18 = (bf16[2,1280,128]{2,1,0:T(8,128)(2,1)}, bf16[2,1280,128]{2,1,0:T(8,128)(2,1)S(1)}, u32[]{:S(2)}, u32[]{:S(2)}) collective-permute-start(bf16[2,1280,128]{2,1,0:T(8,128)(2,1)} %get-tuple-element.144), channel_id=1, source_target_pairs={{0,3},{1,2},{2,1},{3,0},{4,7},{5,6},{6,5},{7,4},{8,11},{9,10},{10,... | collective-permute-start | bytes 1966088 | tf_op jit(solution)/shard_map/ppermute | solution.py:195
  172.3 49.1 %collective-permute-start.19 = (bf16[2,1280,128]{2,1,0:T(8,128)(2,1)}, bf16[2,1280,128]{2,1,0:T(8,128)(2,1)}, u32[]{:S(2)}, u32[]{:S(2)}) collective-permute-start(bf16[2,1280,128]{2,1,0:T(8,128)(2,1)} %get-tuple-element.145), channel_id=1, source_target_pairs={{0,7},{1,6},{2,5},{3,4},{4,3},{5,2},{6,1},{7,0},{8,15},{9,14},{10,... | collective-permute-start | bytes 1966088 | tf_op jit(solution)/shard_map/ppermute | solution.py:195
  179.9 42.9 %collective-permute-start.20 = (bf16[2,1280,128]{2,1,0:T(8,128)(2,1)}, bf16[2,1280,128]{2,1,0:T(8,128)(2,1)}, u32[]{:S(2)}, u32[]{:S(2)}) collective-permute-start(bf16[2,1280,128]{2,1,0:T(8,128)(2,1)} %get-tuple-element.146), channel_id=1, source_target_pairs={{0,1},{1,0},{2,3},{3,2},{4,5},{5,4},{6,7},{7,6},{8,9},{9,8},{10,11... | collective-permute-start | bytes 1966088 | tf_op jit(solution)/shard_map/ppermute | solution.py:195
  194.5 38.9 %collective-permute-start.42 = (bf16[2,896,128]{2,1,0:T(8,128)(2,1)}, bf16[2,896,128]{2,1,0:T(8,128)(2,1)S(1)}, u32[]{:S(2)}, u32[]{:S(2)}) collective-permute-start(bf16[2,896,128]{2,1,0:T(8,128)(2,1)} %get-tuple-element.202), channel_id=1, source_target_pairs={{0,4},{1,5},{2,6},{3,7},{4,0},{5,1},{6,2},{7,3},{8,12},{9,13},{10,... | collective-permute-start | bytes 1376264 | tf_op jit(solution)/shard_map/ppermute | solution.py:195
  199.3 36.0 %collective-permute-start.43 = (bf16[2,896,128]{2,1,0:T(8,128)(2,1)}, bf16[2,896,128]{2,1,0:T(8,128)(2,1)S(1)}, u32[]{:S(2)}, u32[]{:S(2)}) collective-permute-start(bf16[2,896,128]{2,1,0:T(8,128)(2,1)} %get-tuple-element.203), channel_id=1, source_target_pairs={{0,2},{1,3},{2,0},{3,1},{4,6},{5,7},{6,4},{7,5},{8,10},{9,11},{10,... | collective-permute-start | bytes 1376264 | tf_op jit(solution)/shard_map/ppermute | solution.py:195
  233.4 28.8 %collective-permute-start.47 = (bf16[2,896,128]{2,1,0:T(8,128)(2,1)}, bf16[2,896,128]{2,1,0:T(8,128)(2,1)}, u32[]{:S(2)}, u32[]{:S(2)}) collective-permute-start(bf16[2,896,128]{2,1,0:T(8,128)(2,1)} %get-tuple-element.207), channel_id=1, source_target_pairs={{0,7},{1,6},{2,5},{3,4},{4,3},{5,2},{6,1},{7,0},{8,15},{9,14},{10,... | collective-permute-start | bytes 1376264 | tf_op jit(solution)/shard_map/ppermute | solution.py:195
  235.4 28.9 %collective-permute-start.48 = (bf16[2,896,128]{2,1,0:T(8,128)(2,1)}, bf16[2,896,128]{2,1,0:T(8,128)(2,1)}, u32[]{:S(2)}, u32[]{:S(2)}) collective-permute-start(bf16[2,896,128]{2,1,0:T(8,128)(2,1)} %get-tuple-element.208), channel_id=1, source_target_pairs={{0,1},{1,0},{2,3},{3,2},{4,5},{5,4},{6,7},{7,6},{8,9},{9,8},{10,11... | collective-permute-start | bytes 1376264 | tf_op jit(solution)/shard_map/ppermute | solution.py:195
  243.5 43.5 %collective-permute-start.37 = (bf16[2,128,128]{2,1,0:T(8,128)(2,1)S(1)}, bf16[2,128,128]{2,1,0:T(8,128)(2,1)S(1)}, u32[]{:S(2)}, u32[]{:S(2)}) collective-permute-start(bf16[2,128,128]{2,1,0:T(8,128)(2,1)S(1)} %copy-done.47), channel_id=1, source_target_pairs={{0,6},{1,7},{2,4},{3,5},{4,2},{5,3},{6,0},{7,1},{8,14},{9,15},{10,... | collective-permute-start | bytes 196616 | tf_op jit(solution)/shard_map/ppermute | solution.py:195
  247.8 39.2 %collective-permute-start.38 = (bf16[2,128,128]{2,1,0:T(8,128)(2,1)S(1)}, bf16[2,128,128]{2,1,0:T(8,128)(2,1)S(1)}, u32[]{:S(2)}, u32[]{:S(2)}) collective-permute-start(bf16[2,128,128]{2,1,0:T(8,128)(2,1)S(1)} %copy-done.46), channel_id=1, source_target_pairs={{0,5},{1,4},{2,7},{3,6},{4,1},{5,0},{6,3},{7,2},{8,13},{9,12},{10,... | collective-permute-start | bytes 196616 | tf_op jit(solution)/shard_map/ppermute | solution.py:195
  252.5 34.5 %collective-permute-start.39 = (bf16[2,128,128]{2,1,0:T(8,128)(2,1)S(1)}, bf16[2,128,128]{2,1,0:T(8,128)(2,1)S(1)}, u32[]{:S(2)}, u32[]{:S(2)}) collective-permute-start(bf16[2,128,128]{2,1,0:T(8,128)(2,1)S(1)} %copy-done.45), channel_id=1, source_target_pairs={{0,3},{1,2},{2,1},{3,0},{4,7},{5,6},{6,5},{7,4},{8,11},{9,10},{10,... | collective-permute-start | bytes 196616 | tf_op jit(solution)/shard_map/ppermute | solution.py:195
  (80 other events, 1416.3 us)

commit v4 on v3

--- a/solution.py
+++ b/solution.py
@@ -14,10 +14,11 @@
 PEERS = 8
 GROUP = 32
 WRAP = 256
-CHUNKS = ((256, 256), (512, 1280), (1792, 1280), (3072, 896), (3968, 128))
+CHUNKS = ((256, 256), (512, 1280), (1792, 1280), (3072, 640), (3712, 256), (3968, 128))
 BLOCK = 256
-ORDER = (4, 2, 6, 5, 3, 7, 1)
-VMEM_LIMIT = 60 * 1024 * 1024
+ORDER = (6, 4, 2, 7, 5, 3, 1)
+VMEM_LIMIT = 56 * 1024 * 1024
+LAST_VMEM_LIMIT = 8 * 1024 * 1024
 
 
 def rotate(heads, positions):
@@ -32,36 +33,30 @@
     return jnp.concatenate([first_half * cos_part - second_half * sin_part, second_half * cos_part + first_half * sin_part], axis=-1).astype(jnp.bfloat16)
 
 
-def pack_kernel(first, count, me_ref, k_ref, v_ref, *refs):
-    outs = refs[:len(ORDER)]
-    held, in_sems, out_sems = refs[len(ORDER):]
+def pack_kernel(first, count, has_own, me_ref, k_ref, v_ref, *refs):
+    offsets = ORDER + (0,) * has_own
+    outs, sems = refs[:-1], refs[-1]
     me = me_ref[0]
-    reads = []
-    for at, offset in enumerate(ORDER):
+    copies = []
+    for at, offset in enumerate(offsets):
         for kv, src in enumerate((k_ref, v_ref)):
-            reads.append(pltpu.make_async_copy(src.at[me ^ offset, pl.ds(first, count)], held.at[at, kv], in_sems.at[at, kv]))
-            reads[-1].start()
-    writes = []
-    for at, out in enumerate(outs):
-        reads[2 * at].wait()
-        reads[2 * at + 1].wait()
-        writes.append(pltpu.make_async_copy(held.at[at], out, out_sems.at[at]))
-        writes[-1].start()
-    for write in writes:
-        write.wait()
-
-
-def pack(first, count, me, k_mine, v_mine):
+            copies.append(pltpu.make_async_copy(src.at[me ^ offset, pl.ds(first, count)], outs[at].at[kv], sems.at[at, kv]))
+            copies[-1].start()
+    for copy in copies:
+        copy.wait()
+
+
+def pack(first, count, has_own, me, k_mine, v_mine):
     dim = k_mine.shape[2]
-    piece = jax.ShapeDtypeStruct((2, count, dim), jnp.bfloat16)
+    pieces = len(ORDER) + has_own
     return pl.pallas_call(
-        functools.partial(pack_kernel, first, count),
-        out_shape=[piece] * len(ORDER),
+        functools.partial(pack_kernel, first, count, has_own),
+        out_shape=[jax.ShapeDtypeStruct((2, count, dim), jnp.bfloat16)] * pieces,
         in_specs=[pl.BlockSpec(memory_space=pltpu.SMEM)] + [pl.BlockSpec(memory_space=pltpu.HBM)] * 2,
-        out_specs=[pl.BlockSpec(memory_space=pltpu.HBM)] * len(ORDER),
-        scratch_shapes=[pltpu.VMEM((len(ORDER), 2, count, dim), jnp.bfloat16), pltpu.SemaphoreType.DMA((len(ORDER), 2)), pltpu.SemaphoreType.DMA((len(ORDER),))],
+        out_specs=[pl.BlockSpec(memory_space=pltpu.VMEM)] * pieces,
+        scratch_shapes=[pltpu.SemaphoreType.DMA((pieces, 2))],
         compiler_params=pltpu.CompilerParams(vmem_limit_bytes=VMEM_LIMIT),
-        cost_estimate=pl.CostEstimate(flops=0, bytes_accessed=len(ORDER) * 4 * count * dim * 2, transcendentals=0),
+        cost_estimate=pl.CostEstimate(flops=0, bytes_accessed=pieces * 4 * count * dim * 2, transcendentals=0),
     )(me, k_mine, v_mine)
 
 
@@ -186,6 +181,48 @@
     )(*args)
 
 
+def last_kernel(first, count, me_ref, len_ref, new_ref, *refs):
+    pieces = refs[:PEERS]
+    k_out, v_out, mixed, sems = refs[PEERS + 2:]
+    me = me_ref[0]
+    row_len = len_ref[0]
+    new_slot = lax.rem(row_len, WINDOW)
+    by_offset = pieces[-1:] + tuple(pieces[ORDER.index(offset)] for offset in range(1, PEERS))
+    copies = []
+    for kv, out in enumerate((k_out, v_out)):
+        new = jnp.concatenate([new_ref[kv]] * GROUP, axis=0)
+        slot_of_row = lax.broadcasted_iota(jnp.int32, new.shape, 0) // PEERS
+        for at in range(0, count, GROUP):
+            heads = [ref[kv, at:at + GROUP, :] for ref in by_offset]
+            for bit in (1, 2, 4):
+                swapped = (me & bit) != 0
+                heads = [jnp.where(swapped, heads[head ^ bit], heads[head]) for head in range(PEERS)]
+            rows = jnp.swapaxes(jnp.stack(heads, axis=0), 0, 1).reshape(GROUP * PEERS, -1)
+            slots = slot_of_row + (first + at)
+            rows = jnp.where(slots < row_len, rows.astype(jnp.float32), 0.0)
+            rows = jnp.where(slots == new_slot, new, rows)
+            mixed[kv, at * PEERS:(at + GROUP) * PEERS, :] = rows.astype(jnp.bfloat16)
+        copies.append(pltpu.make_async_copy(mixed.at[kv], out.at[pl.ds(first * PEERS, count * PEERS)], sems.at[kv]))
+        copies[-1].start()
+    for copy in copies:
+        copy.wait()
+
+
+def interleave_last(first, me, row_len, new, pieces, caches):
+    count, dim = pieces[0].shape[1:]
+    cache = jax.ShapeDtypeStruct((WINDOW * PEERS, dim), jnp.bfloat16)
+    return pl.pallas_call(
+        functools.partial(last_kernel, first, count),
+        out_shape=[cache, cache],
+        in_specs=[pl.BlockSpec(memory_space=pltpu.SMEM)] * 2 + [pl.BlockSpec(memory_space=pltpu.VMEM)] * (1 + PEERS) + [pl.BlockSpec(memory_space=pltpu.HBM)] * 2,
+        out_specs=[pl.BlockSpec(memory_space=pltpu.HBM)] * 2,
+        input_output_aliases={3 + PEERS: 0, 4 + PEERS: 1},
+        scratch_shapes=[pltpu.VMEM((2, count * PEERS, dim), jnp.bfloat16), pltpu.SemaphoreType.DMA((2,))],
+        compiler_params=pltpu.CompilerParams(vmem_limit_bytes=LAST_VMEM_LIMIT),
+        cost_estimate=pl.CostEstimate(flops=count * 64 * dim, bytes_accessed=count * PEERS * dim * 8, transcendentals=0),
+    )(me, row_len, new, *pieces, *caches)
+
+
 def solution(mesh):
     head_spec = P('dp', None, 'sh', None)
     row_spec = P(('dp', 'sh'))
@@ -218,9 +255,10 @@
             place = me_vec
             if after is not None:
                 place, after = lax.optimization_barrier((place, after))
-            pieces = pack(*chunk, place, k_mine, v_mine)
+            pieces = pack(*chunk, chunk == CHUNKS[-1], place, k_mine, v_mine)
             pieces, before = lax.optimization_barrier((pieces, before))
             send(chunk[0], pieces)
+            received[chunk[0]] += pieces[len(ORDER):]
             return after, before
 
         _, residual = start(CHUNKS[0], before=residual)
@@ -266,6 +304,8 @@
 
         def store(first, caches):
             own = [wrapped[-1]] if first == 0 else [k_mine, v_mine]
+            if first == CHUNKS[-1][0]:
+                return interleave_last(first, place, my_len, new, received[first], caches)
             return interleave(first, place, my_len, new, own, received[first], caches)
 
         caches = store(CHUNKS[0][0], caches)
@@ -273,10 +313,11 @@
         caches, caches = start(CHUNKS[3], after=caches, before=caches)
         caches, caches = start(CHUNKS[4], after=caches, before=caches)
         caches = store(CHUNKS[2][0], caches)
+        caches, caches = start(CHUNKS[5], after=caches, before=caches)
         attn_parts, caches = lax.optimization_barrier((attn_parts, caches))
         attn_out = by_device(attn_parts, me).reshape(1, -1)
         resid_out = (resid_f32 + jnp.dot(attn_out, w_out, preferred_element_type=jnp.float32)).astype(jnp.bfloat16)
-        for first in (0, CHUNKS[3][0], CHUNKS[4][0]):
+        for first in (0,) + tuple(chunk[0] for chunk in CHUNKS[3:]):
             caches = store(first, caches)
         shape = (1, WINDOW, PEERS, head_dim)
         return resid_out, caches[0].reshape(shape), caches[1].reshape(shape)

time: 294 us -> 338 us (1.15)
  waiting for transfers between devices: 131 us -> 157 us
  starting transfers between devices: 57.9 us -> 69.3 us
  Pallas kernels: 47.2 us -> 53 us
    ppermute x56 -> x63, waiting for transfers between devices: 131 us -> 157 us  [swap(): return lax.ppermute(value, 'sh', [(i, i ^ offset) for i in range(PEERS)])]
    ppermute x56 -> x63, starting transfers between devices: 57.9 us -> 69.3 us  [swap(): return lax.ppermute(value, 'sh', [(i, i ^ offset) for i in range(PEERS)])]
    pallas_call x5 -> x7, Pallas kernels: 14.9 us -> 20.8 us  [the longest x6 18.8 us: pack(): pl.pallas_call(functools.partial(pack_kernel, first, count, has_own), out...]
  transfers between devices with their start and end apart: 56 -> 63, of which waited for: 26 -> 21; matrix products, arithmetic and copies ran while one was open for 9% -> 8% of each run, Pallas kernels for 13% -> 13%
where the time goes in v4:
time: 338 us; the launch traced here: 335 us
  waiting for transfers between devices  157 us (46%)
  starting transfers between devices  69.3 us (21%)
  Pallas kernels  53 us (16%)
  matrix products  46.9 us (14%)
  between operations  3.39 us (1%)
    ppermute x63, waiting for transfers between devices, swap(): return lax.ppermute(value, 'sh', [(i, i ^ offset) for i in range(PEERS)])  157 us
    ppermute x63, starting transfers between devices, swap(): return lax.ppermute(value, 'sh', [(i, i ^ offset) for i in range(PEERS)])  69.3 us
    pallas_call x6, Pallas kernels, interleave(): pl.pallas_call(functools.partial(interleave_kernel, first, count, block,...  29.6 us
    pallas_call x6, Pallas kernels, pack(): pl.pallas_call(functools.partial(pack_kernel, first, count, has_own), out...  18.8 us
    dot_general x1, matrix products, per_device(): jnp.dot(attn_out, w_out, preferred_element_type=jnp.float32)  13.6 us
    dot_general x1, matrix products, per_device(): jnp.dot(normed, w_query, preferred_element_type=jnp.float32)  13 us
  transfers between devices with their start and end apart: 63, of which 21 were waited for; matrix products, arithmetic and copies ran while one was open for 8% of the time, Pallas kernels for 13%

profile of v4, /device:TPU:0, one launch (start us, length us, event | category | flops | bytes accessed | tf_op | source)
XLA Modules:
  0.0 335.1 jit_solution(18074749692999604861)
XLA Ops:
  3.0 4.5 %shard_map.113 = (bf16[2,1280,128]{2,1,0:T(8,128)(2,1)}, bf16[2,1280,128]{2,1,0:T(8,128)(2,1)}, bf16[2,1280,128]{2,1,0:T(8,128)(2,1)}, bf16[2,1280,128]{2,1,0:T(...) custom-call(s32[1]{0:T(128)} %bitcast.me_ref, ...), custom_call_target="tpu_custom_call" | custom-call | bytes 9175040 | tf_op jit(solution)/shard_map/pallas_call | solution.py:52
  8.8 4.6 %fusion.14 = f32[1,1024]{1,0:T(1,128)S(1)} fusion(bf16[4096,1024]{1,0:T(8,128)(2,1)} %param.15, f32[1,4096]{1,0:T(1,128)S(1)} %bitcast.89, bf16[1,4096]{1,0:T(2,128)(2,1)S(1)} %copy-done.2, f32[]{:T(128)S(6)} %rsqrt.4), kind=kOutput, calls=%fused_computation.28 | convolution fusion | flops 8404992 | bytes 8417284 | tf_op jit(solution)/shard_map/dot_general | solution.py:271
  14.8 4.6 %fusion.12 = f32[1,1024]{1,0:T(1,128)S(1)} fusion(bf16[4096,1024]{1,0:T(8,128)(2,1)} %param.16, f32[1,4096]{1,0:T(1,128)S(1)} %bitcast.90, bf16[1,4096]{1,0:T(2,128)(2,1)S(1)} %copy-done.2, f32[]{:T(128)S(6)} %rsqrt.4), kind=kOutput, calls=%fused_computation.26 | convolution fusion | flops 8404992 | bytes 8417284 | tf_op jit(solution)/shard_map/dot_general | solution.py:272
  19.4 13.0 %fusion.16 = f32[1,4096]{1,0:T(1,128)S(1)} fusion(bf16[4096,4096]{1,0:T(8,128)(2,1)} %param.14, f32[1,4096]{1,0:T(1,128)S(1)} %bitcast.91, bf16[1,4096]{1,0:T(2,128)(2,1)S(1)} %copy-done.2, f32[]{:T(128)S(6)} %rsqrt.4), kind=kOutput, calls=%fused_computation.30 | convolution fusion | flops 33570816 | bytes 33595396 | tf_op jit(solution)/shard_map/dot_general | solution.py:270
  46.9 6.0 %fusion.32 = (f32[8,4]{1,0:T(8,128)S(1)}, f32[8,4,4352]{2,1,0:T(4,128)S(1)}) fusion(bf16[8,4352,1,128]{3,1,2,0:T(8,128)(2,1)} %param.9, bf16[8,6,128]{2,1,0:T(8,128)(2,1)S(1)} %copy_select_fusion, pred[8,4352]{1,0:T(8,128)(4,1)S(1)} %fusion.7), kind=kOutput, calls=%fused_computation.90 | convolution fusion | flops 36069344 | bytes 9513088 | tf_op jit(solution)/shard_map/bgd,bsd->bgs/dot_general | solution.py:288
  53.3 5.1 %fusion.3 = bf16[1,8,4,128]{3,2,1,0:T(4,128)(2,1)S(1)} fusion(f32[8,4,4352]{2,1,0:T(4,128)S(1)} %get-tuple-element.294, f32[8,4]{1,0:T(8,128)S(1)} %get-tuple-element.270, f32[8,4]{1,0:T(8,128)S(1)} %multiply_maximum_fusion, f32[8,128]{1,0:T(8,128)S(1)} %bitcast.93, f32[8,4]{1,0:T(8,128)S(1)} %get-tuple-element.269, bf16[8,4352,1,128]{3,1,2,0:T(8,128)(2,1)} %param.10), kind=kOutput, calls=%fused_computation.8 | convolution fusion | flops 36081664 | bytes 9482624 | tf_op jit(solution)/shard_map/bgs,bsd->bgd/dot_general | solution.py:298
  70.1 3.9 %collective-permute-done.13 = bf16[1,512]{1,0:T(2,128)(2,1)S(1)} collective-permute-done((bf16[1,512]{1,0:T(2,128)(2,1)S(1)}, bf16[1,512]{1,0:T(2,128)(2,1)S(1)}, u32[]{:S(2)}, u32[]{:S(2)}) %collective-permute-start.13) | collective-permute-done | bytes 1056 | tf_op jit(solution)/shard_map/ppermute | solution.py:232
  93.5 39.2 %collective-permute-done.56.refs_1_ = bf16[2,256,128]{2,1,0:T(8,128)(2,1)S(1)} collective-permute-done((bf16[2,256,128]{2,1,0:T(8,128)(2,1)}, bf16[2,256,128]{2,1,0:T(8,128)(2,1)S(1)}, u32[]{:S(2)}, u32[]{:S(2)}) %collective-permute-start.56) | collective-permute-done | bytes 131104 | tf_op jit(solution)/shard_map/ppermute | solution.py:232
  139.7 4.5 %shard_map.114 = (bf16[2,1280,128]{2,1,0:T(8,128)(2,1)}, bf16[2,1280,128]{2,1,0:T(8,128)(2,1)}, bf16[2,1280,128]{2,1,0:T(8,128)(2,1)}, bf16[2,1280,128]{2,1,0:T(...) custom-call(s32[1]{0:T(128)} %bitcast.me_ref, ...), custom_call_target="tpu_custom_call" | custom-call | bytes 9175040 | tf_op jit(solution)/shard_map/pallas_call | solution.py:52
  148.1 14.8 %collective-permute-done.25.refs_6_ = bf16[2,1280,128]{2,1,0:T(8,128)(2,1)S(1)} collective-permute-done((bf16[2,1280,128]{2,1,0:T(8,128)(2,1)S(1)}, bf16[2,1280,128]{2,1,0:T(8,128)(2,1)S(1)}, u32[]{:S(2)}, u32[]{:S(2)}) %collective-permute-start.25) | collective-permute-done | bytes 655392 | tf_op jit(solution)/shard_map/ppermute | solution.py:232
  166.2 11.1 %collective-permute-done.14.refs_2_ = bf16[2,1280,128]{2,1,0:T(8,128)(2,1)S(1)} collective-permute-done((bf16[2,1280,128]{2,1,0:T(8,128)(2,1)}, bf16[2,1280,128]{2,1,0:T(8,128)(2,1)S(1)}, u32[]{:S(2)}, u32[]{:S(2)}) %collective-permute-start.14) | collective-permute-done | bytes 655392 | tf_op jit(solution)/shard_map/ppermute | solution.py:232
  177.2 10.4 %collective-permute-done.15.refs_3_ = bf16[2,1280,128]{2,1,0:T(8,128)(2,1)S(1)} collective-permute-done((bf16[2,1280,128]{2,1,0:T(8,128)(2,1)}, bf16[2,1280,128]{2,1,0:T(8,128)(2,1)S(1)}, u32[]{:S(2)}, u32[]{:S(2)}) %collective-permute-start.15) | collective-permute-done | bytes 655392 | tf_op jit(solution)/shard_map/ppermute | solution.py:232
  191.5 11.8 %collective-permute-done.17.refs_5_ = bf16[2,1280,128]{2,1,0:T(8,128)(2,1)S(1)} collective-permute-done((bf16[2,1280,128]{2,1,0:T(8,128)(2,1)}, bf16[2,1280,128]{2,1,0:T(8,128)(2,1)S(1)}, u32[]{:S(2)}, u32[]{:S(2)}) %collective-permute-start.17) | collective-permute-done | bytes 655392 | tf_op jit(solution)/shard_map/ppermute | solution.py:232
  205.2 13.7 %collective-permute-done.18.refs_6_ = bf16[2,1280,128]{2,1,0:T(8,128)(2,1)S(1)} collective-permute-done((bf16[2,1280,128]{2,1,0:T(8,128)(2,1)}, bf16[2,1280,128]{2,1,0:T(8,128)(2,1)S(1)}, u32[]{:S(2)}, u32[]{:S(2)}) %collective-permute-start.18) | collective-permute-done | bytes 655392 | tf_op jit(solution)/shard_map/ppermute | solution.py:232
  219.7 4.1 %shard_map.115 = (bf16[32768,128]{1,0:T(8,128)(2,1)}, bf16[32768,128]{1,0:T(8,128)(2,1)}) custom-call(s32[1]{0:T(128)} %bitcast.me_ref, s32[1]{0:T(128)} %dynamic_slice.51.len_ref, f32[2,8,128]{2,1,0:T(8,128)} %maximum_convert_fusion.new_ref, bf16[8,4352,128]{2,1,0:T(8,128)(2,1)} %bitcast.79, bf16[8,4352,128]{2,1,0:T(8,128)(2,1)} %bitcast.66, ...), custom_call_target="tpu_custom_call" | custom-call | flops 2097152 | bytes 2097152 | tf_op jit(solution)/shard_map/pallas_call | solution.py:167
  224.0 6.6 %shard_map.116 = (bf16[32768,128]{1,0:T(8,128)(2,1)}, bf16[32768,128]{1,0:T(8,128)(2,1)}) custom-call(s32[1]{0:T(128)} %bitcast.me_ref, s32[1]{0:T(128)} %dynamic_slice.51.len_ref, f32[2,8,128]{2,1,0:T(8,128)} %maximum_convert_fusion.new_ref, bf16[8,4352,128]{2,1,0:T(8,128)(2,1)} %bitcast.80, ...), custom_call_target="tpu_custom_call", output_to_operand_aliasing={{0}: (12, {}), {1}: (13, {})} | custom-call | flops 10485760 | bytes 10485760 | tf_op jit(solution)/shard_map/pallas_call | solution.py:167
  236.8 6.6 %shard_map.119 = (bf16[32768,128]{1,0:T(8,128)(2,1)}, bf16[32768,128]{1,0:T(8,128)(2,1)}) custom-call(s32[1]{0:T(128)} %bitcast.me_ref, s32[1]{0:T(128)} %dynamic_slice.51.len_ref, f32[2,8,128]{2,1,0:T(8,128)} %maximum_convert_fusion.new_ref, bf16[8,4352,128]{2,1,0:T(8,128)(2,1)} %bitcast.83, ...), custom_call_target="tpu_custom_call", output_to_operand_aliasing={{0}: (12, {}), {1}: (13, {})} | custom-call | flops 10485760 | bytes 10485760 | tf_op jit(solution)/shard_map/pallas_call | solution.py:167
  256.7 5.5 %collective-permute-done.36.refs_1_ = bf16[2,128,128]{2,1,0:T(8,128)(2,1)S(1)} collective-permute-done((bf16[2,128,128]{2,1,0:T(8,128)(2,1)}, bf16[2,128,128]{2,1,0:T(8,128)(2,1)S(1)}, u32[]{:S(2)}, u32[]{:S(2)}) %collective-permute-start.36) | collective-permute-done | bytes 65568 | tf_op jit(solution)/shard_map/ppermute | solution.py:232
  264.3 9.8 %collective-permute-done.43.refs_3_ = bf16[2,256,128]{2,1,0:T(8,128)(2,1)S(1)} collective-permute-done((bf16[2,256,128]{2,1,0:T(8,128)(2,1)S(1)}, bf16[2,256,128]{2,1,0:T(8,128)(2,1)S(1)}, u32[]{:S(2)}, u32[]{:S(2)}) %collective-permute-start.43) | collective-permute-done | bytes 131104 | tf_op jit(solution)/shard_map/ppermute | solution.py:232
  286.6 4.5 %collective-permute-done.51.refs_4_ = bf16[2,640,128]{2,1,0:T(8,128)(2,1)S(1)} collective-permute-done((bf16[2,640,128]{2,1,0:T(8,128)(2,1)}, bf16[2,640,128]{2,1,0:T(8,128)(2,1)S(1)}, u32[]{:S(2)}, u32[]{:S(2)}) %collective-permute-start.51) | collective-permute-done | bytes 327712 | tf_op jit(solution)/shard_map/ppermute | solution.py:232
  293.2 4.7 %collective-permute-done.52.refs_5_ = bf16[2,640,128]{2,1,0:T(8,128)(2,1)S(1)} collective-permute-done((bf16[2,640,128]{2,1,0:T(8,128)(2,1)}, bf16[2,640,128]{2,1,0:T(8,128)(2,1)S(1)}, u32[]{:S(2)}, u32[]{:S(2)}) %collective-permute-start.52) | collective-permute-done | bytes 327712 | tf_op jit(solution)/shard_map/ppermute | solution.py:232
  300.7 4.2 %collective-permute-done.54.refs_7_ = bf16[2,640,128]{2,1,0:T(8,128)(2,1)S(1)} collective-permute-done((bf16[2,640,128]{2,1,0:T(8,128)(2,1)}, bf16[2,640,128]{2,1,0:T(8,128)(2,1)S(1)}, u32[]{:S(2)}, u32[]{:S(2)}) %collective-permute-start.54) | collective-permute-done | bytes 327712 | tf_op jit(solution)/shard_map/ppermute | solution.py:232
  307.0 13.6 %fusion.1 = bf16[1,4096]{1,0:T(2,128)(2,1)} fusion(bf16[4096,1]{0,1:T(2,128)(2,1)S(1)} %bitcast.94, bf16[4096,4096]{1,0:T(8,128)(2,1)} %param.17, bf16[1,4096]{1,0:T(2,128)(2,1)S(1)} %copy-done.2), kind=kOutput, calls=%fused_computation.5 | convolution fusion | flops 33566720 | bytes 33579008 | tf_op jit(solution)/shard_map/dot_general | solution.py:319
  324.4 4.8 %shard_map.123 = (bf16[32768,128]{1,0:T(8,128)(2,1)}, bf16[32768,128]{1,0:T(8,128)(2,1)}) custom-call(s32[1]{0:T(128)} %bitcast.me_ref, s32[1]{0:T(128)} %dynamic_slice.51.len_ref, f32[2,8,128]{2,1,0:T(8,128)} %maximum_convert_fusion.new_ref, bf16[8,4352,128]{2,1,0:T(8,128)(2,1)} %bitcast.85, ...), custom_call_target="tpu_custom_call", output_to_operand_aliasing={{0}: (12, {}), {1}: (13, {})} | custom-call | flops 5242880 | bytes 5242880 | tf_op jit(solution)/shard_map/pallas_call | solution.py:167
  (323 shorter events, 120.1 us)
Async XLA Ops:
  40.8 41.0 %collective-permute-start.28 = (bf16[2,256,128]{2,1,0:T(8,128)(2,1)S(1)}, bf16[2,256,128]{2,1,0:T(8,128)(2,1)S(1)}, u32[]{:S(2)}, u32[]{:S(2)}) collective-permute-start(bf16[2,256,128]{2,1,0:T(8,128)(2,1)S(1)} %copy-done.75), channel_id=1, source_target_pairs={{0,6},{1,7},{2,4},{3,5},{4,2},{5,3},{6,0},{7,1},{8,14},{9,15},{10,... | collective-permute-start | bytes 393224 | tf_op jit(solution)/shard_map/ppermute | solution.py:232
  43.4 39.6 %collective-permute-start.29 = (bf16[2,256,128]{2,1,0:T(8,128)(2,1)S(1)}, bf16[2,256,128]{2,1,0:T(8,128)(2,1)S(1)}, u32[]{:S(2)}, u32[]{:S(2)}) collective-permute-start(bf16[2,256,128]{2,1,0:T(8,128)(2,1)S(1)} %copy-done.74), channel_id=1, source_target_pairs={{0,4},{1,5},{2,6},{3,7},{4,0},{5,1},{6,2},{7,3},{8,12},{9,13},{10,... | collective-permute-start | bytes 393224 | tf_op jit(solution)/shard_map/ppermute | solution.py:232
  44.0 41.2 %collective-permute-start.30 = (bf16[2,256,128]{2,1,0:T(8,128)(2,1)S(1)}, bf16[2,256,128]{2,1,0:T(8,128)(2,1)S(1)}, u32[]{:S(2)}, u32[]{:S(2)}) collective-permute-start(bf16[2,256,128]{2,1,0:T(8,128)(2,1)S(1)} %copy-done.73), channel_id=1, source_target_pairs={{0,2},{1,3},{2,0},{3,1},{4,6},{5,7},{6,4},{7,5},{8,10},{9,11},{10,... | collective-permute-start | bytes 393224 | tf_op jit(solution)/shard_map/ppermute | solution.py:232
  44.4 41.3 %collective-permute-start.31 = (bf16[2,256,128]{2,1,0:T(8,128)(2,1)S(1)}, bf16[2,256,128]{2,1,0:T(8,128)(2,1)S(1)}, u32[]{:S(2)}, u32[]{:S(2)}) collective-permute-start(bf16[2,256,128]{2,1,0:T(8,128)(2,1)S(1)} %copy-done.72), channel_id=1, source_target_pairs={{0,7},{1,6},{2,5},{3,4},{4,3},{5,2},{6,1},{7,0},{8,15},{9,14},{10,... | collective-permute-start | bytes 393224 | tf_op jit(solution)/shard_map/ppermute | solution.py:232
  83.1 61.3 %collective-permute-start.21 = (bf16[2,1280,128]{2,1,0:T(8,128)(2,1)S(1)}, bf16[2,1280,128]{2,1,0:T(8,128)(2,1)S(1)}, u32[]{:S(2)}, u32[]{:S(2)}) collective-permute-start(bf16[2,1280,128]{2,1,0:T(8,128)(2,1)S(1)} %copy-done.66), channel_id=1, source_target_pairs={{0,6},{1,7},{2,4},{3,5},{4,2},{5,3},{6,0},{7,1},{8,14},{9,15},{10,... | collective-permute-start | bytes 1966088 | tf_op jit(solution)/shard_map/ppermute | solution.py:232
  85.2 60.7 %collective-permute-start.22 = (bf16[2,1280,128]{2,1,0:T(8,128)(2,1)S(1)}, bf16[2,1280,128]{2,1,0:T(8,128)(2,1)S(1)}, u32[]{:S(2)}, u32[]{:S(2)}) collective-permute-start(bf16[2,1280,128]{2,1,0:T(8,128)(2,1)S(1)} %copy-done.65), channel_id=1, source_target_pairs={{0,4},{1,5},{2,6},{3,7},{4,0},{5,1},{6,2},{7,3},{8,12},{9,13},{10,... | collective-permute-start | bytes 1966088 | tf_op jit(solution)/shard_map/ppermute | solution.py:232
  85.7 60.3 %collective-permute-start.23 = (bf16[2,1280,128]{2,1,0:T(8,128)(2,1)}, bf16[2,1280,128]{2,1,0:T(8,128)(2,1)S(1)}, u32[]{:S(2)}, u32[]{:S(2)}) collective-permute-start(bf16[2,1280,128]{2,1,0:T(8,128)(2,1)} %get-tuple-element.170), channel_id=1, source_target_pairs={{0,2},{1,3},{2,0},{3,1},{4,6},{5,7},{6,4},{7,5},{8,10},{9,11},{10,... | collective-permute-start | bytes 1966088 | tf_op jit(solution)/shard_map/ppermute | solution.py:232
  87.5 60.2 %collective-permute-start.24 = (bf16[2,1280,128]{2,1,0:T(8,128)(2,1)S(1)}, bf16[2,1280,128]{2,1,0:T(8,128)(2,1)S(1)}, u32[]{:S(2)}, u32[]{:S(2)}) collective-permute-start(bf16[2,1280,128]{2,1,0:T(8,128)(2,1)S(1)} %copy-done.64), channel_id=1, source_target_pairs={{0,7},{1,6},{2,5},{3,4},{4,3},{5,2},{6,1},{7,0},{8,15},{9,14},{10,... | collective-permute-start | bytes 1966088 | tf_op jit(solution)/shard_map/ppermute | solution.py:232
  91.8 40.9 %collective-permute-start.56 = (bf16[2,256,128]{2,1,0:T(8,128)(2,1)}, bf16[2,256,128]{2,1,0:T(8,128)(2,1)S(1)}, u32[]{:S(2)}, u32[]{:S(2)}) collective-permute-start(bf16[2,256,128]{2,1,0:T(8,128)(2,1)} %get-tuple-element.250), channel_id=1, source_target_pairs={{0,6},{1,7},{2,4},{3,5},{4,2},{5,3},{6,0},{7,1},{8,14},{9,15},{10,... | collective-permute-start | bytes 393224 | tf_op jit(solution)/shard_map/ppermute | solution.py:232
  146.0 31.2 %collective-permute-start.14 = (bf16[2,1280,128]{2,1,0:T(8,128)(2,1)}, bf16[2,1280,128]{2,1,0:T(8,128)(2,1)S(1)}, u32[]{:S(2)}, u32[]{:S(2)}) collective-permute-start(bf16[2,1280,128]{2,1,0:T(8,128)(2,1)} %get-tuple-element.161), channel_id=1, source_target_pairs={{0,6},{1,7},{2,4},{3,5},{4,2},{5,3},{6,0},{7,1},{8,14},{9,15},{10,... | collective-permute-start | bytes 1966088 | tf_op jit(solution)/shard_map/ppermute | solution.py:232
  147.8 39.9 %collective-permute-start.15 = (bf16[2,1280,128]{2,1,0:T(8,128)(2,1)}, bf16[2,1280,128]{2,1,0:T(8,128)(2,1)S(1)}, u32[]{:S(2)}, u32[]{:S(2)}) collective-permute-start(bf16[2,1280,128]{2,1,0:T(8,128)(2,1)} %get-tuple-element.162), channel_id=1, source_target_pairs={{0,4},{1,5},{2,6},{3,7},{4,0},{5,1},{6,2},{7,3},{8,12},{9,13},{10,... | collective-permute-start | bytes 1966088 | tf_op jit(solution)/shard_map/ppermute | solution.py:232
  163.0 40.4 %collective-permute-start.17 = (bf16[2,1280,128]{2,1,0:T(8,128)(2,1)}, bf16[2,1280,128]{2,1,0:T(8,128)(2,1)S(1)}, u32[]{:S(2)}, u32[]{:S(2)}) collective-permute-start(bf16[2,1280,128]{2,1,0:T(8,128)(2,1)} %get-tuple-element.164), channel_id=1, source_target_pairs={{0,7},{1,6},{2,5},{3,4},{4,3},{5,2},{6,1},{7,0},{8,15},{9,14},{10,... | collective-permute-start | bytes 1966088 | tf_op jit(solution)/shard_map/ppermute | solution.py:232
  163.5 55.4 %collective-permute-start.18 = (bf16[2,1280,128]{2,1,0:T(8,128)(2,1)}, bf16[2,1280,128]{2,1,0:T(8,128)(2,1)S(1)}, u32[]{:S(2)}, u32[]{:S(2)}) collective-permute-start(bf16[2,1280,128]{2,1,0:T(8,128)(2,1)} %get-tuple-element.165), channel_id=1, source_target_pairs={{0,5},{1,4},{2,7},{3,6},{4,1},{5,0},{6,3},{7,2},{8,13},{9,12},{10,... | collective-permute-start | bytes 1966088 | tf_op jit(solution)/shard_map/ppermute | solution.py:232
  177.2 41.7 %collective-permute-start.19 = (bf16[2,1280,128]{2,1,0:T(8,128)(2,1)}, bf16[2,1280,128]{2,1,0:T(8,128)(2,1)}, u32[]{:S(2)}, u32[]{:S(2)}) collective-permute-start(bf16[2,1280,128]{2,1,0:T(8,128)(2,1)} %get-tuple-element.166), channel_id=1, source_target_pairs={{0,3},{1,2},{2,1},{3,0},{4,7},{5,6},{6,5},{7,4},{8,11},{9,10},{10,... | collective-permute-start | bytes 1966088 | tf_op jit(solution)/shard_map/ppermute | solution.py:232
  187.6 48.5 %collective-permute-start.20 = (bf16[2,1280,128]{2,1,0:T(8,128)(2,1)}, bf16[2,1280,128]{2,1,0:T(8,128)(2,1)}, u32[]{:S(2)}, u32[]{:S(2)}) collective-permute-start(bf16[2,1280,128]{2,1,0:T(8,128)(2,1)} %get-tuple-element.167), channel_id=1, source_target_pairs={{0,1},{1,0},{2,3},{3,2},{4,5},{5,4},{6,7},{7,6},{8,9},{9,8},{10,11... | collective-permute-start | bytes 1966088 | tf_op jit(solution)/shard_map/ppermute | solution.py:232
  191.1 54.5 %collective-permute-start.59 = (bf16[2,256,128]{2,1,0:T(8,128)(2,1)S(1)}, bf16[2,256,128]{2,1,0:T(8,128)(2,1)S(1)}, u32[]{:S(2)}, u32[]{:S(2)}) collective-permute-start(bf16[2,256,128]{2,1,0:T(8,128)(2,1)S(1)} %copy-done.76), channel_id=1, source_target_pairs={{0,7},{1,6},{2,5},{3,4},{4,3},{5,2},{6,1},{7,0},{8,15},{9,14},{10,... | collective-permute-start | bytes 393224 | tf_op jit(solution)/shard_map/ppermute | solution.py:232
  203.3 44.7 %collective-permute-start.60 = (bf16[2,256,128]{2,1,0:T(8,128)(2,1)}, bf16[2,256,128]{2,1,0:T(8,128)(2,1)S(1)}, u32[]{:S(2)}, u32[]{:S(2)}) collective-permute-start(bf16[2,256,128]{2,1,0:T(8,128)(2,1)} %get-tuple-element.254), channel_id=1, source_target_pairs={{0,5},{1,4},{2,7},{3,6},{4,1},{5,0},{6,3},{7,2},{8,13},{9,12},{10,... | collective-permute-start | bytes 393224 | tf_op jit(solution)/shard_map/ppermute | solution.py:232
  218.9 32.9 %collective-permute-start.61 = (bf16[2,256,128]{2,1,0:T(8,128)(2,1)}, bf16[2,256,128]{2,1,0:T(8,128)(2,1)}, u32[]{:S(2)}, u32[]{:S(2)}) collective-permute-start(bf16[2,256,128]{2,1,0:T(8,128)(2,1)} %get-tuple-element.255), channel_id=1, source_target_pairs={{0,3},{1,2},{2,1},{3,0},{4,7},{5,6},{6,5},{7,4},{8,11},{9,10},{10,... | collective-permute-start | bytes 393224 | tf_op jit(solution)/shard_map/ppermute | solution.py:232
  218.9 34.5 %collective-permute-start.62 = (bf16[2,256,128]{2,1,0:T(8,128)(2,1)}, bf16[2,256,128]{2,1,0:T(8,128)(2,1)}, u32[]{:S(2)}, u32[]{:S(2)}) collective-permute-start(bf16[2,256,128]{2,1,0:T(8,128)(2,1)} %get-tuple-element.256), channel_id=1, source_target_pairs={{0,1},{1,0},{2,3},{3,2},{4,5},{5,4},{6,7},{7,6},{8,9},{9,8},{10,11... | collective-permute-start | bytes 393224 | tf_op jit(solution)/shard_map/ppermute | solution.py:232
  251.8 31.8 %collective-permute-start.49 = (bf16[2,640,128]{2,1,0:T(8,128)(2,1)S(1)}, bf16[2,640,128]{2,1,0:T(8,128)(2,1)S(1)}, u32[]{:S(2)}, u32[]{:S(2)}) collective-permute-start(bf16[2,640,128]{2,1,0:T(8,128)(2,1)S(1)} %copy-done.68), channel_id=1, source_target_pairs={{0,6},{1,7},{2,4},{3,5},{4,2},{5,3},{6,0},{7,1},{8,14},{9,15},{10,... | collective-permute-start | bytes 983048 | tf_op jit(solution)/shard_map/ppermute | solution.py:232
  253.5 31.7 %collective-permute-start.50 = (bf16[2,640,128]{2,1,0:T(8,128)(2,1)S(1)}, bf16[2,640,128]{2,1,0:T(8,128)(2,1)S(1)}, u32[]{:S(2)}, u32[]{:S(2)}) collective-permute-start(bf16[2,640,128]{2,1,0:T(8,128)(2,1)S(1)} %copy-done.67), channel_id=1, source_target_pairs={{0,4},{1,5},{2,6},{3,7},{4,0},{5,1},{6,2},{7,3},{8,12},{9,13},{10,... | collective-permute-start | bytes 983048 | tf_op jit(solution)/shard_map/ppermute | solution.py:232
  291.1 41.7 %collective-permute-start.37 = (bf16[2,128,128]{2,1,0:T(8,128)(2,1)}, bf16[2,128,128]{2,1,0:T(8,128)(2,1)S(1)}, u32[]{:S(2)}, u32[]{:S(2)}) collective-permute-start(bf16[2,128,128]{2,1,0:T(8,128)(2,1)} %get-tuple-element.229), channel_id=1, source_target_pairs={{0,2},{1,3},{2,0},{3,1},{4,6},{5,7},{6,4},{7,5},{8,10},{9,11},{10,... | collective-permute-start | bytes 196616 | tf_op jit(solution)/shard_map/ppermute | solution.py:232
  297.9 35.0 %collective-permute-start.38 = (bf16[2,128,128]{2,1,0:T(8,128)(2,1)}, bf16[2,128,128]{2,1,0:T(8,128)(2,1)S(1)}, u32[]{:S(2)}, u32[]{:S(2)}) collective-permute-start(bf16[2,128,128]{2,1,0:T(8,128)(2,1)} %get-tuple-element.230), channel_id=1, source_target_pairs={{0,7},{1,6},{2,5},{3,4},{4,3},{5,2},{6,1},{7,0},{8,15},{9,14},{10,... | collective-permute-start | bytes 196616 | tf_op jit(solution)/shard_map/ppermute | solution.py:232
  300.6 32.3 %collective-permute-start.39 = (bf16[2,128,128]{2,1,0:T(8,128)(2,1)}, bf16[2,128,128]{2,1,0:T(8,128)(2,1)S(1)}, u32[]{:S(2)}, u32[]{:S(2)}) collective-permute-start(bf16[2,128,128]{2,1,0:T(8,128)(2,1)} %get-tuple-element.231), channel_id=1, source_target_pairs={{0,5},{1,4},{2,7},{3,6},{4,1},{5,0},{6,3},{7,2},{8,13},{9,12},{10,... | collective-permute-start | bytes 196616 | tf_op jit(solution)/shard_map/ppermute | solution.py:232
  (122 other events, 2865.7 us)

commit v5 on v4

--- a/solution.py
+++ b/solution.py
@@ -33,10 +33,10 @@
     return jnp.concatenate([first_half * cos_part - second_half * sin_part, second_half * cos_part + first_half * sin_part], axis=-1).astype(jnp.bfloat16)
 
 
-def pack_kernel(first, count, has_own, me_ref, k_ref, v_ref, *refs):
+def pack_kernel(first, count, has_own, k_ref, v_ref, *refs):
     offsets = ORDER + (0,) * has_own
     outs, sems = refs[:-1], refs[-1]
-    me = me_ref[0]
+    me = lax.axis_index('sh')
     copies = []
     for at, offset in enumerate(offsets):
         for kv, src in enumerate((k_ref, v_ref)):
@@ -46,22 +46,22 @@
         copy.wait()
 
 
-def pack(first, count, has_own, me, k_mine, v_mine):
+def pack(first, count, has_own, k_mine, v_mine):
     dim = k_mine.shape[2]
     pieces = len(ORDER) + has_own
     return pl.pallas_call(
         functools.partial(pack_kernel, first, count, has_own),
         out_shape=[jax.ShapeDtypeStruct((2, count, dim), jnp.bfloat16)] * pieces,
-        in_specs=[pl.BlockSpec(memory_space=pltpu.SMEM)] + [pl.BlockSpec(memory_space=pltpu.HBM)] * 2,
+        in_specs=[pl.BlockSpec(memory_space=pltpu.HBM)] * 2,
         out_specs=[pl.BlockSpec(memory_space=pltpu.VMEM)] * pieces,
         scratch_shapes=[pltpu.SemaphoreType.DMA((pieces, 2))],
         compiler_params=pltpu.CompilerParams(vmem_limit_bytes=VMEM_LIMIT),
         cost_estimate=pl.CostEstimate(flops=0, bytes_accessed=pieces * 4 * count * dim * 2, transcendentals=0),
-    )(me, k_mine, v_mine)
-
-
-def wrap_kernel(me_ref, len_ref, k_ref, k_late_ref, v_ref, v_late_ref, *outs):
-    me = me_ref[0]
+    )(k_mine, v_mine)
+
+
+def wrap_kernel(len_ref, k_ref, k_late_ref, v_ref, v_late_ref, *outs):
+    me = lax.axis_index('sh')
     slots = lax.broadcasted_iota(jnp.int32, (WRAP, 128), 0)
     for out, offset in zip(outs, ORDER + (0,)):
         row = me ^ offset
@@ -70,7 +70,7 @@
             out[kv] = jnp.where(late, late_ref[row].astype(jnp.float32), base_ref[row].astype(jnp.float32)).astype(jnp.bfloat16)
 
 
-def wrap_pack(me, lengths, k_mine, v_mine):
+def wrap_pack(lengths, k_mine, v_mine):
     rows, _, dim = k_mine.shape
     base = pl.BlockSpec((rows, WRAP, dim), lambda i: (0, 0, 0))
     late = pl.BlockSpec((rows, WRAP, dim), lambda i: (0, WINDOW // WRAP, 0))
@@ -80,19 +80,19 @@
         grid=(1,),
         out_shape=[piece] * (len(ORDER) + 1),
         out_specs=[pl.BlockSpec((2, WRAP, dim), lambda i: (0, 0, 0))] * (len(ORDER) + 1),
-        in_specs=[pl.BlockSpec(memory_space=pltpu.SMEM)] * 2 + [base, late, base, late],
+        in_specs=[pl.BlockSpec(memory_space=pltpu.SMEM), base, late, base, late],
         compiler_params=pltpu.CompilerParams(vmem_limit_bytes=VMEM_LIMIT),
         cost_estimate=pl.CostEstimate(flops=rows * 8 * WRAP * dim, bytes_accessed=rows * 6 * WRAP * dim * 2, transcendentals=0),
-    )(me, lengths, k_mine, k_mine, v_mine, v_mine)
-
-
-def interleave_kernel(first, count, block, has_own, num_alias, me_ref, len_ref, new_ref, *refs):
+    )(lengths, k_mine, k_mine, v_mine, v_mine)
+
+
+def interleave_kernel(first, count, block, has_own, num_alias, len_ref, new_ref, *refs):
     num_own = 2 if has_own else 1
     own = refs[:num_own]
     pieces = refs[num_own:num_own + len(ORDER)]
     k_out, v_out, held, mixed, in_sems, out_sems = refs[num_own + len(ORDER) + num_alias:]
     tiles = count // block
-    me = me_ref[0]
+    me = lax.axis_index('sh')
     row_len = len_ref[0]
     new_slot = lax.rem(row_len, WINDOW)
     outs = (k_out, v_out)
@@ -151,14 +151,14 @@
             write(tile, kv).wait()
 
 
-def interleave(first, me, row_len, new, own, pieces, caches):
+def interleave(first, row_len, new, own, pieces, caches):
     count, dim = pieces[0].shape[1:]
     block = BLOCK if count % BLOCK == 0 else BLOCK // 2
     tiles = count // block
     cache = jax.ShapeDtypeStruct((WINDOW * PEERS, dim), jnp.bfloat16)
     any_spec = pl.BlockSpec(memory_space=pltpu.HBM)
-    args = [me, row_len, new, *own, *pieces]
-    in_specs = [pl.BlockSpec(memory_space=pltpu.SMEM)] * 2 + [pl.BlockSpec(memory_space=pltpu.VMEM)] + [any_spec] * (len(own) + len(pieces))
+    args = [row_len, new, *own, *pieces]
+    in_specs = [pl.BlockSpec(memory_space=pltpu.SMEM)] + [pl.BlockSpec(memory_space=pltpu.VMEM)] + [any_spec] * (len(own) + len(pieces))
     aliases = {}
     if caches is not None:
         aliases = {len(args): 0, len(args) + 1: 1}
@@ -181,12 +181,12 @@
     )(*args)
 
 
-def last_kernel(first, count, me_ref, len_ref, new_ref, *refs):
+def last_kernel(first, count, new_ref, *refs):
     pieces = refs[:PEERS]
     k_out, v_out, mixed, sems = refs[PEERS + 2:]
-    me = me_ref[0]
-    row_len = len_ref[0]
-    new_slot = lax.rem(row_len, WINDOW)
+    me = lax.axis_index('sh')
+    row_len = jnp.concatenate([new_ref[2].astype(jnp.int32)] * GROUP, axis=0)
+    new_slot = row_len & (WINDOW - 1)
     by_offset = pieces[-1:] + tuple(pieces[ORDER.index(offset)] for offset in range(1, PEERS))
     copies = []
     for kv, out in enumerate((k_out, v_out)):
@@ -208,19 +208,19 @@
         copy.wait()
 
 
-def interleave_last(first, me, row_len, new, pieces, caches):
+def interleave_last(first, new, pieces, caches):
     count, dim = pieces[0].shape[1:]
     cache = jax.ShapeDtypeStruct((WINDOW * PEERS, dim), jnp.bfloat16)
     return pl.pallas_call(
         functools.partial(last_kernel, first, count),
         out_shape=[cache, cache],
-        in_specs=[pl.BlockSpec(memory_space=pltpu.SMEM)] * 2 + [pl.BlockSpec(memory_space=pltpu.VMEM)] * (1 + PEERS) + [pl.BlockSpec(memory_space=pltpu.HBM)] * 2,
+        in_specs=[pl.BlockSpec(memory_space=pltpu.VMEM)] * (1 + PEERS) + [pl.BlockSpec(memory_space=pltpu.HBM)] * 2,
         out_specs=[pl.BlockSpec(memory_space=pltpu.HBM)] * 2,
-        input_output_aliases={3 + PEERS: 0, 4 + PEERS: 1},
+        input_output_aliases={1 + PEERS: 0, 2 + PEERS: 1},
         scratch_shapes=[pltpu.VMEM((2, count * PEERS, dim), jnp.bfloat16), pltpu.SemaphoreType.DMA((2,))],
         compiler_params=pltpu.CompilerParams(vmem_limit_bytes=LAST_VMEM_LIMIT),
         cost_estimate=pl.CostEstimate(flops=count * 64 * dim, bytes_accessed=count * PEERS * dim * 8, transcendentals=0),
-    )(me, row_len, new, *pieces, *caches)
+    )(new, *pieces, *caches)
 
 
 def solution(mesh):
@@ -240,7 +240,6 @@
 
     def per_device(k_prefill, v_prefill, lengths, residual, norm_gain, w_query, w_key, w_value, w_out):
         me = lax.axis_index('sh')
-        me_vec = me.reshape(1).astype(jnp.int32)
         seq_len = k_prefill.shape[1]
         head_dim = k_prefill.shape[3]
         k_mine = k_prefill.reshape(PEERS, seq_len, head_dim)
@@ -252,10 +251,10 @@
             received[first] = [swap(piece, offset) for piece, offset in zip(pieces, ORDER)]
 
         def start(chunk, after=None, before=None):
-            place = me_vec
+            prefills = (k_mine, v_mine)
             if after is not None:
-                place, after = lax.optimization_barrier((place, after))
-            pieces = pack(*chunk, chunk == CHUNKS[-1], place, k_mine, v_mine)
+                prefills, after = lax.optimization_barrier((prefills, after))
+            pieces = pack(*chunk, chunk == CHUNKS[-1], *prefills)
             pieces, before = lax.optimization_barrier((pieces, before))
             send(chunk[0], pieces)
             received[chunk[0]] += pieces[len(ORDER):]
@@ -273,13 +272,13 @@
         q_heads = rotate(q_heads, my_len)
         k_new = rotate(k_new, my_len)
         q_group = q_heads.shape[1] // PEERS
-        new = jnp.concatenate([k_new, v_new], axis=0).astype(jnp.float32)
+        new = jnp.concatenate([k_new.astype(jnp.float32), v_new.astype(jnp.float32), jnp.broadcast_to(my_len.astype(jnp.float32), (1, PEERS, head_dim))], axis=0)
 
         table = jnp.concatenate([q_heads.reshape(PEERS, q_group, head_dim), k_new.reshape(PEERS, 1, head_dim), v_new.reshape(PEERS, 1, head_dim)], axis=1).reshape(PEERS, -1)
         qkv_parts = exchange(table, me)
         _, table = start(CHUNKS[2], after=table, before=table)
-        wrap_place, _ = lax.optimization_barrier((me_vec, table))
-        wrapped = wrap_pack(wrap_place, lengths, k_mine, v_mine)
+        wrap_lengths, _ = lax.optimization_barrier((lengths, table))
+        wrapped = wrap_pack(wrap_lengths, k_mine, v_mine)
         send(0, wrapped[:-1])
         qkv = by_device(qkv_parts, me).reshape(PEERS, q_group + 2, head_dim)
         q_all, k_all, v_all = qkv[:, :q_group], qkv[:, q_group:q_group + 1], qkv[:, q_group + 1:]
@@ -299,14 +298,14 @@
         mixed = (mixed + new_weight * v_all.astype(jnp.float32)).astype(jnp.bfloat16).reshape(PEERS, -1)
         attn_parts = exchange(mixed, me)
 
-        place, _ = lax.optimization_barrier((me_vec, mixed))
+        place_len, _ = lax.optimization_barrier((my_len, mixed))
         caches = None
 
         def store(first, caches):
             own = [wrapped[-1]] if first == 0 else [k_mine, v_mine]
             if first == CHUNKS[-1][0]:
-                return interleave_last(first, place, my_len, new, received[first], caches)
-            return interleave(first, place, my_len, new, own, received[first], caches)
+                return interleave_last(first, new, received[first], caches)
+            return interleave(first, place_len, new, own, received[first], caches)
 
         caches = store(CHUNKS[0][0], caches)
         caches = store(CHUNKS[1][0], caches)

time: 338 us -> 342 us (1.012)
  waiting for transfers between devices: 157 us -> 168 us
  starting transfers between devices: 69.3 us -> 61.9 us
    ppermute x63, waiting for transfers between devices: 157 us -> 168 us  [swap(): return lax.ppermute(value, 'sh', [(i, i ^ offset) for i in range(PEERS)])]
    ppermute x63, starting transfers between devices: 69.3 us -> 61.9 us  [swap(): return lax.ppermute(value, 'sh', [(i, i ^ offset) for i in range(PEERS)])]
  transfers between devices with their start and end apart: 63 -> 63, of which waited for: 21 -> 25; matrix products, arithmetic and copies ran while one was open for 8% -> 8% of each run, Pallas kernels for 13% -> 13%
where the time goes in v5:
time: 342 us; the launch traced here: 339 us
  waiting for transfers between devices  168 us (49%)
  starting transfers between devices  61.9 us (18%)
  Pallas kernels  53.1 us (16%)
  matrix products  46.9 us (14%)
    ppermute x63, waiting for transfers between devices, swap(): return lax.ppermute(value, 'sh', [(i, i ^ offset) for i in range(PEERS)])  168 us
    ppermute x63, starting transfers between devices, swap(): return lax.ppermute(value, 'sh', [(i, i ^ offset) for i in range(PEERS)])  61.9 us
    pallas_call x6, Pallas kernels, interleave(): pl.pallas_call(functools.partial(interleave_kernel, first, count, block,...  30 us
    pallas_call x6, Pallas kernels, pack(): pl.pallas_call(functools.partial(pack_kernel, first, count, has_own), out...  19.1 us
    dot_general x1, matrix products, per_device(): jnp.dot(attn_out, w_out, preferred_element_type=jnp.float32)  13.6 us
    dot_general x1, matrix products, per_device(): jnp.dot(normed, w_query, preferred_element_type=jnp.float32)  13 us
  transfers between devices with their start and end apart: 63, of which 25 were waited for; matrix products, arithmetic and copies ran while one was open for 8% of the time, Pallas kernels for 13%

profile of v5, /device:TPU:0, one launch (start us, length us, event | category | flops | bytes accessed | tf_op | source)
XLA Modules:
  0.0 338.6 jit_solution(13355768187873484887)
XLA Ops:
  3.0 4.5 %shard_map.113 = (bf16[2,1280,128]{2,1,0:T(8,128)(2,1)}, bf16[2,1280,128]{2,1,0:T(8,128)(2,1)}, bf16[2,1280,128]{2,1,0:T(8,128)(2,1)}, bf16[2,1280,128]{2,1,0:T(...) custom-call(bf16[8,4352,128]{2,1,0:T(8,128)(2,1)} %bitcast.75, ...), custom_call_target="tpu_custom_call" | custom-call | bytes 9175040 | tf_op jit(solution)/shard_map/pallas_call | solution.py:52
  8.9 4.6 %fusion.14 = f32[1,1024]{1,0:T(1,128)S(1)} fusion(bf16[4096,1024]{1,0:T(8,128)(2,1)} %param.15, f32[1,4096]{1,0:T(1,128)S(1)} %bitcast.89, bf16[1,4096]{1,0:T(2,128)(2,1)S(1)} %copy-done.2, f32[]{:T(128)S(6)} %rsqrt.4), kind=kOutput, calls=%fused_computation.28 | convolution fusion | flops 8404992 | bytes 8417284 | tf_op jit(solution)/shard_map/dot_general | solution.py:270
  14.9 4.6 %fusion.12 = f32[1,1024]{1,0:T(1,128)S(1)} fusion(bf16[4096,1024]{1,0:T(8,128)(2,1)} %param.16, f32[1,4096]{1,0:T(1,128)S(1)} %bitcast.90, bf16[1,4096]{1,0:T(2,128)(2,1)S(1)} %copy-done.2, f32[]{:T(128)S(6)} %rsqrt.4), kind=kOutput, calls=%fused_computation.26 | convolution fusion | flops 8404992 | bytes 8417284 | tf_op jit(solution)/shard_map/dot_general | solution.py:271
  19.5 13.0 %fusion.16 = f32[1,4096]{1,0:T(1,128)S(1)} fusion(bf16[4096,4096]{1,0:T(8,128)(2,1)} %param.14, f32[1,4096]{1,0:T(1,128)S(1)} %bitcast.91, bf16[1,4096]{1,0:T(2,128)(2,1)S(1)} %copy-done.2, f32[]{:T(128)S(6)} %rsqrt.4), kind=kOutput, calls=%fused_computation.30 | convolution fusion | flops 33570816 | bytes 33595396 | tf_op jit(solution)/shard_map/dot_general | solution.py:269
  47.0 6.0 %fusion.32 = (f32[8,4]{1,0:T(8,128)S(1)}, f32[8,4,4352]{2,1,0:T(4,128)S(1)}) fusion(bf16[8,4352,1,128]{3,1,2,0:T(8,128)(2,1)} %param.9, bf16[8,6,128]{2,1,0:T(8,128)(2,1)S(1)} %copy_select_fusion, pred[8,4352]{1,0:T(8,128)(4,1)S(1)} %fusion.7), kind=kOutput, calls=%fused_computation.91 | convolution fusion | flops 36069344 | bytes 9513088 | tf_op jit(solution)/shard_map/bgd,bsd->bgs/dot_general | solution.py:287
  53.5 5.1 %fusion.3 = bf16[1,8,4,128]{3,2,1,0:T(4,128)(2,1)S(1)} fusion(f32[8,4,4352]{2,1,0:T(4,128)S(1)} %get-tuple-element.304, f32[8,4]{1,0:T(8,128)S(1)} %get-tuple-element.280, f32[8,4]{1,0:T(8,128)S(1)} %multiply_maximum_fusion, f32[8,128]{1,0:T(8,128)S(1)} %bitcast.93, f32[8,4]{1,0:T(8,128)S(1)} %get-tuple-element.279, bf16[8,4352,1,128]{3,1,2,0:T(8,128)(2,1)} %param.10), kind=kOutput, calls=%fused_computation.8 | convolution fusion | flops 36081664 | bytes 9482624 | tf_op jit(solution)/shard_map/bgs,bsd->bgd/dot_general | solution.py:297
  86.0 15.7 %collective-permute-done.32.refs_6_ = bf16[2,256,128]{2,1,0:T(8,128)(2,1)S(1)} collective-permute-done((bf16[2,256,128]{2,1,0:T(8,128)(2,1)S(1)}, bf16[2,256,128]{2,1,0:T(8,128)(2,1)S(1)}, u32[]{:S(2)}, u32[]{:S(2)}) %collective-permute-start.32) | collective-permute-done | bytes 131104 | tf_op jit(solution)/shard_map/ppermute | solution.py:232
  101.7 15.0 %collective-permute-done.33.refs_7_ = bf16[2,256,128]{2,1,0:T(8,128)(2,1)} collective-permute-done((bf16[2,256,128]{2,1,0:T(8,128)(2,1)S(1)}, bf16[2,256,128]{2,1,0:T(8,128)(2,1)}, u32[]{:S(2)}, u32[]{:S(2)}) %collective-permute-start.33) | collective-permute-done | bytes 131104 | tf_op jit(solution)/shard_map/ppermute | solution.py:232
  121.7 15.3 %collective-permute-done.56.refs_1_ = bf16[2,256,128]{2,1,0:T(8,128)(2,1)S(1)} collective-permute-done((bf16[2,256,128]{2,1,0:T(8,128)(2,1)}, bf16[2,256,128]{2,1,0:T(8,128)(2,1)S(1)}, u32[]{:S(2)}, u32[]{:S(2)}) %collective-permute-start.56) | collective-permute-done | bytes 131104 | tf_op jit(solution)/shard_map/ppermute | solution.py:232
  138.1 4.6 %collective-permute-done.57.refs_2_ = bf16[2,256,128]{2,1,0:T(8,128)(2,1)S(1)} collective-permute-done((bf16[2,256,128]{2,1,0:T(8,128)(2,1)}, bf16[2,256,128]{2,1,0:T(8,128)(2,1)S(1)}, u32[]{:S(2)}, u32[]{:S(2)}) %collective-permute-start.57) | collective-permute-done | bytes 131104 | tf_op jit(solution)/shard_map/ppermute | solution.py:232
  143.2 4.7 %shard_map.114 = (bf16[2,1280,128]{2,1,0:T(8,128)(2,1)}, bf16[2,1280,128]{2,1,0:T(8,128)(2,1)}, bf16[2,1280,128]{2,1,0:T(8,128)(2,1)}, bf16[2,1280,128]{2,1,0:T(...) custom-call(bf16[8,4352,128]{2,1,0:T(8,128)(2,1)} %bitcast.78, ...), custom_call_target="tpu_custom_call" | custom-call | bytes 9175040 | tf_op jit(solution)/shard_map/pallas_call | solution.py:52
  153.0 11.9 %collective-permute-done.25.refs_6_ = bf16[2,1280,128]{2,1,0:T(8,128)(2,1)S(1)} collective-permute-done((bf16[2,1280,128]{2,1,0:T(8,128)(2,1)S(1)}, bf16[2,1280,128]{2,1,0:T(8,128)(2,1)S(1)}, u32[]{:S(2)}, u32[]{:S(2)}) %collective-permute-start.25) | collective-permute-done | bytes 655392 | tf_op jit(solution)/shard_map/ppermute | solution.py:232
  169.0 11.9 %collective-permute-done.14.refs_2_ = bf16[2,1280,128]{2,1,0:T(8,128)(2,1)S(1)} collective-permute-done((bf16[2,1280,128]{2,1,0:T(8,128)(2,1)}, bf16[2,1280,128]{2,1,0:T(8,128)(2,1)S(1)}, u32[]{:S(2)}, u32[]{:S(2)}) %collective-permute-start.14) | collective-permute-done | bytes 655392 | tf_op jit(solution)/shard_map/ppermute | solution.py:232
  181.0 12.3 %collective-permute-done.15.refs_3_ = bf16[2,1280,128]{2,1,0:T(8,128)(2,1)S(1)} collective-permute-done((bf16[2,1280,128]{2,1,0:T(8,128)(2,1)}, bf16[2,1280,128]{2,1,0:T(8,128)(2,1)S(1)}, u32[]{:S(2)}, u32[]{:S(2)}) %collective-permute-start.15) | collective-permute-done | bytes 655392 | tf_op jit(solution)/shard_map/ppermute | solution.py:232
  195.1 12.6 %collective-permute-done.17.refs_5_ = bf16[2,1280,128]{2,1,0:T(8,128)(2,1)S(1)} collective-permute-done((bf16[2,1280,128]{2,1,0:T(8,128)(2,1)}, bf16[2,1280,128]{2,1,0:T(8,128)(2,1)S(1)}, u32[]{:S(2)}, u32[]{:S(2)}) %collective-permute-start.17) | collective-permute-done | bytes 655392 | tf_op jit(solution)/shard_map/ppermute | solution.py:232
  210.1 11.0 %collective-permute-done.18.refs_6_ = bf16[2,1280,128]{2,1,0:T(8,128)(2,1)S(1)} collective-permute-done((bf16[2,1280,128]{2,1,0:T(8,128)(2,1)}, bf16[2,1280,128]{2,1,0:T(8,128)(2,1)S(1)}, u32[]{:S(2)}, u32[]{:S(2)}) %collective-permute-start.18) | collective-permute-done | bytes 655392 | tf_op jit(solution)/shard_map/ppermute | solution.py:232
  229.0 6.7 %shard_map.116 = (bf16[32768,128]{1,0:T(8,128)(2,1)}, bf16[32768,128]{1,0:T(8,128)(2,1)}) custom-call(s32[1]{0:T(128)} %dynamic_slice.51.len_ref, f32[3,8,128]{2,1,0:T(8,128)} %maximum_maximum_fusion.new_ref, bf16[8,4352,128]{2,1,0:T(8,128)(2,1)} %bitcast.80, bf16[8,4352,128]{2,1,0:T(8,128)(2,1)} %bitcast.67, ...), custom_call_target="tpu_custom_call", output_to_operand_aliasing={{0}: (11, {}), {1}: (12, {})} | custom-call | flops 10485760 | bytes 10485760 | tf_op jit(solution)/shard_map/pallas_call | solution.py:167
  242.7 6.7 %shard_map.119 = (bf16[32768,128]{1,0:T(8,128)(2,1)}, bf16[32768,128]{1,0:T(8,128)(2,1)}) custom-call(s32[1]{0:T(128)} %dynamic_slice.51.len_ref, f32[3,8,128]{2,1,0:T(8,128)} %maximum_maximum_fusion.new_ref, bf16[8,4352,128]{2,1,0:T(8,128)(2,1)} %bitcast.83, bf16[8,4352,128]{2,1,0:T(8,128)(2,1)} %bitcast.70, ...), custom_call_target="tpu_custom_call", output_to_operand_aliasing={{0}: (11, {}), {1}: (12, {})} | custom-call | flops 10485760 | bytes 10485760 | tf_op jit(solution)/shard_map/pallas_call | solution.py:167
  259.7 6.5 %collective-permute-done.36.refs_1_ = bf16[2,128,128]{2,1,0:T(8,128)(2,1)S(1)} collective-permute-done((bf16[2,128,128]{2,1,0:T(8,128)(2,1)}, bf16[2,128,128]{2,1,0:T(8,128)(2,1)S(1)}, u32[]{:S(2)}, u32[]{:S(2)}) %collective-permute-start.36) | collective-permute-done | bytes 65568 | tf_op jit(solution)/shard_map/ppermute | solution.py:232
  268.2 10.6 %collective-permute-done.43.refs_3_ = bf16[2,256,128]{2,1,0:T(8,128)(2,1)S(1)} collective-permute-done((bf16[2,256,128]{2,1,0:T(8,128)(2,1)S(1)}, bf16[2,256,128]{2,1,0:T(8,128)(2,1)S(1)}, u32[]{:S(2)}, u32[]{:S(2)}) %collective-permute-start.43) | collective-permute-done | bytes 131104 | tf_op jit(solution)/shard_map/ppermute | solution.py:232
  290.5 4.7 %collective-permute-done.51.refs_4_ = bf16[2,640,128]{2,1,0:T(8,128)(2,1)S(1)} collective-permute-done((bf16[2,640,128]{2,1,0:T(8,128)(2,1)}, bf16[2,640,128]{2,1,0:T(8,128)(2,1)S(1)}, u32[]{:S(2)}, u32[]{:S(2)}) %collective-permute-start.51) | collective-permute-done | bytes 327712 | tf_op jit(solution)/shard_map/ppermute | solution.py:232
  297.0 4.7 %collective-permute-done.52.refs_5_ = bf16[2,640,128]{2,1,0:T(8,128)(2,1)S(1)} collective-permute-done((bf16[2,640,128]{2,1,0:T(8,128)(2,1)}, bf16[2,640,128]{2,1,0:T(8,128)(2,1)S(1)}, u32[]{:S(2)}, u32[]{:S(2)}) %collective-permute-start.52) | collective-permute-done | bytes 327712 | tf_op jit(solution)/shard_map/ppermute | solution.py:232
  310.9 13.6 %fusion.1 = bf16[1,4096]{1,0:T(2,128)(2,1)} fusion(bf16[4096,1]{0,1:T(2,128)(2,1)S(1)} %bitcast.94, bf16[4096,4096]{1,0:T(8,128)(2,1)} %param.17, bf16[1,4096]{1,0:T(2,128)(2,1)S(1)} %copy-done.2), kind=kOutput, calls=%fused_computation.5 | convolution fusion | flops 33566720 | bytes 33579008 | tf_op jit(solution)/shard_map/dot_general | solution.py:318
  328.3 4.8 %shard_map.123 = (bf16[32768,128]{1,0:T(8,128)(2,1)}, bf16[32768,128]{1,0:T(8,128)(2,1)}) custom-call(s32[1]{0:T(128)} %dynamic_slice.51.len_ref, f32[3,8,128]{2,1,0:T(8,128)} %maximum_maximum_fusion.new_ref, bf16[8,4352,128]{2,1,0:T(8,128)(2,1)} %bitcast.85, bf16[8,4352,128]{2,1,0:T(8,128)(2,1)} %bitcast.72, ...), custom_call_target="tpu_custom_call", output_to_operand_aliasing={{0}: (11, {}), {1}: (12, {})} | custom-call | flops 5242880 | bytes 5242880 | tf_op jit(solution)/shard_map/pallas_call | solution.py:167
  (323 shorter events, 124.0 us)
Async XLA Ops:
  41.0 41.0 %collective-permute-start.28 = (bf16[2,256,128]{2,1,0:T(8,128)(2,1)S(1)}, bf16[2,256,128]{2,1,0:T(8,128)(2,1)S(1)}, u32[]{:S(2)}, u32[]{:S(2)}) collective-permute-start(bf16[2,256,128]{2,1,0:T(8,128)(2,1)S(1)} %copy-done.74), channel_id=1, source_target_pairs={{0,6},{1,7},{2,4},{3,5},{4,2},{5,3},{6,0},{7,1},{8,14},{9,15},{10,... | collective-permute-start | bytes 393224 | tf_op jit(solution)/shard_map/ppermute | solution.py:232
  43.6 40.1 %collective-permute-start.29 = (bf16[2,256,128]{2,1,0:T(8,128)(2,1)S(1)}, bf16[2,256,128]{2,1,0:T(8,128)(2,1)S(1)}, u32[]{:S(2)}, u32[]{:S(2)}) collective-permute-start(bf16[2,256,128]{2,1,0:T(8,128)(2,1)S(1)} %copy-done.73), channel_id=1, source_target_pairs={{0,4},{1,5},{2,6},{3,7},{4,0},{5,1},{6,2},{7,3},{8,12},{9,13},{10,... | collective-permute-start | bytes 393224 | tf_op jit(solution)/shard_map/ppermute | solution.py:232
  44.1 40.0 %collective-permute-start.30 = (bf16[2,256,128]{2,1,0:T(8,128)(2,1)S(1)}, bf16[2,256,128]{2,1,0:T(8,128)(2,1)S(1)}, u32[]{:S(2)}, u32[]{:S(2)}) collective-permute-start(bf16[2,256,128]{2,1,0:T(8,128)(2,1)S(1)} %copy-done.72), channel_id=1, source_target_pairs={{0,2},{1,3},{2,0},{3,1},{4,6},{5,7},{6,4},{7,5},{8,10},{9,11},{10,... | collective-permute-start | bytes 393224 | tf_op jit(solution)/shard_map/ppermute | solution.py:232
  44.5 41.1 %collective-permute-start.31 = (bf16[2,256,128]{2,1,0:T(8,128)(2,1)S(1)}, bf16[2,256,128]{2,1,0:T(8,128)(2,1)S(1)}, u32[]{:S(2)}, u32[]{:S(2)}) collective-permute-start(bf16[2,256,128]{2,1,0:T(8,128)(2,1)S(1)} %copy-done.71), channel_id=1, source_target_pairs={{0,7},{1,6},{2,5},{3,4},{4,3},{5,2},{6,1},{7,0},{8,15},{9,14},{10,... | collective-permute-start | bytes 393224 | tf_op jit(solution)/shard_map/ppermute | solution.py:232
  82.0 66.1 %collective-permute-start.21 = (bf16[2,1280,128]{2,1,0:T(8,128)(2,1)S(1)}, bf16[2,1280,128]{2,1,0:T(8,128)(2,1)S(1)}, u32[]{:S(2)}, u32[]{:S(2)}) collective-permute-start(bf16[2,1280,128]{2,1,0:T(8,128)(2,1)S(1)} %copy-done.65), channel_id=1, source_target_pairs={{0,6},{1,7},{2,4},{3,5},{4,2},{5,3},{6,0},{7,1},{8,14},{9,15},{10,... | collective-permute-start | bytes 1966088 | tf_op jit(solution)/shard_map/ppermute | solution.py:232
  83.7 66.3 %collective-permute-start.22 = (bf16[2,1280,128]{2,1,0:T(8,128)(2,1)S(1)}, bf16[2,1280,128]{2,1,0:T(8,128)(2,1)S(1)}, u32[]{:S(2)}, u32[]{:S(2)}) collective-permute-start(bf16[2,1280,128]{2,1,0:T(8,128)(2,1)S(1)} %copy-done.64), channel_id=1, source_target_pairs={{0,4},{1,5},{2,6},{3,7},{4,0},{5,1},{6,2},{7,3},{8,12},{9,13},{10,... | collective-permute-start | bytes 1966088 | tf_op jit(solution)/shard_map/ppermute | solution.py:232
  84.1 66.0 %collective-permute-start.23 = (bf16[2,1280,128]{2,1,0:T(8,128)(2,1)}, bf16[2,1280,128]{2,1,0:T(8,128)(2,1)S(1)}, u32[]{:S(2)}, u32[]{:S(2)}) collective-permute-start(bf16[2,1280,128]{2,1,0:T(8,128)(2,1)} %get-tuple-element.177), channel_id=1, source_target_pairs={{0,2},{1,3},{2,0},{3,1},{4,6},{5,7},{6,4},{7,5},{8,10},{9,11},{10,... | collective-permute-start | bytes 1966088 | tf_op jit(solution)/shard_map/ppermute | solution.py:232
  85.6 31.1 %collective-permute-start.33 = (bf16[2,256,128]{2,1,0:T(8,128)(2,1)S(1)}, bf16[2,256,128]{2,1,0:T(8,128)(2,1)}, u32[]{:S(2)}, u32[]{:S(2)}) collective-permute-start(bf16[2,256,128]{2,1,0:T(8,128)(2,1)S(1)} %copy-done.69), channel_id=1, source_target_pairs={{0,3},{1,2},{2,1},{3,0},{4,7},{5,6},{6,5},{7,4},{8,11},{9,10},{10,... | collective-permute-start | bytes 393224 | tf_op jit(solution)/shard_map/ppermute | solution.py:232
  116.7 34.8 %collective-permute-start.24 = (bf16[2,1280,128]{2,1,0:T(8,128)(2,1)S(1)}, bf16[2,1280,128]{2,1,0:T(8,128)(2,1)S(1)}, u32[]{:S(2)}, u32[]{:S(2)}) collective-permute-start(bf16[2,1280,128]{2,1,0:T(8,128)(2,1)S(1)} %copy-done.63), channel_id=1, source_target_pairs={{0,7},{1,6},{2,5},{3,4},{4,3},{5,2},{6,1},{7,0},{8,15},{9,14},{10,... | collective-permute-start | bytes 1966088 | tf_op jit(solution)/shard_map/ppermute | solution.py:232
  150.1 30.9 %collective-permute-start.14 = (bf16[2,1280,128]{2,1,0:T(8,128)(2,1)}, bf16[2,1280,128]{2,1,0:T(8,128)(2,1)S(1)}, u32[]{:S(2)}, u32[]{:S(2)}) collective-permute-start(bf16[2,1280,128]{2,1,0:T(8,128)(2,1)} %get-tuple-element.168), channel_id=1, source_target_pairs={{0,6},{1,7},{2,4},{3,5},{4,2},{5,3},{6,0},{7,1},{8,14},{9,15},{10,... | collective-permute-start | bytes 1966088 | tf_op jit(solution)/shard_map/ppermute | solution.py:232
  151.5 41.8 %collective-permute-start.15 = (bf16[2,1280,128]{2,1,0:T(8,128)(2,1)}, bf16[2,1280,128]{2,1,0:T(8,128)(2,1)S(1)}, u32[]{:S(2)}, u32[]{:S(2)}) collective-permute-start(bf16[2,1280,128]{2,1,0:T(8,128)(2,1)} %get-tuple-element.169), channel_id=1, source_target_pairs={{0,4},{1,5},{2,6},{3,7},{4,0},{5,1},{6,2},{7,3},{8,12},{9,13},{10,... | collective-permute-start | bytes 1966088 | tf_op jit(solution)/shard_map/ppermute | solution.py:232
  167.8 39.9 %collective-permute-start.17 = (bf16[2,1280,128]{2,1,0:T(8,128)(2,1)}, bf16[2,1280,128]{2,1,0:T(8,128)(2,1)S(1)}, u32[]{:S(2)}, u32[]{:S(2)}) collective-permute-start(bf16[2,1280,128]{2,1,0:T(8,128)(2,1)} %get-tuple-element.171), channel_id=1, source_target_pairs={{0,7},{1,6},{2,5},{3,4},{4,3},{5,2},{6,1},{7,0},{8,15},{9,14},{10,... | collective-permute-start | bytes 1966088 | tf_op jit(solution)/shard_map/ppermute | solution.py:232
  168.0 53.1 %collective-permute-start.18 = (bf16[2,1280,128]{2,1,0:T(8,128)(2,1)}, bf16[2,1280,128]{2,1,0:T(8,128)(2,1)S(1)}, u32[]{:S(2)}, u32[]{:S(2)}) collective-permute-start(bf16[2,1280,128]{2,1,0:T(8,128)(2,1)} %get-tuple-element.172), channel_id=1, source_target_pairs={{0,5},{1,4},{2,7},{3,6},{4,1},{5,0},{6,3},{7,2},{8,13},{9,12},{10,... | collective-permute-start | bytes 1966088 | tf_op jit(solution)/shard_map/ppermute | solution.py:232
  181.0 40.5 %collective-permute-start.19 = (bf16[2,1280,128]{2,1,0:T(8,128)(2,1)}, bf16[2,1280,128]{2,1,0:T(8,128)(2,1)}, u32[]{:S(2)}, u32[]{:S(2)}) collective-permute-start(bf16[2,1280,128]{2,1,0:T(8,128)(2,1)} %get-tuple-element.173), channel_id=1, source_target_pairs={{0,3},{1,2},{2,1},{3,0},{4,7},{5,6},{6,5},{7,4},{8,11},{9,10},{10,... | collective-permute-start | bytes 1966088 | tf_op jit(solution)/shard_map/ppermute | solution.py:232
  193.3 48.0 %collective-permute-start.20 = (bf16[2,1280,128]{2,1,0:T(8,128)(2,1)}, bf16[2,1280,128]{2,1,0:T(8,128)(2,1)}, u32[]{:S(2)}, u32[]{:S(2)}) collective-permute-start(bf16[2,1280,128]{2,1,0:T(8,128)(2,1)} %get-tuple-element.174), channel_id=1, source_target_pairs={{0,1},{1,0},{2,3},{3,2},{4,5},{5,4},{6,7},{7,6},{8,9},{9,8},{10,11... | collective-permute-start | bytes 1966088 | tf_op jit(solution)/shard_map/ppermute | solution.py:232
  195.1 56.5 %collective-permute-start.59 = (bf16[2,256,128]{2,1,0:T(8,128)(2,1)S(1)}, bf16[2,256,128]{2,1,0:T(8,128)(2,1)S(1)}, u32[]{:S(2)}, u32[]{:S(2)}) collective-permute-start(bf16[2,256,128]{2,1,0:T(8,128)(2,1)S(1)} %copy-done.75), channel_id=1, source_target_pairs={{0,7},{1,6},{2,5},{3,4},{4,3},{5,2},{6,1},{7,0},{8,15},{9,14},{10,... | collective-permute-start | bytes 393224 | tf_op jit(solution)/shard_map/ppermute | solution.py:232
  207.7 45.5 %collective-permute-start.60 = (bf16[2,256,128]{2,1,0:T(8,128)(2,1)}, bf16[2,256,128]{2,1,0:T(8,128)(2,1)S(1)}, u32[]{:S(2)}, u32[]{:S(2)}) collective-permute-start(bf16[2,256,128]{2,1,0:T(8,128)(2,1)} %get-tuple-element.264), channel_id=1, source_target_pairs={{0,5},{1,4},{2,7},{3,6},{4,1},{5,0},{6,3},{7,2},{8,13},{9,12},{10,... | collective-permute-start | bytes 393224 | tf_op jit(solution)/shard_map/ppermute | solution.py:232
  221.1 34.9 %collective-permute-start.61 = (bf16[2,256,128]{2,1,0:T(8,128)(2,1)}, bf16[2,256,128]{2,1,0:T(8,128)(2,1)}, u32[]{:S(2)}, u32[]{:S(2)}) collective-permute-start(bf16[2,256,128]{2,1,0:T(8,128)(2,1)} %get-tuple-element.265), channel_id=1, source_target_pairs={{0,3},{1,2},{2,1},{3,0},{4,7},{5,6},{6,5},{7,4},{8,11},{9,10},{10,... | collective-permute-start | bytes 393224 | tf_op jit(solution)/shard_map/ppermute | solution.py:232
  221.5 35.2 %collective-permute-start.62 = (bf16[2,256,128]{2,1,0:T(8,128)(2,1)}, bf16[2,256,128]{2,1,0:T(8,128)(2,1)}, u32[]{:S(2)}, u32[]{:S(2)}) collective-permute-start(bf16[2,256,128]{2,1,0:T(8,128)(2,1)} %get-tuple-element.266), channel_id=1, source_target_pairs={{0,1},{1,0},{2,3},{3,2},{4,5},{5,4},{6,7},{7,6},{8,9},{9,8},{10,11... | collective-permute-start | bytes 393224 | tf_op jit(solution)/shard_map/ppermute | solution.py:232
  256.0 31.6 %collective-permute-start.49 = (bf16[2,640,128]{2,1,0:T(8,128)(2,1)S(1)}, bf16[2,640,128]{2,1,0:T(8,128)(2,1)S(1)}, u32[]{:S(2)}, u32[]{:S(2)}) collective-permute-start(bf16[2,640,128]{2,1,0:T(8,128)(2,1)S(1)} %copy-done.67), channel_id=1, source_target_pairs={{0,6},{1,7},{2,4},{3,5},{4,2},{5,3},{6,0},{7,1},{8,14},{9,15},{10,... | collective-permute-start | bytes 983048 | tf_op jit(solution)/shard_map/ppermute | solution.py:232
  256.7 32.2 %collective-permute-start.50 = (bf16[2,640,128]{2,1,0:T(8,128)(2,1)S(1)}, bf16[2,640,128]{2,1,0:T(8,128)(2,1)S(1)}, u32[]{:S(2)}, u32[]{:S(2)}) collective-permute-start(bf16[2,640,128]{2,1,0:T(8,128)(2,1)S(1)} %copy-done.66), channel_id=1, source_target_pairs={{0,4},{1,5},{2,6},{3,7},{4,0},{5,1},{6,2},{7,3},{8,12},{9,13},{10,... | collective-permute-start | bytes 983048 | tf_op jit(solution)/shard_map/ppermute | solution.py:232
  295.2 41.7 %collective-permute-start.37 = (bf16[2,128,128]{2,1,0:T(8,128)(2,1)}, bf16[2,128,128]{2,1,0:T(8,128)(2,1)S(1)}, u32[]{:S(2)}, u32[]{:S(2)}) collective-permute-start(bf16[2,128,128]{2,1,0:T(8,128)(2,1)} %get-tuple-element.239), channel_id=1, source_target_pairs={{0,2},{1,3},{2,0},{3,1},{4,6},{5,7},{6,4},{7,5},{8,10},{9,11},{10,... | collective-permute-start | bytes 196616 | tf_op jit(solution)/shard_map/ppermute | solution.py:232
  301.7 35.2 %collective-permute-start.38 = (bf16[2,128,128]{2,1,0:T(8,128)(2,1)}, bf16[2,128,128]{2,1,0:T(8,128)(2,1)S(1)}, u32[]{:S(2)}, u32[]{:S(2)}) collective-permute-start(bf16[2,128,128]{2,1,0:T(8,128)(2,1)} %get-tuple-element.240), channel_id=1, source_target_pairs={{0,7},{1,6},{2,5},{3,4},{4,3},{5,2},{6,1},{7,0},{8,15},{9,14},{10,... | collective-permute-start | bytes 196616 | tf_op jit(solution)/shard_map/ppermute | solution.py:232
  304.4 32.5 %collective-permute-start.39 = (bf16[2,128,128]{2,1,0:T(8,128)(2,1)}, bf16[2,128,128]{2,1,0:T(8,128)(2,1)S(1)}, u32[]{:S(2)}, u32[]{:S(2)}) collective-permute-start(bf16[2,128,128]{2,1,0:T(8,128)(2,1)} %get-tuple-element.241), channel_id=1, source_target_pairs={{0,5},{1,4},{2,7},{3,6},{4,1},{5,0},{6,3},{7,2},{8,13},{9,12},{10,... | collective-permute-start | bytes 196616 | tf_op jit(solution)/shard_map/ppermute | solution.py:232
  (121 other events, 3206.3 us)

commit v6 on v5

--- a/solution.py
+++ b/solution.py
@@ -14,7 +14,7 @@
 PEERS = 8
 GROUP = 32
 WRAP = 256
-CHUNKS = ((256, 256), (512, 1280), (1792, 1280), (3072, 640), (3712, 256), (3968, 128))
+CHUNKS = ((256, 512), (768, 1024), (1792, 1280), (3072, 640), (3712, 256), (3968, 128))
 BLOCK = 256
 ORDER = (6, 4, 2, 7, 5, 3, 1)
 VMEM_LIMIT = 56 * 1024 * 1024
@@ -33,8 +33,7 @@
     return jnp.concatenate([first_half * cos_part - second_half * sin_part, second_half * cos_part + first_half * sin_part], axis=-1).astype(jnp.bfloat16)
 
 
-def pack_kernel(first, count, has_own, k_ref, v_ref, *refs):
-    offsets = ORDER + (0,) * has_own
+def pack_kernel(first, count, offsets, k_ref, v_ref, *refs):
     outs, sems = refs[:-1], refs[-1]
     me = lax.axis_index('sh')
     copies = []
@@ -46,11 +45,11 @@
         copy.wait()
 
 
-def pack(first, count, has_own, k_mine, v_mine):
+def pack(first, count, offsets, k_mine, v_mine):
     dim = k_mine.shape[2]
-    pieces = len(ORDER) + has_own
+    pieces = len(offsets)
     return pl.pallas_call(
-        functools.partial(pack_kernel, first, count, has_own),
+        functools.partial(pack_kernel, first, count, offsets),
         out_shape=[jax.ShapeDtypeStruct((2, count, dim), jnp.bfloat16)] * pieces,
         in_specs=[pl.BlockSpec(memory_space=pltpu.HBM)] * 2,
         out_specs=[pl.BlockSpec(memory_space=pltpu.VMEM)] * pieces,
@@ -247,20 +246,22 @@
         my_len = lax.dynamic_slice_in_dim(lengths, me, 1)
         received = {}
 
-        def send(first, pieces):
-            received[first] = [swap(piece, offset) for piece, offset in zip(pieces, ORDER)]
-
-        def start(chunk, after=None, before=None):
+        def send(first, pieces, offsets=ORDER):
+            received[first] = received.get(first, []) + [swap(piece, offset) for piece, offset in zip(pieces, offsets)]
+
+        def start(chunk, after=None, before=None, offsets=ORDER):
             prefills = (k_mine, v_mine)
             if after is not None:
                 prefills, after = lax.optimization_barrier((prefills, after))
-            pieces = pack(*chunk, chunk == CHUNKS[-1], *prefills)
+            own = (0,) * (chunk == CHUNKS[-1])
+            pieces = pack(*chunk, offsets + own, *prefills)
             pieces, before = lax.optimization_barrier((pieces, before))
-            send(chunk[0], pieces)
-            received[chunk[0]] += pieces[len(ORDER):]
+            send(chunk[0], pieces, offsets)
+            received[chunk[0]] += pieces[len(offsets):]
             return after, before
 
-        _, residual = start(CHUNKS[0], before=residual)
+        _, residual = start(CHUNKS[0], before=residual, offsets=ORDER[:1])
+        _, residual = start(CHUNKS[0], after=residual, before=residual, offsets=ORDER[1:])
         _, residual = start(CHUNKS[1], after=residual, before=residual)
 
         resid_f32 = residual.astype(jnp.float32)

time: 342 us -> 321 us (0.939)
  waiting for transfers between devices: 168 us -> 150 us
    ppermute x63, waiting for transfers between devices: 168 us -> 150 us  [swap(): return lax.ppermute(value, 'sh', [(i, i ^ offset) for i in range(PEERS)])]
    pallas_call x6 -> x7, Pallas kernels: 19.1 us -> 20.4 us  [pack(): pl.pallas_call(functools.partial(pack_kernel, first, count, offsets), out...]
  transfers between devices with their start and end apart: 63 -> 63, of which waited for: 25 -> 26; matrix products, arithmetic and copies ran while one was open for 8% -> 9% of each run, Pallas kernels for 13% -> 14%
where the time goes in v6:
time: 321 us; the launch traced here: 318 us
  waiting for transfers between devices  150 us (47%)
  starting transfers between devices  59 us (18%)
  Pallas kernels  53.7 us (17%)
  matrix products  46.7 us (15%)
  between operations  3.38 us (1%)
    ppermute x63, waiting for transfers between devices, swap(): return lax.ppermute(value, 'sh', [(i, i ^ offset) for i in range(PEERS)])  150 us
    ppermute x63, starting transfers between devices, swap(): return lax.ppermute(value, 'sh', [(i, i ^ offset) for i in range(PEERS)])  59 us
    pallas_call x6, Pallas kernels, interleave(): pl.pallas_call(functools.partial(interleave_kernel, first, count, block,...  29.2 us
    pallas_call x7, Pallas kernels, pack(): pl.pallas_call(functools.partial(pack_kernel, first, count, offsets), out...  20.4 us
    dot_general x1, matrix products, per_device(): jnp.dot(attn_out, w_out, preferred_element_type=jnp.float32)  13.4 us
    dot_general x1, matrix products, per_device(): jnp.dot(normed, w_query, preferred_element_type=jnp.float32)  12.9 us
  transfers between devices with their start and end apart: 63, of which 26 were waited for; matrix products, arithmetic and copies ran while one was open for 9% of the time, Pallas kernels for 14%

profile of v6, /device:TPU:0, one launch (start us, length us, event | category | flops | bytes accessed | tf_op | source)
XLA Modules:
  0.0 318.2 jit_solution(4803429126887914081)
XLA Ops:
  5.2 3.9 %shard_map.114 = (bf16[2,1024,128]{2,1,0:T(8,128)(2,1)}, bf16[2,1024,128]{2,1,0:T(8,128)(2,1)}, bf16[2,1024,128]{2,1,0:T(8,128)(2,1)}, bf16[2,1024,128]{2,1,0:T(...) custom-call(bf16[8,4352,128]{2,1,0:T(8,128)(2,1)} %bitcast.77, ...), custom_call_target="tpu_custom_call" | custom-call | bytes 7340032 | tf_op jit(solution)/shard_map/pallas_call | solution.py:51
  10.5 4.6 %fusion.14 = f32[1,1024]{1,0:T(1,128)S(1)} fusion(bf16[4096,1024]{1,0:T(8,128)(2,1)} %param.15, f32[1,4096]{1,0:T(1,128)S(1)} %bitcast.91, bf16[1,4096]{1,0:T(2,128)(2,1)S(1)} %copy-done.2, f32[]{:T(128)S(6)} %rsqrt.4), kind=kOutput, calls=%fused_computation.28 | convolution fusion | flops 8404992 | bytes 8417284 | tf_op jit(solution)/shard_map/dot_general | solution.py:271
  16.5 4.6 %fusion.12 = f32[1,1024]{1,0:T(1,128)S(1)} fusion(bf16[4096,1024]{1,0:T(8,128)(2,1)} %param.16, f32[1,4096]{1,0:T(1,128)S(1)} %bitcast.92, bf16[1,4096]{1,0:T(2,128)(2,1)S(1)} %copy-done.2, f32[]{:T(128)S(6)} %rsqrt.4), kind=kOutput, calls=%fused_computation.26 | convolution fusion | flops 8404992 | bytes 8417284 | tf_op jit(solution)/shard_map/dot_general | solution.py:272
  21.1 12.9 %fusion.16 = f32[1,4096]{1,0:T(1,128)S(1)} fusion(bf16[4096,4096]{1,0:T(8,128)(2,1)} %param.14, f32[1,4096]{1,0:T(1,128)S(1)} %bitcast.93, bf16[1,4096]{1,0:T(2,128)(2,1)S(1)} %copy-done.2, f32[]{:T(128)S(6)} %rsqrt.4), kind=kOutput, calls=%fused_computation.30 | convolution fusion | flops 33570816 | bytes 33595396 | tf_op jit(solution)/shard_map/dot_general | solution.py:270
  51.1 6.0 %fusion.32 = (f32[8,4]{1,0:T(8,128)S(1)}, f32[8,4,4352]{2,1,0:T(4,128)S(1)}) fusion(bf16[8,4352,1,128]{3,1,2,0:T(8,128)(2,1)} %param.9, bf16[8,6,128]{2,1,0:T(8,128)(2,1)S(1)} %copy_select_fusion, pred[8,4352]{1,0:T(8,128)(4,1)S(1)} %fusion.7), kind=kOutput, calls=%fused_computation.91 | convolution fusion | flops 36069344 | bytes 9513088 | tf_op jit(solution)/shard_map/bgd,bsd->bgs/dot_general | solution.py:288
  57.6 5.2 %fusion.3 = bf16[1,8,4,128]{3,2,1,0:T(4,128)(2,1)S(1)} fusion(f32[8,4,4352]{2,1,0:T(4,128)S(1)} %get-tuple-element.308, f32[8,4]{1,0:T(8,128)S(1)} %get-tuple-element.284, f32[8,4]{1,0:T(8,128)S(1)} %multiply_maximum_fusion, f32[8,128]{1,0:T(8,128)S(1)} %bitcast.95, f32[8,4]{1,0:T(8,128)S(1)} %get-tuple-element.283, bf16[8,4352,1,128]{3,1,2,0:T(8,128)(2,1)} %param.10), kind=kOutput, calls=%fused_computation.8 | convolution fusion | flops 36081664 | bytes 9482624 | tf_op jit(solution)/shard_map/bgs,bsd->bgd/dot_general | solution.py:298
  70.9 3.6 %collective-permute-done.12 = bf16[1,512]{1,0:T(2,128)(2,1)S(1)} collective-permute-done((bf16[1,512]{1,0:T(2,128)(2,1)S(1)}, bf16[1,512]{1,0:T(2,128)(2,1)S(1)}, u32[]{:S(2)}, u32[]{:S(2)}) %collective-permute-start.12) | collective-permute-done | bytes 1056 | tf_op jit(solution)/shard_map/ppermute | solution.py:231
  74.5 3.9 %collective-permute-done.13 = bf16[1,512]{1,0:T(2,128)(2,1)S(1)} collective-permute-done((bf16[1,512]{1,0:T(2,128)(2,1)S(1)}, bf16[1,512]{1,0:T(2,128)(2,1)S(1)}, u32[]{:S(2)}, u32[]{:S(2)}) %collective-permute-start.13) | collective-permute-done | bytes 1056 | tf_op jit(solution)/shard_map/ppermute | solution.py:231
  104.5 3.6 %collective-permute-done.32.refs_6_ = bf16[2,512,128]{2,1,0:T(8,128)(2,1)} collective-permute-done((bf16[2,512,128]{2,1,0:T(8,128)(2,1)S(1)}, bf16[2,512,128]{2,1,0:T(8,128)(2,1)}, u32[]{:S(2)}, u32[]{:S(2)}) %collective-permute-start.32) | collective-permute-done | bytes 262176 | tf_op jit(solution)/shard_map/ppermute | solution.py:231
  112.2 4.5 %shard_map.115 = (bf16[2,1280,128]{2,1,0:T(8,128)(2,1)}, bf16[2,1280,128]{2,1,0:T(8,128)(2,1)}, bf16[2,1280,128]{2,1,0:T(8,128)(2,1)}, bf16[2,1280,128]{2,1,0:T(...) custom-call(bf16[8,4352,128]{2,1,0:T(8,128)(2,1)} %bitcast.80, ...), custom_call_target="tpu_custom_call" | custom-call | bytes 9175040 | tf_op jit(solution)/shard_map/pallas_call | solution.py:51
  116.8 31.9 %collective-permute-done.28.refs_2_ = bf16[2,512,128]{2,1,0:T(8,128)(2,1)S(1)} collective-permute-done((bf16[2,512,128]{2,1,0:T(8,128)(2,1)S(1)}, bf16[2,512,128]{2,1,0:T(8,128)(2,1)S(1)}, u32[]{:S(2)}, u32[]{:S(2)}) %collective-permute-start.28) | collective-permute-done | bytes 262176 | tf_op jit(solution)/shard_map/ppermute | solution.py:231
  153.3 38.0 %collective-permute-done.25.refs_6_ = bf16[2,1024,128]{2,1,0:T(8,128)(2,1)S(1)} collective-permute-done((bf16[2,1024,128]{2,1,0:T(8,128)(2,1)S(1)}, bf16[2,1024,128]{2,1,0:T(8,128)(2,1)S(1)}, u32[]{:S(2)}, u32[]{:S(2)}) %collective-permute-start.25) | collective-permute-done | bytes 524320 | tf_op jit(solution)/shard_map/ppermute | solution.py:231
  196.7 4.7 %shard_map.116 = (bf16[32768,128]{1,0:T(8,128)(2,1)}, bf16[32768,128]{1,0:T(8,128)(2,1)}) custom-call(s32[1]{0:T(128)} %dynamic_slice.51.len_ref, f32[3,8,128]{2,1,0:T(8,128)} %maximum_maximum_fusion.new_ref, bf16[8,4352,128]{2,1,0:T(8,128)(2,1)} %bitcast.81, bf16[8,4352,128]{2,1,0:T(8,128)(2,1)} %bitcast.67, bf16[2,512,128]{2,1,0:T(8,128)(2,1)} %copy-done.27, ...), custom_call_target="tpu_custom_call" | custom-call | flops 4194304 | bytes 4194304 | tf_op jit(solution)/shard_map/pallas_call | solution.py:166
  201.5 5.4 %shard_map.117 = (bf16[32768,128]{1,0:T(8,128)(2,1)}, bf16[32768,128]{1,0:T(8,128)(2,1)}) custom-call(s32[1]{0:T(128)} %dynamic_slice.51.len_ref, f32[3,8,128]{2,1,0:T(8,128)} %maximum_maximum_fusion.new_ref, bf16[8,4352,128]{2,1,0:T(8,128)(2,1)} %bitcast.82, bf16[8,4352,128]{2,1,0:T(8,128)(2,1)} %bitcast.68, ...), custom_call_target="tpu_custom_call", output_to_operand_aliasing={{0}: (11, {}), {1}: (12, {})} | custom-call | flops 8388608 | bytes 8388608 | tf_op jit(solution)/shard_map/pallas_call | solution.py:166
  213.5 8.6 %collective-permute-done.17.refs_5_ = bf16[2,1280,128]{2,1,0:T(8,128)(2,1)S(1)} collective-permute-done((bf16[2,1280,128]{2,1,0:T(8,128)(2,1)}, bf16[2,1280,128]{2,1,0:T(8,128)(2,1)S(1)}, u32[]{:S(2)}, u32[]{:S(2)}) %collective-permute-start.17) | collective-permute-done | bytes 655392 | tf_op jit(solution)/shard_map/ppermute | solution.py:231
  224.4 11.7 %collective-permute-done.19.refs_7_ = bf16[2,1280,128]{2,1,0:T(8,128)(2,1)S(1)} collective-permute-done((bf16[2,1280,128]{2,1,0:T(8,128)(2,1)}, bf16[2,1280,128]{2,1,0:T(8,128)(2,1)S(1)}, u32[]{:S(2)}, u32[]{:S(2)}) %collective-permute-start.19) | collective-permute-done | bytes 655392 | tf_op jit(solution)/shard_map/ppermute | solution.py:231
  242.8 8.8 %collective-permute-done.45.refs_5_ = bf16[2,256,128]{2,1,0:T(8,128)(2,1)S(1)} collective-permute-done((bf16[2,256,128]{2,1,0:T(8,128)(2,1)}, bf16[2,256,128]{2,1,0:T(8,128)(2,1)S(1)}, u32[]{:S(2)}, u32[]{:S(2)}) %collective-permute-start.45) | collective-permute-done | bytes 131104 | tf_op jit(solution)/shard_map/ppermute | solution.py:231
  253.1 6.7 %shard_map.120 = (bf16[32768,128]{1,0:T(8,128)(2,1)}, bf16[32768,128]{1,0:T(8,128)(2,1)}) custom-call(s32[1]{0:T(128)} %dynamic_slice.51.len_ref, f32[3,8,128]{2,1,0:T(8,128)} %maximum_maximum_fusion.new_ref, bf16[8,4352,128]{2,1,0:T(8,128)(2,1)} %bitcast.85, bf16[8,4352,128]{2,1,0:T(8,128)(2,1)} %bitcast.71, ...), custom_call_target="tpu_custom_call", output_to_operand_aliasing={{0}: (11, {}), {1}: (12, {})} | custom-call | flops 10485760 | bytes 10485760 | tf_op jit(solution)/shard_map/pallas_call | solution.py:166
  272.3 4.1 %collective-permute-done.51.refs_4_ = bf16[2,640,128]{2,1,0:T(8,128)(2,1)S(1)} collective-permute-done((bf16[2,640,128]{2,1,0:T(8,128)(2,1)}, bf16[2,640,128]{2,1,0:T(8,128)(2,1)S(1)}, u32[]{:S(2)}, u32[]{:S(2)}) %collective-permute-start.51) | collective-permute-done | bytes 327712 | tf_op jit(solution)/shard_map/ppermute | solution.py:231
  276.7 4.7 %collective-permute-done.52.refs_5_ = bf16[2,640,128]{2,1,0:T(8,128)(2,1)S(1)} collective-permute-done((bf16[2,640,128]{2,1,0:T(8,128)(2,1)}, bf16[2,640,128]{2,1,0:T(8,128)(2,1)S(1)}, u32[]{:S(2)}, u32[]{:S(2)}) %collective-permute-start.52) | collective-permute-done | bytes 327712 | tf_op jit(solution)/shard_map/ppermute | solution.py:231
  290.7 13.4 %fusion.1 = bf16[1,4096]{1,0:T(2,128)(2,1)} fusion(bf16[4096,1]{0,1:T(2,128)(2,1)S(1)} %bitcast.96, bf16[4096,4096]{1,0:T(8,128)(2,1)} %param.17, bf16[1,4096]{1,0:T(2,128)(2,1)S(1)} %copy-done.2), kind=kOutput, calls=%fused_computation.5 | convolution fusion | flops 33566720 | bytes 33579008 | tf_op jit(solution)/shard_map/dot_general | solution.py:319
  304.2 3.8 %shard_map.123 = (bf16[32768,128]{1,0:T(8,128)(2,1)}, bf16[32768,128]{1,0:T(8,128)(2,1)}) custom-call(s32[1]{0:T(128)} %dynamic_slice.51.len_ref, f32[3,8,128]{2,1,0:T(8,128)} %maximum_maximum_fusion.new_ref, bf16[2,256,128]{2,1,0:T(8,128)(2,1)} %get-tuple-element.263.refs_0_, ...), custom_call_target="tpu_custom_call", output_to_operand_aliasing={{0}: (10, {}), {1}: (11, {})} | custom-call | flops 2097152 | bytes 2097152 | tf_op jit(solution)/shard_map/pallas_call | solution.py:166
  308.0 4.8 %shard_map.124 = (bf16[32768,128]{1,0:T(8,128)(2,1)}, bf16[32768,128]{1,0:T(8,128)(2,1)}) custom-call(s32[1]{0:T(128)} %dynamic_slice.51.len_ref, f32[3,8,128]{2,1,0:T(8,128)} %maximum_maximum_fusion.new_ref, bf16[8,4352,128]{2,1,0:T(8,128)(2,1)} %bitcast.87, bf16[8,4352,128]{2,1,0:T(8,128)(2,1)} %bitcast.73, ...), custom_call_target="tpu_custom_call", output_to_operand_aliasing={{0}: (11, {}), {1}: (12, {})} | custom-call | flops 5242880 | bytes 5242880 | tf_op jit(solution)/shard_map/pallas_call | solution.py:166
  312.8 3.8 %shard_map.125 = (bf16[32768,128]{1,0:T(8,128)(2,1)}, bf16[32768,128]{1,0:T(8,128)(2,1)}) custom-call(s32[1]{0:T(128)} %dynamic_slice.51.len_ref, f32[3,8,128]{2,1,0:T(8,128)} %maximum_maximum_fusion.new_ref, bf16[8,4352,128]{2,1,0:T(8,128)(2,1)} %bitcast.88, bf16[8,4352,128]{2,1,0:T(8,128)(2,1)} %bitcast.74, ...), custom_call_target="tpu_custom_call", output_to_operand_aliasing={{0}: (11, {}), {1}: (12, {})} | custom-call | flops 2097152 | bytes 2097152 | tf_op jit(solution)/shard_map/pallas_call | solution.py:166
  (322 shorter events, 111.7 us)
Async XLA Ops:
  45.0 41.2 %collective-permute-start.56 = (bf16[2,256,128]{2,1,0:T(8,128)(2,1)}, bf16[2,256,128]{2,1,0:T(8,128)(2,1)S(1)}, u32[]{:S(2)}, u32[]{:S(2)}) collective-permute-start(bf16[2,256,128]{2,1,0:T(8,128)(2,1)} %get-tuple-element.264), channel_id=1, source_target_pairs={{0,6},{1,7},{2,4},{3,5},{4,2},{5,3},{6,0},{7,1},{8,14},{9,15},{10,... | collective-permute-start | bytes 393224 | tf_op jit(solution)/shard_map/ppermute | solution.py:231
  47.6 39.8 %collective-permute-start.57 = (bf16[2,256,128]{2,1,0:T(8,128)(2,1)}, bf16[2,256,128]{2,1,0:T(8,128)(2,1)S(1)}, u32[]{:S(2)}, u32[]{:S(2)}) collective-permute-start(bf16[2,256,128]{2,1,0:T(8,128)(2,1)} %get-tuple-element.265), channel_id=1, source_target_pairs={{0,4},{1,5},{2,6},{3,7},{4,0},{5,1},{6,2},{7,3},{8,12},{9,13},{10,... | collective-permute-start | bytes 393224 | tf_op jit(solution)/shard_map/ppermute | solution.py:231
  48.2 39.4 %collective-permute-start.58 = (bf16[2,256,128]{2,1,0:T(8,128)(2,1)}, bf16[2,256,128]{2,1,0:T(8,128)(2,1)S(1)}, u32[]{:S(2)}, u32[]{:S(2)}) collective-permute-start(bf16[2,256,128]{2,1,0:T(8,128)(2,1)} %get-tuple-element.266), channel_id=1, source_target_pairs={{0,2},{1,3},{2,0},{3,1},{4,6},{5,7},{6,4},{7,5},{8,10},{9,11},{10,... | collective-permute-start | bytes 393224 | tf_op jit(solution)/shard_map/ppermute | solution.py:231
  48.6 40.2 %collective-permute-start.59 = (bf16[2,256,128]{2,1,0:T(8,128)(2,1)}, bf16[2,256,128]{2,1,0:T(8,128)(2,1)S(1)}, u32[]{:S(2)}, u32[]{:S(2)}) collective-permute-start(bf16[2,256,128]{2,1,0:T(8,128)(2,1)} %get-tuple-element.267), channel_id=1, source_target_pairs={{0,7},{1,6},{2,5},{3,4},{4,3},{5,2},{6,1},{7,0},{8,15},{9,14},{10,... | collective-permute-start | bytes 393224 | tf_op jit(solution)/shard_map/ppermute | solution.py:231
  98.2 52.1 %collective-permute-start.21 = (bf16[2,1024,128]{2,1,0:T(8,128)(2,1)S(1)}, bf16[2,1024,128]{2,1,0:T(8,128)(2,1)S(1)}, u32[]{:S(2)}, u32[]{:S(2)}) collective-permute-start(bf16[2,1024,128]{2,1,0:T(8,128)(2,1)S(1)} %copy-done.68), channel_id=1, source_target_pairs={{0,6},{1,7},{2,4},{3,5},{4,2},{5,3},{6,0},{7,1},{8,14},{9,15},{10,... | collective-permute-start | bytes 1572872 | tf_op jit(solution)/shard_map/ppermute | solution.py:231
  103.4 48.1 %collective-permute-start.22 = (bf16[2,1024,128]{2,1,0:T(8,128)(2,1)S(1)}, bf16[2,1024,128]{2,1,0:T(8,128)(2,1)S(1)}, u32[]{:S(2)}, u32[]{:S(2)}) collective-permute-start(bf16[2,1024,128]{2,1,0:T(8,128)(2,1)S(1)} %copy-done.67), channel_id=1, source_target_pairs={{0,4},{1,5},{2,6},{3,7},{4,0},{5,1},{6,2},{7,3},{8,12},{9,13},{10,... | collective-permute-start | bytes 1572872 | tf_op jit(solution)/shard_map/ppermute | solution.py:231
  108.1 43.5 %collective-permute-start.23 = (bf16[2,1024,128]{2,1,0:T(8,128)(2,1)S(1)}, bf16[2,1024,128]{2,1,0:T(8,128)(2,1)S(1)}, u32[]{:S(2)}, u32[]{:S(2)}) collective-permute-start(bf16[2,1024,128]{2,1,0:T(8,128)(2,1)S(1)} %copy-done.66), channel_id=1, source_target_pairs={{0,2},{1,3},{2,0},{3,1},{4,6},{5,7},{6,4},{7,5},{8,10},{9,11},{10,... | collective-permute-start | bytes 1572872 | tf_op jit(solution)/shard_map/ppermute | solution.py:231
  109.2 44.0 %collective-permute-start.24 = (bf16[2,1024,128]{2,1,0:T(8,128)(2,1)S(1)}, bf16[2,1024,128]{2,1,0:T(8,128)(2,1)S(1)}, u32[]{:S(2)}, u32[]{:S(2)}) collective-permute-start(bf16[2,1024,128]{2,1,0:T(8,128)(2,1)S(1)} %copy-done.65), channel_id=1, source_target_pairs={{0,7},{1,6},{2,5},{3,4},{4,3},{5,2},{6,1},{7,0},{8,15},{9,14},{10,... | collective-permute-start | bytes 1572872 | tf_op jit(solution)/shard_map/ppermute | solution.py:231
  111.0 37.7 %collective-permute-start.28 = (bf16[2,512,128]{2,1,0:T(8,128)(2,1)S(1)}, bf16[2,512,128]{2,1,0:T(8,128)(2,1)S(1)}, u32[]{:S(2)}, u32[]{:S(2)}) collective-permute-start(bf16[2,512,128]{2,1,0:T(8,128)(2,1)S(1)} %copy-done.23), channel_id=1, source_target_pairs={{0,6},{1,7},{2,4},{3,5},{4,2},{5,3},{6,0},{7,1},{8,14},{9,15},{10,... | collective-permute-start | bytes 786440 | tf_op jit(solution)/shard_map/ppermute | solution.py:231
  148.7 45.8 %collective-permute-start.14 = (bf16[2,1280,128]{2,1,0:T(8,128)(2,1)}, bf16[2,1280,128]{2,1,0:T(8,128)(2,1)S(1)}, u32[]{:S(2)}, u32[]{:S(2)}) collective-permute-start(bf16[2,1280,128]{2,1,0:T(8,128)(2,1)} %get-tuple-element.172), channel_id=1, source_target_pairs={{0,6},{1,7},{2,4},{3,5},{4,2},{5,3},{6,0},{7,1},{8,14},{9,15},{10,... | collective-permute-start | bytes 1966088 | tf_op jit(solution)/shard_map/ppermute | solution.py:231
  150.3 44.9 %collective-permute-start.15 = (bf16[2,1280,128]{2,1,0:T(8,128)(2,1)}, bf16[2,1280,128]{2,1,0:T(8,128)(2,1)S(1)}, u32[]{:S(2)}, u32[]{:S(2)}) collective-permute-start(bf16[2,1280,128]{2,1,0:T(8,128)(2,1)} %get-tuple-element.173), channel_id=1, source_target_pairs={{0,4},{1,5},{2,6},{3,7},{4,0},{5,1},{6,2},{7,3},{8,12},{9,13},{10,... | collective-permute-start | bytes 1966088 | tf_op jit(solution)/shard_map/ppermute | solution.py:231
  151.5 39.7 %collective-permute-start.25 = (bf16[2,1024,128]{2,1,0:T(8,128)(2,1)S(1)}, bf16[2,1024,128]{2,1,0:T(8,128)(2,1)S(1)}, u32[]{:S(2)}, u32[]{:S(2)}) collective-permute-start(bf16[2,1024,128]{2,1,0:T(8,128)(2,1)S(1)} %copy-done.64), channel_id=1, source_target_pairs={{0,5},{1,4},{2,7},{3,6},{4,1},{5,0},{6,3},{7,2},{8,13},{9,12},{10,... | collective-permute-start | bytes 1572872 | tf_op jit(solution)/shard_map/ppermute | solution.py:231
  151.6 40.9 %collective-permute-start.26 = (bf16[2,1024,128]{2,1,0:T(8,128)(2,1)S(1)}, bf16[2,1024,128]{2,1,0:T(8,128)(2,1)S(1)}, u32[]{:S(2)}, u32[]{:S(2)}) collective-permute-start(bf16[2,1024,128]{2,1,0:T(8,128)(2,1)S(1)} %copy-done.63), channel_id=1, source_target_pairs={{0,3},{1,2},{2,1},{3,0},{4,7},{5,6},{6,5},{7,4},{8,11},{9,10},{10,... | collective-permute-start | bytes 1572872 | tf_op jit(solution)/shard_map/ppermute | solution.py:231
  153.2 40.1 %collective-permute-start.27 = (bf16[2,1024,128]{2,1,0:T(8,128)(2,1)S(1)}, bf16[2,1024,128]{2,1,0:T(8,128)(2,1)}, u32[]{:S(2)}, u32[]{:S(2)}) collective-permute-start(bf16[2,1024,128]{2,1,0:T(8,128)(2,1)S(1)} %copy-done.62), channel_id=1, source_target_pairs={{0,1},{1,0},{2,3},{3,2},{4,5},{5,4},{6,7},{7,6},{8,9},{9,8},{10,11... | collective-permute-start | bytes 1572872 | tf_op jit(solution)/shard_map/ppermute | solution.py:231
  192.5 29.5 %collective-permute-start.17 = (bf16[2,1280,128]{2,1,0:T(8,128)(2,1)}, bf16[2,1280,128]{2,1,0:T(8,128)(2,1)S(1)}, u32[]{:S(2)}, u32[]{:S(2)}) collective-permute-start(bf16[2,1280,128]{2,1,0:T(8,128)(2,1)} %get-tuple-element.175), channel_id=1, source_target_pairs={{0,7},{1,6},{2,5},{3,4},{4,3},{5,2},{6,1},{7,0},{8,15},{9,14},{10,... | collective-permute-start | bytes 1966088 | tf_op jit(solution)/shard_map/ppermute | solution.py:231
  193.3 30.4 %collective-permute-start.18 = (bf16[2,1280,128]{2,1,0:T(8,128)(2,1)}, bf16[2,1280,128]{2,1,0:T(8,128)(2,1)S(1)}, u32[]{:S(2)}, u32[]{:S(2)}) collective-permute-start(bf16[2,1280,128]{2,1,0:T(8,128)(2,1)} %get-tuple-element.176), channel_id=1, source_target_pairs={{0,5},{1,4},{2,7},{3,6},{4,1},{5,0},{6,3},{7,2},{8,13},{9,12},{10,... | collective-permute-start | bytes 1966088 | tf_op jit(solution)/shard_map/ppermute | solution.py:231
  194.5 41.6 %collective-permute-start.19 = (bf16[2,1280,128]{2,1,0:T(8,128)(2,1)}, bf16[2,1280,128]{2,1,0:T(8,128)(2,1)S(1)}, u32[]{:S(2)}, u32[]{:S(2)}) collective-permute-start(bf16[2,1280,128]{2,1,0:T(8,128)(2,1)} %get-tuple-element.177), channel_id=1, source_target_pairs={{0,3},{1,2},{2,1},{3,0},{4,7},{5,6},{6,5},{7,4},{8,11},{9,10},{10,... | collective-permute-start | bytes 1966088 | tf_op jit(solution)/shard_map/ppermute | solution.py:231
  195.2 42.2 %collective-permute-start.20 = (bf16[2,1280,128]{2,1,0:T(8,128)(2,1)}, bf16[2,1280,128]{2,1,0:T(8,128)(2,1)S(1)}, u32[]{:S(2)}, u32[]{:S(2)}) collective-permute-start(bf16[2,1280,128]{2,1,0:T(8,128)(2,1)} %get-tuple-element.178), channel_id=1, source_target_pairs={{0,1},{1,0},{2,3},{3,2},{4,5},{5,4},{6,7},{7,6},{8,9},{9,8},{10,11... | collective-permute-start | bytes 1966088 | tf_op jit(solution)/shard_map/ppermute | solution.py:231
  236.1 34.6 %collective-permute-start.49 = (bf16[2,640,128]{2,1,0:T(8,128)(2,1)S(1)}, bf16[2,640,128]{2,1,0:T(8,128)(2,1)S(1)}, u32[]{:S(2)}, u32[]{:S(2)}) collective-permute-start(bf16[2,640,128]{2,1,0:T(8,128)(2,1)S(1)} %copy-done.71), channel_id=1, source_target_pairs={{0,6},{1,7},{2,4},{3,5},{4,2},{5,3},{6,0},{7,1},{8,14},{9,15},{10,... | collective-permute-start | bytes 983048 | tf_op jit(solution)/shard_map/ppermute | solution.py:231
  237.4 33.9 %collective-permute-start.50 = (bf16[2,640,128]{2,1,0:T(8,128)(2,1)S(1)}, bf16[2,640,128]{2,1,0:T(8,128)(2,1)S(1)}, u32[]{:S(2)}, u32[]{:S(2)}) collective-permute-start(bf16[2,640,128]{2,1,0:T(8,128)(2,1)S(1)} %copy-done.70), channel_id=1, source_target_pairs={{0,4},{1,5},{2,6},{3,7},{4,0},{5,1},{6,2},{7,3},{8,12},{9,13},{10,... | collective-permute-start | bytes 983048 | tf_op jit(solution)/shard_map/ppermute | solution.py:231
  276.4 40.2 %collective-permute-start.37 = (bf16[2,128,128]{2,1,0:T(8,128)(2,1)}, bf16[2,128,128]{2,1,0:T(8,128)(2,1)S(1)}, u32[]{:S(2)}, u32[]{:S(2)}) collective-permute-start(bf16[2,128,128]{2,1,0:T(8,128)(2,1)} %get-tuple-element.243), channel_id=1, source_target_pairs={{0,2},{1,3},{2,0},{3,1},{4,6},{5,7},{6,4},{7,5},{8,10},{9,11},{10,... | collective-permute-start | bytes 196616 | tf_op jit(solution)/shard_map/ppermute | solution.py:231
  281.4 35.2 %collective-permute-start.38 = (bf16[2,128,128]{2,1,0:T(8,128)(2,1)}, bf16[2,128,128]{2,1,0:T(8,128)(2,1)S(1)}, u32[]{:S(2)}, u32[]{:S(2)}) collective-permute-start(bf16[2,128,128]{2,1,0:T(8,128)(2,1)} %get-tuple-element.244), channel_id=1, source_target_pairs={{0,7},{1,6},{2,5},{3,4},{4,3},{5,2},{6,1},{7,0},{8,15},{9,14},{10,... | collective-permute-start | bytes 196616 | tf_op jit(solution)/shard_map/ppermute | solution.py:231
  286.3 30.4 %collective-permute-start.39 = (bf16[2,128,128]{2,1,0:T(8,128)(2,1)}, bf16[2,128,128]{2,1,0:T(8,128)(2,1)S(1)}, u32[]{:S(2)}, u32[]{:S(2)}) collective-permute-start(bf16[2,128,128]{2,1,0:T(8,128)(2,1)} %get-tuple-element.245), channel_id=1, source_target_pairs={{0,5},{1,4},{2,7},{3,6},{4,1},{5,0},{6,3},{7,2},{8,13},{9,12},{10,... | collective-permute-start | bytes 196616 | tf_op jit(solution)/shard_map/ppermute | solution.py:231
  288.4 28.2 %collective-permute-start.40 = (bf16[2,128,128]{2,1,0:T(8,128)(2,1)}, bf16[2,128,128]{2,1,0:T(8,128)(2,1)S(1)}, u32[]{:S(2)}, u32[]{:S(2)}) collective-permute-start(bf16[2,128,128]{2,1,0:T(8,128)(2,1)} %get-tuple-element.246), channel_id=1, source_target_pairs={{0,3},{1,2},{2,1},{3,0},{4,7},{5,6},{6,5},{7,4},{8,11},{9,10},{10,... | collective-permute-start | bytes 196616 | tf_op jit(solution)/shard_map/ppermute | solution.py:231
  (120 other events, 2487.9 us)

commit v7 on v6

--- a/solution.py
+++ b/solution.py
@@ -14,11 +14,12 @@
 PEERS = 8
 GROUP = 32
 WRAP = 256
+SMALL = 256
 CHUNKS = ((256, 512), (768, 1024), (1792, 1280), (3072, 640), (3712, 256), (3968, 128))
 BLOCK = 256
 ORDER = (6, 4, 2, 7, 5, 3, 1)
 VMEM_LIMIT = 56 * 1024 * 1024
-LAST_VMEM_LIMIT = 8 * 1024 * 1024
+SMALL_VMEM_LIMIT = 8 * 1024 * 1024
 
 
 def rotate(heads, positions):
@@ -85,11 +86,11 @@
     )(lengths, k_mine, k_mine, v_mine, v_mine)
 
 
-def interleave_kernel(first, count, block, has_own, num_alias, len_ref, new_ref, *refs):
-    num_own = 2 if has_own else 1
-    own = refs[:num_own]
-    pieces = refs[num_own:num_own + len(ORDER)]
-    k_out, v_out, held, mixed, in_sems, out_sems = refs[num_own + len(ORDER) + num_alias:]
+def interleave_kernel(first, count, block, lead, num_alias, len_ref, new_ref, *refs):
+    own = refs[:2]
+    num_pieces = len(ORDER) + lead
+    pieces = refs[2:2 + num_pieces]
+    k_out, v_out, held, mixed, in_sems, out_sems = refs[2 + num_pieces + num_alias:]
     tiles = count // block
     me = lax.axis_index('sh')
     row_len = len_ref[0]
@@ -98,12 +99,12 @@
 
     def read(tile, kv, offset):
         at = pl.multiple_of(tile * block, block)
-        if offset:
-            src = pieces[ORDER.index(offset)].at[kv, pl.ds(at, block)]
-        elif has_own:
+        if lead and offset == ORDER[0]:
+            src = pieces[kv].at[0, pl.ds(at, block)]
+        elif offset:
+            src = pieces[ORDER.index(offset) + lead].at[kv, pl.ds(at, block)]
+        else:
             src = own[kv].at[me, pl.ds(first + at, block)]
-        else:
-            src = own[0].at[kv, pl.ds(at, block)]
         return pltpu.make_async_copy(src, held.at[tile, kv, me ^ offset], in_sems.at[tile, kv, offset])
 
     def write(tile, kv):
@@ -152,6 +153,7 @@
 
 def interleave(first, row_len, new, own, pieces, caches):
     count, dim = pieces[0].shape[1:]
+    lead = len(pieces) - len(ORDER)
     block = BLOCK if count % BLOCK == 0 else BLOCK // 2
     tiles = count // block
     cache = jax.ShapeDtypeStruct((WINDOW * PEERS, dim), jnp.bfloat16)
@@ -164,7 +166,7 @@
         args += caches
         in_specs += [any_spec] * 2
     return pl.pallas_call(
-        functools.partial(interleave_kernel, first, count, block, len(own) == 2, len(aliases)),
+        functools.partial(interleave_kernel, first, count, block, lead, len(aliases)),
         out_shape=[cache, cache],
         in_specs=in_specs,
         out_specs=[any_spec] * 2,
@@ -180,7 +182,7 @@
     )(*args)
 
 
-def last_kernel(first, count, new_ref, *refs):
+def small_kernel(first, count, new_ref, *refs):
     pieces = refs[:PEERS]
     k_out, v_out, mixed, sems = refs[PEERS + 2:]
     me = lax.axis_index('sh')
@@ -207,17 +209,17 @@
         copy.wait()
 
 
-def interleave_last(first, new, pieces, caches):
+def interleave_small(first, new, pieces, caches):
     count, dim = pieces[0].shape[1:]
     cache = jax.ShapeDtypeStruct((WINDOW * PEERS, dim), jnp.bfloat16)
     return pl.pallas_call(
-        functools.partial(last_kernel, first, count),
+        functools.partial(small_kernel, first, count),
         out_shape=[cache, cache],
         in_specs=[pl.BlockSpec(memory_space=pltpu.VMEM)] * (1 + PEERS) + [pl.BlockSpec(memory_space=pltpu.HBM)] * 2,
         out_specs=[pl.BlockSpec(memory_space=pltpu.HBM)] * 2,
         input_output_aliases={1 + PEERS: 0, 2 + PEERS: 1},
         scratch_shapes=[pltpu.VMEM((2, count * PEERS, dim), jnp.bfloat16), pltpu.SemaphoreType.DMA((2,))],
-        compiler_params=pltpu.CompilerParams(vmem_limit_bytes=LAST_VMEM_LIMIT),
+        compiler_params=pltpu.CompilerParams(vmem_limit_bytes=SMALL_VMEM_LIMIT),
         cost_estimate=pl.CostEstimate(flops=count * 64 * dim, bytes_accessed=count * PEERS * dim * 8, transcendentals=0),
     )(new, *pieces, *caches)
 
@@ -253,14 +255,17 @@
             prefills = (k_mine, v_mine)
             if after is not None:
                 prefills, after = lax.optimization_barrier((prefills, after))
-            own = (0,) * (chunk == CHUNKS[-1])
+            own = (0,) * (chunk[1] <= SMALL and chunk != CHUNKS[0])
             pieces = pack(*chunk, offsets + own, *prefills)
             pieces, before = lax.optimization_barrier((pieces, before))
             send(chunk[0], pieces, offsets)
             received[chunk[0]] += pieces[len(offsets):]
             return after, before
 
-        _, residual = start(CHUNKS[0], before=residual, offsets=ORDER[:1])
+        first, count = CHUNKS[0]
+        lead = [lax.dynamic_slice(prefill, (me ^ ORDER[0], first, 0), (1, count, head_dim)) for prefill in (k_mine, v_mine)]
+        lead, residual = lax.optimization_barrier((lead, residual))
+        send(first, lead, ORDER[:1] * 2)
         _, residual = start(CHUNKS[0], after=residual, before=residual, offsets=ORDER[1:])
         _, residual = start(CHUNKS[1], after=residual, before=residual)
 
@@ -281,6 +286,7 @@
         wrap_lengths, _ = lax.optimization_barrier((lengths, table))
         wrapped = wrap_pack(wrap_lengths, k_mine, v_mine)
         send(0, wrapped[:-1])
+        received[0] += wrapped[-1:]
         qkv = by_device(qkv_parts, me).reshape(PEERS, q_group + 2, head_dim)
         q_all, k_all, v_all = qkv[:, :q_group], qkv[:, q_group:q_group + 1], qkv[:, q_group + 1:]
         positions = jnp.arange(seq_len, dtype=jnp.int32)[None, :]
@@ -303,10 +309,9 @@
         caches = None
 
         def store(first, caches):
-            own = [wrapped[-1]] if first == 0 else [k_mine, v_mine]
-            if first == CHUNKS[-1][0]:
-                return interleave_last(first, new, received[first], caches)
-            return interleave(first, place_len, new, own, received[first], caches)
+            if received[first][0].shape[1] <= SMALL:
+                return interleave_small(first, new, received[first], caches)
+            return interleave(first, place_len, new, [k_mine, v_mine], received[first], caches)
 
         caches = store(CHUNKS[0][0], caches)
         caches = store(CHUNKS[1][0], caches)

time: 321 us -> 313 us (0.975)
  waiting for transfers between devices: 150 us -> 142 us
  Pallas kernels: 53.7 us -> 48.3 us
  local copies, waits for them, and re-layouts: 3.14 us -> 6.4 us
    pallas_call x6 -> x4, Pallas kernels: 29.2 us -> 21.4 us  [interleave(): pl.pallas_call(functools.partial(interleave_kernel, first, count, block,...]
    ppermute x63 -> x64, waiting for transfers between devices: 150 us -> 142 us  [swap(): return lax.ppermute(value, 'sh', [(i, i ^ offset) for i in range(PEERS)])]
    pallas_call x1 -> x3, Pallas kernels: 1.36 us -> 5.54 us  [interleave_small(): pl.pallas_call(functools.partial(small_kernel, first, count), out_shape=[...]
    ppermute x63 -> x64, starting transfers between devices: 59 us -> 61.6 us  [swap(): return lax.ppermute(value, 'sh', [(i, i ^ offset) for i in range(PEERS)])]
    pallas_call x7 -> x6, Pallas kernels: 20.4 us -> 18.7 us  [pack(): pl.pallas_call(functools.partial(pack_kernel, first, count, offsets), out...]
  transfers between devices with their start and end apart: 63 -> 64, of which waited for: 26 -> 28; matrix products, arithmetic and copies ran while one was open for 9% -> 9% of each run, Pallas kernels for 14% -> 13%
where the time goes in v7:
time: 313 us; the launch traced here: 311 us
  waiting for transfers between devices  142 us (45%)
  starting transfers between devices  61.6 us (20%)
  Pallas kernels  48.3 us (15%)
  matrix products  46.7 us (15%)
  local copies, waits for them, and re-layouts  6.4 us (2%)
    ppermute x64, waiting for transfers between devices, swap(): return lax.ppermute(value, 'sh', [(i, i ^ offset) for i in range(PEERS)])  142 us
    ppermute x64, starting transfers between devices, swap(): return lax.ppermute(value, 'sh', [(i, i ^ offset) for i in range(PEERS)])  61.6 us
    pallas_call x4, Pallas kernels, interleave(): pl.pallas_call(functools.partial(interleave_kernel, first, count, block,...  21.4 us
    pallas_call x6, Pallas kernels, pack(): pl.pallas_call(functools.partial(pack_kernel, first, count, offsets), out...  18.7 us
    dot_general x1, matrix products, per_device(): jnp.dot(attn_out, w_out, preferred_element_type=jnp.float32)  13.5 us
    dot_general x1, matrix products, per_device(): jnp.dot(normed, w_query, preferred_element_type=jnp.float32)  12.8 us
  transfers between devices with their start and end apart: 64, of which 28 were waited for; matrix products, arithmetic and copies ran while one was open for 9% of the time, Pallas kernels for 13%

profile of v7, /device:TPU:0, one launch (start us, length us, event | category | flops | bytes accessed | tf_op | source)
XLA Modules:
  0.0 311.3 jit_solution(2233378460277381145)
XLA Ops:
  4.4 3.9 %shard_map.113 = (bf16[2,1024,128]{2,1,0:T(8,128)(2,1)}, bf16[2,1024,128]{2,1,0:T(8,128)(2,1)}, bf16[2,1024,128]{2,1,0:T(8,128)(2,1)}, bf16[2,1024,128]{2,1,0:T(...) custom-call(bf16[8,4352,128]{2,1,0:T(8,128)(2,1)} %bitcast.78, ...), custom_call_target="tpu_custom_call" | custom-call | bytes 7340032 | tf_op jit(solution)/shard_map/pallas_call | solution.py:52
  9.7 4.6 %fusion.14 = f32[1,1024]{1,0:T(1,128)S(1)} fusion(bf16[4096,1024]{1,0:T(8,128)(2,1)} %param.15, f32[1,4096]{1,0:T(1,128)S(1)} %bitcast.91, bf16[1,4096]{1,0:T(2,128)(2,1)S(1)} %copy-done.5, f32[]{:T(128)S(6)} %rsqrt.4), kind=kOutput, calls=%fused_computation.30 | convolution fusion | flops 8404992 | bytes 8417284 | tf_op jit(solution)/shard_map/dot_general | solution.py:276
  15.6 4.6 %fusion.12 = f32[1,1024]{1,0:T(1,128)S(1)} fusion(bf16[4096,1024]{1,0:T(8,128)(2,1)} %param.16, f32[1,4096]{1,0:T(1,128)S(1)} %bitcast.92, bf16[1,4096]{1,0:T(2,128)(2,1)S(1)} %copy-done.5, f32[]{:T(128)S(6)} %rsqrt.4), kind=kOutput, calls=%fused_computation.28 | convolution fusion | flops 8404992 | bytes 8417284 | tf_op jit(solution)/shard_map/dot_general | solution.py:277
  20.8 12.8 %fusion.16 = f32[1,4096]{1,0:T(1,128)S(1)} fusion(bf16[4096,4096]{1,0:T(8,128)(2,1)} %param.14, f32[1,4096]{1,0:T(1,128)S(1)} %bitcast.93, bf16[1,4096]{1,0:T(2,128)(2,1)S(1)} %copy-done.5, f32[]{:T(128)S(6)} %rsqrt.4), kind=kOutput, calls=%fused_computation.32 | convolution fusion | flops 33570816 | bytes 33595396 | tf_op jit(solution)/shard_map/dot_general | solution.py:275
  51.9 6.0 %fusion.32 = (f32[8,4]{1,0:T(8,128)S(1)}, f32[8,4,4352]{2,1,0:T(4,128)S(1)}) fusion(bf16[8,4352,1,128]{3,1,2,0:T(8,128)(2,1)} %param.9, bf16[8,6,128]{2,1,0:T(8,128)(2,1)S(1)} %copy_select_fusion, pred[8,4352]{1,0:T(8,128)(4,1)S(1)} %fusion.7), kind=kOutput, calls=%fused_computation.93 | convolution fusion | flops 36069344 | bytes 9513088 | tf_op jit(solution)/shard_map/bgd,bsd->bgs/dot_general | solution.py:294
  58.4 5.2 %fusion.3 = bf16[1,8,4,128]{3,2,1,0:T(4,128)(2,1)S(1)} fusion(f32[8,4,4352]{2,1,0:T(4,128)S(1)} %get-tuple-element.314, f32[8,4]{1,0:T(8,128)S(1)} %get-tuple-element.290, f32[8,4]{1,0:T(8,128)S(1)} %multiply_maximum_fusion, f32[8,128]{1,0:T(8,128)S(1)} %bitcast.95, f32[8,4]{1,0:T(8,128)S(1)} %get-tuple-element.289, bf16[8,4352,1,128]{3,1,2,0:T(8,128)(2,1)} %param.10), kind=kOutput, calls=%fused_computation.8 | convolution fusion | flops 36081664 | bytes 9482624 | tf_op jit(solution)/shard_map/bgs,bsd->bgd/dot_general | solution.py:304
  75.3 3.9 %collective-permute-done.13 = bf16[1,512]{1,0:T(2,128)(2,1)S(1)} collective-permute-done((bf16[1,512]{1,0:T(2,128)(2,1)S(1)}, bf16[1,512]{1,0:T(2,128)(2,1)S(1)}, u32[]{:S(2)}, u32[]{:S(2)}) %collective-permute-start.13) | collective-permute-done | bytes 1056 | tf_op jit(solution)/shard_map/ppermute | solution.py:233
  101.2 3.5 %collective-permute-done.30.refs_4_ = bf16[2,512,128]{2,1,0:T(8,128)(2,1)} collective-permute-done((bf16[2,512,128]{2,1,0:T(8,128)(2,1)S(1)}, bf16[2,512,128]{2,1,0:T(8,128)(2,1)}, u32[]{:S(2)}, u32[]{:S(2)}) %collective-permute-start.30) | collective-permute-done | bytes 262176 | tf_op jit(solution)/shard_map/ppermute | solution.py:233
  110.6 3.6 %collective-permute-done.33.refs_7_ = bf16[2,512,128]{2,1,0:T(8,128)(2,1)S(1)} collective-permute-done((bf16[2,512,128]{2,1,0:T(8,128)(2,1)S(1)}, bf16[2,512,128]{2,1,0:T(8,128)(2,1)S(1)}, u32[]{:S(2)}, u32[]{:S(2)}) %collective-permute-start.33) | collective-permute-done | bytes 262176 | tf_op jit(solution)/shard_map/ppermute | solution.py:233
  117.5 4.5 %shard_map.114 = (bf16[2,1280,128]{2,1,0:T(8,128)(2,1)}, bf16[2,1280,128]{2,1,0:T(8,128)(2,1)}, bf16[2,1280,128]{2,1,0:T(8,128)(2,1)}, bf16[2,1280,128]{2,1,0:T(...) custom-call(bf16[8,4352,128]{2,1,0:T(8,128)(2,1)} %bitcast.81, ...), custom_call_target="tpu_custom_call" | custom-call | bytes 9175040 | tf_op jit(solution)/shard_map/pallas_call | solution.py:52
  123.8 3.3 %collective-permute-done.21.refs_2_ = bf16[2,1024,128]{2,1,0:T(8,128)(2,1)S(1)} collective-permute-done((bf16[2,1024,128]{2,1,0:T(8,128)(2,1)S(1)}, bf16[2,1024,128]{2,1,0:T(8,128)(2,1)S(1)}, u32[]{:S(2)}, u32[]{:S(2)}) %collective-permute-start.21) | collective-permute-done | bytes 524320 | tf_op jit(solution)/shard_map/ppermute | solution.py:233
  127.5 10.7 %collective-permute-done.22.refs_3_ = bf16[2,1024,128]{2,1,0:T(8,128)(2,1)S(1)} collective-permute-done((bf16[2,1024,128]{2,1,0:T(8,128)(2,1)S(1)}, bf16[2,1024,128]{2,1,0:T(8,128)(2,1)S(1)}, u32[]{:S(2)}, u32[]{:S(2)}) %collective-permute-start.22) | collective-permute-done | bytes 524320 | tf_op jit(solution)/shard_map/ppermute | solution.py:233
  139.7 9.3 %collective-permute-done.24.refs_5_ = bf16[2,1024,128]{2,1,0:T(8,128)(2,1)S(1)} collective-permute-done((bf16[2,1024,128]{2,1,0:T(8,128)(2,1)S(1)}, bf16[2,1024,128]{2,1,0:T(8,128)(2,1)S(1)}, u32[]{:S(2)}, u32[]{:S(2)}) %collective-permute-start.24) | collective-permute-done | bytes 524320 | tf_op jit(solution)/shard_map/ppermute | solution.py:233
  149.5 37.7 %collective-permute-done.25.refs_6_ = bf16[2,1024,128]{2,1,0:T(8,128)(2,1)S(1)} collective-permute-done((bf16[2,1024,128]{2,1,0:T(8,128)(2,1)S(1)}, bf16[2,1024,128]{2,1,0:T(8,128)(2,1)S(1)}, u32[]{:S(2)}, u32[]{:S(2)}) %collective-permute-start.25) | collective-permute-done | bytes 524320 | tf_op jit(solution)/shard_map/ppermute | solution.py:233
  193.4 4.6 %shard_map.115 = (bf16[32768,128]{1,0:T(8,128)(2,1)}, bf16[32768,128]{1,0:T(8,128)(2,1)}) custom-call(s32[1]{0:T(128)} %dynamic_slice.65.len_ref, f32[3,8,128]{2,1,0:T(8,128)} %maximum_maximum_fusion.new_ref, bf16[8,4352,128]{2,1,0:T(8,128)(2,1)} %bitcast.82, bf16[8,4352,128]{2,1,0:T(8,128)(2,1)} %bitcast.70, bf16[1,512,128]{2,1,0:T(8,128)(2,1)} %copy-done.24, ...), custom_call_target="tpu_custom_call" | custom-call | flops 4194304 | bytes 4194304 | tf_op jit(solution)/shard_map/pallas_call | solution.py:168
  198.1 5.3 %shard_map.116 = (bf16[32768,128]{1,0:T(8,128)(2,1)}, bf16[32768,128]{1,0:T(8,128)(2,1)}) custom-call(s32[1]{0:T(128)} %dynamic_slice.65.len_ref, f32[3,8,128]{2,1,0:T(8,128)} %maximum_maximum_fusion.new_ref, bf16[8,4352,128]{2,1,0:T(8,128)(2,1)} %bitcast.83, bf16[8,4352,128]{2,1,0:T(8,128)(2,1)} %bitcast.71, ...), custom_call_target="tpu_custom_call", output_to_operand_aliasing={{0}: (11, {}), {1}: (12, {})} | custom-call | flops 8388608 | bytes 8388608 | tf_op jit(solution)/shard_map/pallas_call | solution.py:168
  210.0 8.7 %collective-permute-done.17.refs_5_ = bf16[2,1280,128]{2,1,0:T(8,128)(2,1)S(1)} collective-permute-done((bf16[2,1280,128]{2,1,0:T(8,128)(2,1)}, bf16[2,1280,128]{2,1,0:T(8,128)(2,1)S(1)}, u32[]{:S(2)}, u32[]{:S(2)}) %collective-permute-start.17) | collective-permute-done | bytes 655392 | tf_op jit(solution)/shard_map/ppermute | solution.py:233
  221.2 11.6 %collective-permute-done.19.refs_7_ = bf16[2,1280,128]{2,1,0:T(8,128)(2,1)S(1)} collective-permute-done((bf16[2,1280,128]{2,1,0:T(8,128)(2,1)}, bf16[2,1280,128]{2,1,0:T(8,128)(2,1)S(1)}, u32[]{:S(2)}, u32[]{:S(2)}) %collective-permute-start.19) | collective-permute-done | bytes 655392 | tf_op jit(solution)/shard_map/ppermute | solution.py:233
  239.2 9.0 %collective-permute-done.46.refs_3_ = bf16[2,256,128]{2,1,0:T(8,128)(2,1)S(1)} collective-permute-done((bf16[2,256,128]{2,1,0:T(8,128)(2,1)}, bf16[2,256,128]{2,1,0:T(8,128)(2,1)S(1)}, u32[]{:S(2)}, u32[]{:S(2)}) %collective-permute-start.46) | collective-permute-done | bytes 131104 | tf_op jit(solution)/shard_map/ppermute | solution.py:233
  249.8 6.6 %shard_map.119 = (bf16[32768,128]{1,0:T(8,128)(2,1)}, bf16[32768,128]{1,0:T(8,128)(2,1)}) custom-call(s32[1]{0:T(128)} %dynamic_slice.65.len_ref, f32[3,8,128]{2,1,0:T(8,128)} %maximum_maximum_fusion.new_ref, bf16[8,4352,128]{2,1,0:T(8,128)(2,1)} %bitcast.86, bf16[8,4352,128]{2,1,0:T(8,128)(2,1)} %bitcast.74, ...), custom_call_target="tpu_custom_call", output_to_operand_aliasing={{0}: (11, {}), {1}: (12, {})} | custom-call | flops 10485760 | bytes 10485760 | tf_op jit(solution)/shard_map/pallas_call | solution.py:168
  269.0 4.0 %collective-permute-done.52.refs_4_ = bf16[2,640,128]{2,1,0:T(8,128)(2,1)S(1)} collective-permute-done((bf16[2,640,128]{2,1,0:T(8,128)(2,1)}, bf16[2,640,128]{2,1,0:T(8,128)(2,1)S(1)}, u32[]{:S(2)}, u32[]{:S(2)}) %collective-permute-start.52) | collective-permute-done | bytes 327712 | tf_op jit(solution)/shard_map/ppermute | solution.py:233
  273.0 4.9 %collective-permute-done.53.refs_5_ = bf16[2,640,128]{2,1,0:T(8,128)(2,1)S(1)} collective-permute-done((bf16[2,640,128]{2,1,0:T(8,128)(2,1)}, bf16[2,640,128]{2,1,0:T(8,128)(2,1)S(1)}, u32[]{:S(2)}, u32[]{:S(2)}) %collective-permute-start.53) | collective-permute-done | bytes 327712 | tf_op jit(solution)/shard_map/ppermute | solution.py:233
  287.1 13.5 %fusion.1 = bf16[1,4096]{1,0:T(2,128)(2,1)} fusion(bf16[4096,1]{0,1:T(2,128)(2,1)S(1)} %bitcast.96, bf16[4096,4096]{1,0:T(8,128)(2,1)} %param.17, bf16[1,4096]{1,0:T(2,128)(2,1)S(1)} %copy-done.5), kind=kOutput, calls=%fused_computation.5 | convolution fusion | flops 33566720 | bytes 33579008 | tf_op jit(solution)/shard_map/dot_general | solution.py:324
  302.7 4.8 %shard_map.123 = (bf16[32768,128]{1,0:T(8,128)(2,1)}, bf16[32768,128]{1,0:T(8,128)(2,1)}) custom-call(s32[1]{0:T(128)} %dynamic_slice.65.len_ref, f32[3,8,128]{2,1,0:T(8,128)} %maximum_maximum_fusion.new_ref, bf16[8,4352,128]{2,1,0:T(8,128)(2,1)} %bitcast.88, bf16[8,4352,128]{2,1,0:T(8,128)(2,1)} %bitcast.76, ...), custom_call_target="tpu_custom_call", output_to_operand_aliasing={{0}: (11, {}), {1}: (12, {})} | custom-call | flops 5242880 | bytes 5242880 | tf_op jit(solution)/shard_map/pallas_call | solution.py:168
  (304 shorter events, 121.3 us)
Async XLA Ops:
  45.0 42.5 %collective-permute-start.28 = (bf16[1,512,128]{2,1,0:T(8,128)(2,1)S(1)}, bf16[1,512,128]{2,1,0:T(8,128)(2,1)S(1)}, u32[]{:S(2)}, u32[]{:S(2)}) collective-permute-start(bf16[1,512,128]{2,1,0:T(8,128)(2,1)S(1)} %get-tuple-element.189), channel_id=1, source_target_pairs={{0,6},{1,7},{2,4},{3,5},{4,2},{5,3},{6,0},{7,1},{8,14},{9,15},{10,... | collective-permute-start | bytes 393224 | tf_op jit(solution)/shard_map/ppermute | solution.py:233
  47.6 41.4 %collective-permute-start.29 = (bf16[1,512,128]{2,1,0:T(8,128)(2,1)S(1)}, bf16[1,512,128]{2,1,0:T(8,128)(2,1)S(1)}, u32[]{:S(2)}, u32[]{:S(2)}) collective-permute-start(bf16[1,512,128]{2,1,0:T(8,128)(2,1)S(1)} %get-tuple-element.190), channel_id=1, source_target_pairs={{0,6},{1,7},{2,4},{3,5},{4,2},{5,3},{6,0},{7,1},{8,14},{9,15},{10,... | collective-permute-start | bytes 393224 | tf_op jit(solution)/shard_map/ppermute | solution.py:233
  48.0 43.6 %collective-permute-start.57 = (bf16[2,256,128]{2,1,0:T(8,128)(2,1)}, bf16[2,256,128]{2,1,0:T(8,128)(2,1)S(1)}, u32[]{:S(2)}, u32[]{:S(2)}) collective-permute-start(bf16[2,256,128]{2,1,0:T(8,128)(2,1)} %get-tuple-element.269), channel_id=1, source_target_pairs={{0,6},{1,7},{2,4},{3,5},{4,2},{5,3},{6,0},{7,1},{8,14},{9,15},{10,... | collective-permute-start | bytes 393224 | tf_op jit(solution)/shard_map/ppermute | solution.py:233
  50.5 41.1 %collective-permute-start.58 = (bf16[2,256,128]{2,1,0:T(8,128)(2,1)}, bf16[2,256,128]{2,1,0:T(8,128)(2,1)S(1)}, u32[]{:S(2)}, u32[]{:S(2)}) collective-permute-start(bf16[2,256,128]{2,1,0:T(8,128)(2,1)} %get-tuple-element.270), channel_id=1, source_target_pairs={{0,4},{1,5},{2,6},{3,7},{4,0},{5,1},{6,2},{7,3},{8,12},{9,13},{10,... | collective-permute-start | bytes 393224 | tf_op jit(solution)/shard_map/ppermute | solution.py:233
  105.9 32.4 %collective-permute-start.22 = (bf16[2,1024,128]{2,1,0:T(8,128)(2,1)S(1)}, bf16[2,1024,128]{2,1,0:T(8,128)(2,1)S(1)}, u32[]{:S(2)}, u32[]{:S(2)}) collective-permute-start(bf16[2,1024,128]{2,1,0:T(8,128)(2,1)S(1)} %copy-done.56), channel_id=1, source_target_pairs={{0,4},{1,5},{2,6},{3,7},{4,0},{5,1},{6,2},{7,3},{8,12},{9,13},{10,... | collective-permute-start | bytes 1572872 | tf_op jit(solution)/shard_map/ppermute | solution.py:233
  109.6 28.6 %collective-permute-start.23 = (bf16[2,1024,128]{2,1,0:T(8,128)(2,1)S(1)}, bf16[2,1024,128]{2,1,0:T(8,128)(2,1)S(1)}, u32[]{:S(2)}, u32[]{:S(2)}) collective-permute-start(bf16[2,1024,128]{2,1,0:T(8,128)(2,1)S(1)} %copy-done.55), channel_id=1, source_target_pairs={{0,2},{1,3},{2,0},{3,1},{4,6},{5,7},{6,4},{7,5},{8,10},{9,11},{10,... | collective-permute-start | bytes 1572872 | tf_op jit(solution)/shard_map/ppermute | solution.py:233
  114.9 34.1 %collective-permute-start.24 = (bf16[2,1024,128]{2,1,0:T(8,128)(2,1)S(1)}, bf16[2,1024,128]{2,1,0:T(8,128)(2,1)S(1)}, u32[]{:S(2)}, u32[]{:S(2)}) collective-permute-start(bf16[2,1024,128]{2,1,0:T(8,128)(2,1)S(1)} %copy-done.54), channel_id=1, source_target_pairs={{0,7},{1,6},{2,5},{3,4},{4,3},{5,2},{6,1},{7,0},{8,15},{9,14},{10,... | collective-permute-start | bytes 1572872 | tf_op jit(solution)/shard_map/ppermute | solution.py:233
  122.1 68.4 %collective-permute-start.14 = (bf16[2,1280,128]{2,1,0:T(8,128)(2,1)}, bf16[2,1280,128]{2,1,0:T(8,128)(2,1)S(1)}, u32[]{:S(2)}, u32[]{:S(2)}) collective-permute-start(bf16[2,1280,128]{2,1,0:T(8,128)(2,1)} %get-tuple-element.175), channel_id=1, source_target_pairs={{0,6},{1,7},{2,4},{3,5},{4,2},{5,3},{6,0},{7,1},{8,14},{9,15},{10,... | collective-permute-start | bytes 1966088 | tf_op jit(solution)/shard_map/ppermute | solution.py:233
  127.1 64.8 %collective-permute-start.15 = (bf16[2,1280,128]{2,1,0:T(8,128)(2,1)}, bf16[2,1280,128]{2,1,0:T(8,128)(2,1)S(1)}, u32[]{:S(2)}, u32[]{:S(2)}) collective-permute-start(bf16[2,1280,128]{2,1,0:T(8,128)(2,1)} %get-tuple-element.176), channel_id=1, source_target_pairs={{0,4},{1,5},{2,6},{3,7},{4,0},{5,1},{6,2},{7,3},{8,12},{9,13},{10,... | collective-permute-start | bytes 1966088 | tf_op jit(solution)/shard_map/ppermute | solution.py:233
  138.2 49.0 %collective-permute-start.25 = (bf16[2,1024,128]{2,1,0:T(8,128)(2,1)S(1)}, bf16[2,1024,128]{2,1,0:T(8,128)(2,1)S(1)}, u32[]{:S(2)}, u32[]{:S(2)}) collective-permute-start(bf16[2,1024,128]{2,1,0:T(8,128)(2,1)S(1)} %copy-done.53), channel_id=1, source_target_pairs={{0,5},{1,4},{2,7},{3,6},{4,1},{5,0},{6,3},{7,2},{8,13},{9,12},{10,... | collective-permute-start | bytes 1572872 | tf_op jit(solution)/shard_map/ppermute | solution.py:233
  138.3 50.9 %collective-permute-start.26 = (bf16[2,1024,128]{2,1,0:T(8,128)(2,1)S(1)}, bf16[2,1024,128]{2,1,0:T(8,128)(2,1)}, u32[]{:S(2)}, u32[]{:S(2)}) collective-permute-start(bf16[2,1024,128]{2,1,0:T(8,128)(2,1)S(1)} %copy-done.52), channel_id=1, source_target_pairs={{0,3},{1,2},{2,1},{3,0},{4,7},{5,6},{6,5},{7,4},{8,11},{9,10},{10,... | collective-permute-start | bytes 1572872 | tf_op jit(solution)/shard_map/ppermute | solution.py:233
  149.0 40.9 %collective-permute-start.27 = (bf16[2,1024,128]{2,1,0:T(8,128)(2,1)S(1)}, bf16[2,1024,128]{2,1,0:T(8,128)(2,1)}, u32[]{:S(2)}, u32[]{:S(2)}) collective-permute-start(bf16[2,1024,128]{2,1,0:T(8,128)(2,1)S(1)} %copy-done.51), channel_id=1, source_target_pairs={{0,1},{1,0},{2,3},{3,2},{4,5},{5,4},{6,7},{7,6},{8,9},{9,8},{10,11... | collective-permute-start | bytes 1572872 | tf_op jit(solution)/shard_map/ppermute | solution.py:233
  189.2 29.5 %collective-permute-start.17 = (bf16[2,1280,128]{2,1,0:T(8,128)(2,1)}, bf16[2,1280,128]{2,1,0:T(8,128)(2,1)S(1)}, u32[]{:S(2)}, u32[]{:S(2)}) collective-permute-start(bf16[2,1280,128]{2,1,0:T(8,128)(2,1)} %get-tuple-element.178), channel_id=1, source_target_pairs={{0,7},{1,6},{2,5},{3,4},{4,3},{5,2},{6,1},{7,0},{8,15},{9,14},{10,... | collective-permute-start | bytes 1966088 | tf_op jit(solution)/shard_map/ppermute | solution.py:233
  189.9 30.4 %collective-permute-start.18 = (bf16[2,1280,128]{2,1,0:T(8,128)(2,1)}, bf16[2,1280,128]{2,1,0:T(8,128)(2,1)S(1)}, u32[]{:S(2)}, u32[]{:S(2)}) collective-permute-start(bf16[2,1280,128]{2,1,0:T(8,128)(2,1)} %get-tuple-element.179), channel_id=1, source_target_pairs={{0,5},{1,4},{2,7},{3,6},{4,1},{5,0},{6,3},{7,2},{8,13},{9,12},{10,... | collective-permute-start | bytes 1966088 | tf_op jit(solution)/shard_map/ppermute | solution.py:233
  190.5 42.3 %collective-permute-start.19 = (bf16[2,1280,128]{2,1,0:T(8,128)(2,1)}, bf16[2,1280,128]{2,1,0:T(8,128)(2,1)S(1)}, u32[]{:S(2)}, u32[]{:S(2)}) collective-permute-start(bf16[2,1280,128]{2,1,0:T(8,128)(2,1)} %get-tuple-element.180), channel_id=1, source_target_pairs={{0,3},{1,2},{2,1},{3,0},{4,7},{5,6},{6,5},{7,4},{8,11},{9,10},{10,... | collective-permute-start | bytes 1966088 | tf_op jit(solution)/shard_map/ppermute | solution.py:233
  191.9 42.2 %collective-permute-start.20 = (bf16[2,1280,128]{2,1,0:T(8,128)(2,1)}, bf16[2,1280,128]{2,1,0:T(8,128)(2,1)S(1)}, u32[]{:S(2)}, u32[]{:S(2)}) collective-permute-start(bf16[2,1280,128]{2,1,0:T(8,128)(2,1)} %get-tuple-element.181), channel_id=1, source_target_pairs={{0,1},{1,0},{2,3},{3,2},{4,5},{5,4},{6,7},{7,6},{8,9},{9,8},{10,11... | collective-permute-start | bytes 1966088 | tf_op jit(solution)/shard_map/ppermute | solution.py:233
  209.1 28.1 %collective-permute-start.43 = (bf16[2,256,128]{2,1,0:T(8,128)(2,1)}, bf16[2,256,128]{2,1,0:T(8,128)(2,1)S(1)}, u32[]{:S(2)}, u32[]{:S(2)}) collective-permute-start(bf16[2,256,128]{2,1,0:T(8,128)(2,1)} %get-tuple-element.254), channel_id=1, source_target_pairs={{0,6},{1,7},{2,4},{3,5},{4,2},{5,3},{6,0},{7,1},{8,14},{9,15},{10,... | collective-permute-start | bytes 393224 | tf_op jit(solution)/shard_map/ppermute | solution.py:233
  232.8 35.2 %collective-permute-start.50 = (bf16[2,640,128]{2,1,0:T(8,128)(2,1)S(1)}, bf16[2,640,128]{2,1,0:T(8,128)(2,1)S(1)}, u32[]{:S(2)}, u32[]{:S(2)}) collective-permute-start(bf16[2,640,128]{2,1,0:T(8,128)(2,1)S(1)} %copy-done.59), channel_id=1, source_target_pairs={{0,6},{1,7},{2,4},{3,5},{4,2},{5,3},{6,0},{7,1},{8,14},{9,15},{10,... | collective-permute-start | bytes 983048 | tf_op jit(solution)/shard_map/ppermute | solution.py:233
  234.1 33.9 %collective-permute-start.51 = (bf16[2,640,128]{2,1,0:T(8,128)(2,1)S(1)}, bf16[2,640,128]{2,1,0:T(8,128)(2,1)S(1)}, u32[]{:S(2)}, u32[]{:S(2)}) collective-permute-start(bf16[2,640,128]{2,1,0:T(8,128)(2,1)S(1)} %copy-done.58), channel_id=1, source_target_pairs={{0,4},{1,5},{2,6},{3,7},{4,0},{5,1},{6,2},{7,3},{8,12},{9,13},{10,... | collective-permute-start | bytes 983048 | tf_op jit(solution)/shard_map/ppermute | solution.py:233
  273.0 36.6 %collective-permute-start.38 = (bf16[2,128,128]{2,1,0:T(8,128)(2,1)}, bf16[2,128,128]{2,1,0:T(8,128)(2,1)S(1)}, u32[]{:S(2)}, u32[]{:S(2)}) collective-permute-start(bf16[2,128,128]{2,1,0:T(8,128)(2,1)} %get-tuple-element.248), channel_id=1, source_target_pairs={{0,2},{1,3},{2,0},{3,1},{4,6},{5,7},{6,4},{7,5},{8,10},{9,11},{10,... | collective-permute-start | bytes 196616 | tf_op jit(solution)/shard_map/ppermute | solution.py:233
  278.0 31.7 %collective-permute-start.39 = (bf16[2,128,128]{2,1,0:T(8,128)(2,1)}, bf16[2,128,128]{2,1,0:T(8,128)(2,1)S(1)}, u32[]{:S(2)}, u32[]{:S(2)}) collective-permute-start(bf16[2,128,128]{2,1,0:T(8,128)(2,1)} %get-tuple-element.249), channel_id=1, source_target_pairs={{0,7},{1,6},{2,5},{3,4},{4,3},{5,2},{6,1},{7,0},{8,15},{9,14},{10,... | collective-permute-start | bytes 196616 | tf_op jit(solution)/shard_map/ppermute | solution.py:233
  283.2 26.4 %collective-permute-start.40 = (bf16[2,128,128]{2,1,0:T(8,128)(2,1)}, bf16[2,128,128]{2,1,0:T(8,128)(2,1)S(1)}, u32[]{:S(2)}, u32[]{:S(2)}) collective-permute-start(bf16[2,128,128]{2,1,0:T(8,128)(2,1)} %get-tuple-element.250), channel_id=1, source_target_pairs={{0,5},{1,4},{2,7},{3,6},{4,1},{5,0},{6,3},{7,2},{8,13},{9,12},{10,... | collective-permute-start | bytes 196616 | tf_op jit(solution)/shard_map/ppermute | solution.py:233
  284.7 25.0 %collective-permute-start.41 = (bf16[2,128,128]{2,1,0:T(8,128)(2,1)}, bf16[2,128,128]{2,1,0:T(8,128)(2,1)S(1)}, u32[]{:S(2)}, u32[]{:S(2)}) collective-permute-start(bf16[2,128,128]{2,1,0:T(8,128)(2,1)} %get-tuple-element.251), channel_id=1, source_target_pairs={{0,3},{1,2},{2,1},{3,0},{4,7},{5,6},{6,5},{7,4},{8,11},{9,10},{10,... | collective-permute-start | bytes 196616 | tf_op jit(solution)/shard_map/ppermute | solution.py:233
  286.6 23.1 %collective-permute-start.42 = (bf16[2,128,128]{2,1,0:T(8,128)(2,1)}, bf16[2,128,128]{2,1,0:T(8,128)(2,1)S(1)}, u32[]{:S(2)}, u32[]{:S(2)}) collective-permute-start(bf16[2,128,128]{2,1,0:T(8,128)(2,1)} %get-tuple-element.252), channel_id=1, source_target_pairs={{0,1},{1,0},{2,3},{3,2},{4,5},{5,4},{6,7},{7,6},{8,9},{9,8},{10,11... | collective-permute-start | bytes 196616 | tf_op jit(solution)/shard_map/ppermute | solution.py:233
  (111 other events, 2368.8 us)

commit v8 on v7

--- a/solution.py
+++ b/solution.py
@@ -15,7 +15,7 @@
 GROUP = 32
 WRAP = 256
 SMALL = 256
-CHUNKS = ((256, 512), (768, 1024), (1792, 1280), (3072, 640), (3712, 256), (3968, 128))
+CHUNKS = ((256, 512), (768, 1024), (1792, 1280), (3072, 768), (3840, 192), (4032, 64))
 BLOCK = 256
 ORDER = (6, 4, 2, 7, 5, 3, 1)
 VMEM_LIMIT = 56 * 1024 * 1024
@@ -86,11 +86,10 @@
     )(lengths, k_mine, k_mine, v_mine, v_mine)
 
 
-def interleave_kernel(first, count, block, lead, num_alias, len_ref, new_ref, *refs):
+def interleave_kernel(first, count, block, num_alias, len_ref, new_ref, *refs):
     own = refs[:2]
-    num_pieces = len(ORDER) + lead
-    pieces = refs[2:2 + num_pieces]
-    k_out, v_out, held, mixed, in_sems, out_sems = refs[2 + num_pieces + num_alias:]
+    pieces = refs[2:2 + len(ORDER)]
+    k_out, v_out, held, mixed, in_sems, out_sems = refs[2 + len(ORDER) + num_alias:]
     tiles = count // block
     me = lax.axis_index('sh')
     row_len = len_ref[0]
@@ -99,10 +98,8 @@
 
     def read(tile, kv, offset):
         at = pl.multiple_of(tile * block, block)
-        if lead and offset == ORDER[0]:
-            src = pieces[kv].at[0, pl.ds(at, block)]
-        elif offset:
-            src = pieces[ORDER.index(offset) + lead].at[kv, pl.ds(at, block)]
+        if offset:
+            src = pieces[ORDER.index(offset)].at[kv, pl.ds(at, block)]
         else:
             src = own[kv].at[me, pl.ds(first + at, block)]
         return pltpu.make_async_copy(src, held.at[tile, kv, me ^ offset], in_sems.at[tile, kv, offset])
@@ -153,7 +150,6 @@
 
 def interleave(first, row_len, new, own, pieces, caches):
     count, dim = pieces[0].shape[1:]
-    lead = len(pieces) - len(ORDER)
     block = BLOCK if count % BLOCK == 0 else BLOCK // 2
     tiles = count // block
     cache = jax.ShapeDtypeStruct((WINDOW * PEERS, dim), jnp.bfloat16)
@@ -166,7 +162,7 @@
         args += caches
         in_specs += [any_spec] * 2
     return pl.pallas_call(
-        functools.partial(interleave_kernel, first, count, block, lead, len(aliases)),
+        functools.partial(interleave_kernel, first, count, block, len(aliases)),
         out_shape=[cache, cache],
         in_specs=in_specs,
         out_specs=[any_spec] * 2,
@@ -262,10 +258,7 @@
             received[chunk[0]] += pieces[len(offsets):]
             return after, before
 
-        first, count = CHUNKS[0]
-        lead = [lax.dynamic_slice(prefill, (me ^ ORDER[0], first, 0), (1, count, head_dim)) for prefill in (k_mine, v_mine)]
-        lead, residual = lax.optimization_barrier((lead, residual))
-        send(first, lead, ORDER[:1] * 2)
+        _, residual = start(CHUNKS[0], before=residual, offsets=ORDER[:1])
         _, residual = start(CHUNKS[0], after=residual, before=residual, offsets=ORDER[1:])
         _, residual = start(CHUNKS[1], after=residual, before=residual)
 
@@ -309,7 +302,7 @@
         caches = None
 
         def store(first, caches):
-            if received[first][0].shape[1] <= SMALL:
+            if len(received[first]) == PEERS:
                 return interleave_small(first, new, received[first], caches)
             return interleave(first, place_len, new, [k_mine, v_mine], received[first], caches)
 

time: 313 us -> 310 us (level)
  waiting for transfers between devices: 142 us -> 128 us
  starting transfers between devices: 61.6 us -> 75.5 us
  local copies, waits for them, and re-layouts: 6.4 us -> 3.02 us
    ppermute x64 -> x63, waiting for transfers between devices: 142 us -> 128 us  [swap(): return lax.ppermute(value, 'sh', [(i, i ^ offset) for i in range(PEERS)])]
    ppermute x64 -> x63, starting transfers between devices: 61.6 us -> 75.5 us  [swap(): return lax.ppermute(value, 'sh', [(i, i ^ offset) for i in range(PEERS)])]
    pallas_call x6 -> x7, Pallas kernels: 18.7 us -> 20.6 us  [pack(): pl.pallas_call(functools.partial(pack_kernel, first, count, offsets), out...]
  transfers between devices with their start and end apart: 64 -> 63, of which waited for: 28 -> 27; matrix products, arithmetic and copies ran while one was open for 9% -> 9% of each run, Pallas kernels for 13% -> 13%
where the time goes in v8:
time: 310 us; the launch traced here: 308 us
  waiting for transfers between devices  128 us (41%)
  starting transfers between devices  75.5 us (24%)
  Pallas kernels  49.6 us (16%)
  matrix products  46.7 us (15%)
    ppermute x63, waiting for transfers between devices, swap(): return lax.ppermute(value, 'sh', [(i, i ^ offset) for i in range(PEERS)])  128 us
    ppermute x63, starting transfers between devices, swap(): return lax.ppermute(value, 'sh', [(i, i ^ offset) for i in range(PEERS)])  75.5 us
    pallas_call x4, Pallas kernels, interleave(): pl.pallas_call(functools.partial(interleave_kernel, first, count, block,...  21.5 us
    pallas_call x7, Pallas kernels, pack(): pl.pallas_call(functools.partial(pack_kernel, first, count, offsets), out...  20.6 us
    dot_general x1, matrix products, per_device(): jnp.dot(attn_out, w_out, preferred_element_type=jnp.float32)  13.5 us
    dot_general x1, matrix products, per_device(): jnp.dot(normed, w_query, preferred_element_type=jnp.float32)  12.9 us
  transfers between devices with their start and end apart: 63, of which 27 were waited for; matrix products, arithmetic and copies ran while one was open for 9% of the time, Pallas kernels for 13%

profile of v8, /device:TPU:0, one launch (start us, length us, event | category | flops | bytes accessed | tf_op | source)
XLA Modules:
  0.0 307.9 jit_solution(9678967948119368524)
XLA Ops:
  5.2 3.9 %shard_map.114 = (bf16[2,1024,128]{2,1,0:T(8,128)(2,1)}, bf16[2,1024,128]{2,1,0:T(8,128)(2,1)}, bf16[2,1024,128]{2,1,0:T(8,128)(2,1)}, bf16[2,1024,128]{2,1,0:T(...) custom-call(bf16[8,4352,128]{2,1,0:T(8,128)(2,1)} %bitcast.76, ...), custom_call_target="tpu_custom_call" | custom-call | bytes 7340032 | tf_op jit(solution)/shard_map/pallas_call | solution.py:52
  10.5 4.6 %fusion.14 = f32[1,1024]{1,0:T(1,128)S(1)} fusion(bf16[4096,1024]{1,0:T(8,128)(2,1)} %param.15, f32[1,4096]{1,0:T(1,128)S(1)} %bitcast.89, bf16[1,4096]{1,0:T(2,128)(2,1)S(1)} %copy-done.5, f32[]{:T(128)S(6)} %rsqrt.4), kind=kOutput, calls=%fused_computation.28 | convolution fusion | flops 8404992 | bytes 8417284 | tf_op jit(solution)/shard_map/dot_general | solution.py:269
  16.3 4.6 %fusion.12 = f32[1,1024]{1,0:T(1,128)S(1)} fusion(bf16[4096,1024]{1,0:T(8,128)(2,1)} %param.16, f32[1,4096]{1,0:T(1,128)S(1)} %bitcast.90, bf16[1,4096]{1,0:T(2,128)(2,1)S(1)} %copy-done.5, f32[]{:T(128)S(6)} %rsqrt.4), kind=kOutput, calls=%fused_computation.26 | convolution fusion | flops 8404992 | bytes 8417284 | tf_op jit(solution)/shard_map/dot_general | solution.py:270
  20.9 12.9 %fusion.16 = f32[1,4096]{1,0:T(1,128)S(1)} fusion(bf16[4096,4096]{1,0:T(8,128)(2,1)} %param.14, f32[1,4096]{1,0:T(1,128)S(1)} %bitcast.91, bf16[1,4096]{1,0:T(2,128)(2,1)S(1)} %copy-done.5, f32[]{:T(128)S(6)} %rsqrt.4), kind=kOutput, calls=%fused_computation.30 | convolution fusion | flops 33570816 | bytes 33595396 | tf_op jit(solution)/shard_map/dot_general | solution.py:268
  50.4 6.0 %fusion.32 = (f32[8,4]{1,0:T(8,128)S(1)}, f32[8,4,4352]{2,1,0:T(4,128)S(1)}) fusion(bf16[8,4352,1,128]{3,1,2,0:T(8,128)(2,1)} %param.9, bf16[8,6,128]{2,1,0:T(8,128)(2,1)S(1)} %copy_select_fusion, pred[8,4352]{1,0:T(8,128)(4,1)S(1)} %fusion.7), kind=kOutput, calls=%fused_computation.91 | convolution fusion | flops 36069344 | bytes 9513088 | tf_op jit(solution)/shard_map/bgd,bsd->bgs/dot_general | solution.py:287
  56.9 5.1 %fusion.3 = bf16[1,8,4,128]{3,2,1,0:T(4,128)(2,1)S(1)} fusion(f32[8,4,4352]{2,1,0:T(4,128)S(1)} %get-tuple-element.312, f32[8,4]{1,0:T(8,128)S(1)} %get-tuple-element.288, f32[8,4]{1,0:T(8,128)S(1)} %multiply_maximum_fusion, f32[8,128]{1,0:T(8,128)S(1)} %bitcast.93, f32[8,4]{1,0:T(8,128)S(1)} %get-tuple-element.287, bf16[8,4352,1,128]{3,1,2,0:T(8,128)(2,1)} %param.10), kind=kOutput, calls=%fused_computation.8 | convolution fusion | flops 36081664 | bytes 9482624 | tf_op jit(solution)/shard_map/bgs,bsd->bgd/dot_general | solution.py:297
  87.9 5.4 %collective-permute-done.31.refs_5_ = bf16[2,512,128]{2,1,0:T(8,128)(2,1)S(1)} collective-permute-done((bf16[2,512,128]{2,1,0:T(8,128)(2,1)S(1)}, bf16[2,512,128]{2,1,0:T(8,128)(2,1)S(1)}, u32[]{:S(2)}, u32[]{:S(2)}) %collective-permute-start.31) | collective-permute-done | bytes 262176 | tf_op jit(solution)/shard_map/ppermute | solution.py:229
  94.1 13.3 %collective-permute-start.28 = (bf16[2,512,128]{2,1,0:T(8,128)(2,1)S(1)}, bf16[2,512,128]{2,1,0:T(8,128)(2,1)S(1)}, u32[]{:S(2)}, u32[]{:S(2)}) collective-permute-start(bf16[2,512,128]{2,1,0:T(8,128)(2,1)S(1)} %copy-done.24), channel_id=1, source_target_pairs={{0,6},{1,7},{2,4},{3,5},{4,2},{5,3},{6,0},{7,1},{8,14},{9,15},{10,... | collective-permute-start | bytes 786440 | tf_op jit(solution)/shard_map/ppermute | solution.py:229
  121.9 4.7 %shard_map.115 = (bf16[2,1280,128]{2,1,0:T(8,128)(2,1)}, bf16[2,1280,128]{2,1,0:T(8,128)(2,1)}, bf16[2,1280,128]{2,1,0:T(8,128)(2,1)}, bf16[2,1280,128]{2,1,0:T(...) custom-call(bf16[8,4352,128]{2,1,0:T(8,128)(2,1)} %bitcast.79, ...), custom_call_target="tpu_custom_call" | custom-call | bytes 9175040 | tf_op jit(solution)/shard_map/pallas_call | solution.py:52
  130.3 8.1 %collective-permute-done.24.refs_5_ = bf16[2,1024,128]{2,1,0:T(8,128)(2,1)S(1)} collective-permute-done((bf16[2,1024,128]{2,1,0:T(8,128)(2,1)S(1)}, bf16[2,1024,128]{2,1,0:T(8,128)(2,1)S(1)}, u32[]{:S(2)}, u32[]{:S(2)}) %collective-permute-start.24) | collective-permute-done | bytes 524320 | tf_op jit(solution)/shard_map/ppermute | solution.py:229
  140.0 4.2 %collective-permute-done.25.refs_6_ = bf16[2,1024,128]{2,1,0:T(8,128)(2,1)S(1)} collective-permute-done((bf16[2,1024,128]{2,1,0:T(8,128)(2,1)}, bf16[2,1024,128]{2,1,0:T(8,128)(2,1)S(1)}, u32[]{:S(2)}, u32[]{:S(2)}) %collective-permute-start.25) | collective-permute-done | bytes 524320 | tf_op jit(solution)/shard_map/ppermute | solution.py:229
  144.1 5.5 %collective-permute-done.26.refs_7_ = bf16[2,1024,128]{2,1,0:T(8,128)(2,1)S(1)} collective-permute-done((bf16[2,1024,128]{2,1,0:T(8,128)(2,1)}, bf16[2,1024,128]{2,1,0:T(8,128)(2,1)S(1)}, u32[]{:S(2)}, u32[]{:S(2)}) %collective-permute-start.26) | collective-permute-done | bytes 524320 | tf_op jit(solution)/shard_map/ppermute | solution.py:229
  151.5 4.7 %shard_map.116 = (bf16[32768,128]{1,0:T(8,128)(2,1)}, bf16[32768,128]{1,0:T(8,128)(2,1)}) custom-call(s32[1]{0:T(128)} %dynamic_slice.51.len_ref, f32[3,8,128]{2,1,0:T(8,128)} %maximum_maximum_fusion.new_ref, bf16[8,4352,128]{2,1,0:T(8,128)(2,1)} %bitcast.80, bf16[8,4352,128]{2,1,0:T(8,128)(2,1)} %bitcast.67, bf16[2,512,128]{2,1,0:T(8,128)(2,1)} %copy-done.31, ...), custom_call_target="tpu_custom_call" | custom-call | flops 4194304 | bytes 4194304 | tf_op jit(solution)/shard_map/pallas_call | solution.py:164
  156.2 5.4 %shard_map.117 = (bf16[32768,128]{1,0:T(8,128)(2,1)}, bf16[32768,128]{1,0:T(8,128)(2,1)}) custom-call(s32[1]{0:T(128)} %dynamic_slice.51.len_ref, f32[3,8,128]{2,1,0:T(8,128)} %maximum_maximum_fusion.new_ref, bf16[8,4352,128]{2,1,0:T(8,128)(2,1)} %bitcast.81, bf16[8,4352,128]{2,1,0:T(8,128)(2,1)} %bitcast.68, ...), custom_call_target="tpu_custom_call", output_to_operand_aliasing={{0}: (11, {}), {1}: (12, {})} | custom-call | flops 8388608 | bytes 8388608 | tf_op jit(solution)/shard_map/pallas_call | solution.py:164
  167.4 7.7 %collective-permute-done.60.refs_4_ = bf16[2,256,128]{2,1,0:T(8,128)(2,1)S(1)} collective-permute-done((bf16[2,256,128]{2,1,0:T(8,128)(2,1)}, bf16[2,256,128]{2,1,0:T(8,128)(2,1)S(1)}, u32[]{:S(2)}, u32[]{:S(2)}) %collective-permute-start.60) | collective-permute-done | bytes 131104 | tf_op jit(solution)/shard_map/ppermute | solution.py:229
  184.0 26.7 %collective-permute-done.44.refs_2_ = bf16[2,192,128]{2,1,0:T(8,128)(2,1)S(1)} collective-permute-done((bf16[2,192,128]{2,1,0:T(8,128)(2,1)}, bf16[2,192,128]{2,1,0:T(8,128)(2,1)S(1)}, u32[]{:S(2)}, u32[]{:S(2)}) %collective-permute-start.44) | collective-permute-done | bytes 98336 | tf_op jit(solution)/shard_map/ppermute | solution.py:229
  212.0 4.8 %collective-permute-done.45.refs_3_ = bf16[2,192,128]{2,1,0:T(8,128)(2,1)S(1)} collective-permute-done((bf16[2,192,128]{2,1,0:T(8,128)(2,1)}, bf16[2,192,128]{2,1,0:T(8,128)(2,1)S(1)}, u32[]{:S(2)}, u32[]{:S(2)}) %collective-permute-start.45) | collective-permute-done | bytes 98336 | tf_op jit(solution)/shard_map/ppermute | solution.py:229
  221.1 12.7 %collective-permute-done.18.refs_6_ = bf16[2,1280,128]{2,1,0:T(8,128)(2,1)S(1)} collective-permute-done((bf16[2,1280,128]{2,1,0:T(8,128)(2,1)}, bf16[2,1280,128]{2,1,0:T(8,128)(2,1)S(1)}, u32[]{:S(2)}, u32[]{:S(2)}) %collective-permute-start.18) | collective-permute-done | bytes 655392 | tf_op jit(solution)/shard_map/ppermute | solution.py:229
  237.5 6.6 %shard_map.120 = (bf16[32768,128]{1,0:T(8,128)(2,1)}, bf16[32768,128]{1,0:T(8,128)(2,1)}) custom-call(s32[1]{0:T(128)} %dynamic_slice.51.len_ref, f32[3,8,128]{2,1,0:T(8,128)} %maximum_maximum_fusion.new_ref, bf16[8,4352,128]{2,1,0:T(8,128)(2,1)} %bitcast.84, bf16[8,4352,128]{2,1,0:T(8,128)(2,1)} %bitcast.71, ...), custom_call_target="tpu_custom_call", output_to_operand_aliasing={{0}: (11, {}), {1}: (12, {})} | custom-call | flops 10485760 | bytes 10485760 | tf_op jit(solution)/shard_map/pallas_call | solution.py:164
  245.9 6.8 %collective-permute-done.46.refs_4_ = bf16[2,192,128]{2,1,0:T(8,128)(2,1)S(1)} collective-permute-done((bf16[2,192,128]{2,1,0:T(8,128)(2,1)}, bf16[2,192,128]{2,1,0:T(8,128)(2,1)S(1)}, u32[]{:S(2)}, u32[]{:S(2)}) %collective-permute-start.46) | collective-permute-done | bytes 98336 | tf_op jit(solution)/shard_map/ppermute | solution.py:229
  261.8 5.4 %collective-permute-done.51.refs_4_ = bf16[2,768,128]{2,1,0:T(8,128)(2,1)S(1)} collective-permute-done((bf16[2,768,128]{2,1,0:T(8,128)(2,1)}, bf16[2,768,128]{2,1,0:T(8,128)(2,1)S(1)}, u32[]{:S(2)}, u32[]{:S(2)}) %collective-permute-start.51) | collective-permute-done | bytes 393248 | tf_op jit(solution)/shard_map/ppermute | solution.py:229
  268.4 6.1 %collective-permute-done.52.refs_5_ = bf16[2,768,128]{2,1,0:T(8,128)(2,1)S(1)} collective-permute-done((bf16[2,768,128]{2,1,0:T(8,128)(2,1)}, bf16[2,768,128]{2,1,0:T(8,128)(2,1)S(1)}, u32[]{:S(2)}, u32[]{:S(2)}) %collective-permute-start.52) | collective-permute-done | bytes 393248 | tf_op jit(solution)/shard_map/ppermute | solution.py:229
  284.5 13.5 %fusion.1 = bf16[1,4096]{1,0:T(2,128)(2,1)} fusion(bf16[4096,1]{0,1:T(2,128)(2,1)S(1)} %bitcast.94, bf16[4096,4096]{1,0:T(8,128)(2,1)} %param.17, bf16[1,4096]{1,0:T(2,128)(2,1)S(1)} %copy-done.5), kind=kOutput, calls=%fused_computation.5 | convolution fusion | flops 33566720 | bytes 33579008 | tf_op jit(solution)/shard_map/dot_general | solution.py:317
  300.1 4.8 %shard_map.124 = (bf16[32768,128]{1,0:T(8,128)(2,1)}, bf16[32768,128]{1,0:T(8,128)(2,1)}) custom-call(s32[1]{0:T(128)} %dynamic_slice.51.len_ref, f32[3,8,128]{2,1,0:T(8,128)} %maximum_maximum_fusion.new_ref, bf16[8,4352,128]{2,1,0:T(8,128)(2,1)} %bitcast.86, bf16[8,4352,128]{2,1,0:T(8,128)(2,1)} %bitcast.73, ...), custom_call_target="tpu_custom_call", output_to_operand_aliasing={{0}: (11, {}), {1}: (12, {})} | custom-call | flops 6291456 | bytes 6291456 | tf_op jit(solution)/shard_map/pallas_call | solution.py:164
  (260 shorter events, 121.7 us)
Async XLA Ops:
  44.9 38.6 %collective-permute-start.29 = (bf16[2,512,128]{2,1,0:T(8,128)(2,1)S(1)}, bf16[2,512,128]{2,1,0:T(8,128)(2,1)S(1)}, u32[]{:S(2)}, u32[]{:S(2)}) collective-permute-start(bf16[2,512,128]{2,1,0:T(8,128)(2,1)S(1)} %copy-done.45), channel_id=1, source_target_pairs={{0,4},{1,5},{2,6},{3,7},{4,0},{5,1},{6,2},{7,3},{8,12},{9,13},{10,... | collective-permute-start | bytes 786440 | tf_op jit(solution)/shard_map/ppermute | solution.py:229
  46.6 29.3 %collective-permute-start.56 = (bf16[2,256,128]{2,1,0:T(8,128)(2,1)}, bf16[2,256,128]{2,1,0:T(8,128)(2,1)S(1)}, u32[]{:S(2)}, u32[]{:S(2)}) collective-permute-start(bf16[2,256,128]{2,1,0:T(8,128)(2,1)} %get-tuple-element.267), channel_id=1, source_target_pairs={{0,6},{1,7},{2,4},{3,5},{4,2},{5,3},{6,0},{7,1},{8,14},{9,15},{10,... | collective-permute-start | bytes 393224 | tf_op jit(solution)/shard_map/ppermute | solution.py:229
  48.1 28.4 %collective-permute-start.57 = (bf16[2,256,128]{2,1,0:T(8,128)(2,1)}, bf16[2,256,128]{2,1,0:T(8,128)(2,1)S(1)}, u32[]{:S(2)}, u32[]{:S(2)}) collective-permute-start(bf16[2,256,128]{2,1,0:T(8,128)(2,1)} %get-tuple-element.268), channel_id=1, source_target_pairs={{0,4},{1,5},{2,6},{3,7},{4,0},{5,1},{6,2},{7,3},{8,12},{9,13},{10,... | collective-permute-start | bytes 393224 | tf_op jit(solution)/shard_map/ppermute | solution.py:229
  82.0 34.7 %collective-permute-start.21 = (bf16[2,1024,128]{2,1,0:T(8,128)(2,1)S(1)}, bf16[2,1024,128]{2,1,0:T(8,128)(2,1)S(1)}, u32[]{:S(2)}, u32[]{:S(2)}) collective-permute-start(bf16[2,1024,128]{2,1,0:T(8,128)(2,1)S(1)} %copy-done.39), channel_id=1, source_target_pairs={{0,6},{1,7},{2,4},{3,5},{4,2},{5,3},{6,0},{7,1},{8,14},{9,15},{10,... | collective-permute-start | bytes 1572872 | tf_op jit(solution)/shard_map/ppermute | solution.py:229
  83.5 38.4 %collective-permute-start.22 = (bf16[2,1024,128]{2,1,0:T(8,128)(2,1)S(1)}, bf16[2,1024,128]{2,1,0:T(8,128)(2,1)S(1)}, u32[]{:S(2)}, u32[]{:S(2)}) collective-permute-start(bf16[2,1024,128]{2,1,0:T(8,128)(2,1)S(1)} %copy-done.38), channel_id=1, source_target_pairs={{0,4},{1,5},{2,6},{3,7},{4,0},{5,1},{6,2},{7,3},{8,12},{9,13},{10,... | collective-permute-start | bytes 1572872 | tf_op jit(solution)/shard_map/ppermute | solution.py:229
  110.7 27.6 %collective-permute-start.24 = (bf16[2,1024,128]{2,1,0:T(8,128)(2,1)S(1)}, bf16[2,1024,128]{2,1,0:T(8,128)(2,1)S(1)}, u32[]{:S(2)}, u32[]{:S(2)}) collective-permute-start(bf16[2,1024,128]{2,1,0:T(8,128)(2,1)S(1)} %copy-done.36), channel_id=1, source_target_pairs={{0,7},{1,6},{2,5},{3,4},{4,3},{5,2},{6,1},{7,0},{8,15},{9,14},{10,... | collective-permute-start | bytes 1572872 | tf_op jit(solution)/shard_map/ppermute | solution.py:229
  116.7 27.4 %collective-permute-start.25 = (bf16[2,1024,128]{2,1,0:T(8,128)(2,1)}, bf16[2,1024,128]{2,1,0:T(8,128)(2,1)S(1)}, u32[]{:S(2)}, u32[]{:S(2)}) collective-permute-start(bf16[2,1024,128]{2,1,0:T(8,128)(2,1)} %get-tuple-element.185), channel_id=1, source_target_pairs={{0,5},{1,4},{2,7},{3,6},{4,1},{5,0},{6,3},{7,2},{8,13},{9,12},{10,... | collective-permute-start | bytes 1572872 | tf_op jit(solution)/shard_map/ppermute | solution.py:229
  116.7 32.9 %collective-permute-start.26 = (bf16[2,1024,128]{2,1,0:T(8,128)(2,1)}, bf16[2,1024,128]{2,1,0:T(8,128)(2,1)S(1)}, u32[]{:S(2)}, u32[]{:S(2)}) collective-permute-start(bf16[2,1024,128]{2,1,0:T(8,128)(2,1)} %get-tuple-element.186), channel_id=1, source_target_pairs={{0,3},{1,2},{2,1},{3,0},{4,7},{5,6},{6,5},{7,4},{8,11},{9,10},{10,... | collective-permute-start | bytes 1572872 | tf_op jit(solution)/shard_map/ppermute | solution.py:229
  121.9 28.8 %collective-permute-start.27 = (bf16[2,1024,128]{2,1,0:T(8,128)(2,1)}, bf16[2,1024,128]{2,1,0:T(8,128)(2,1)S(1)}, u32[]{:S(2)}, u32[]{:S(2)}) collective-permute-start(bf16[2,1024,128]{2,1,0:T(8,128)(2,1)} %get-tuple-element.187), channel_id=1, source_target_pairs={{0,1},{1,0},{2,3},{3,2},{4,5},{5,4},{6,7},{7,6},{8,9},{9,8},{10,11... | collective-permute-start | bytes 1572872 | tf_op jit(solution)/shard_map/ppermute | solution.py:229
  126.7 90.1 %collective-permute-start.14 = (bf16[2,1280,128]{2,1,0:T(8,128)(2,1)}, bf16[2,1280,128]{2,1,0:T(8,128)(2,1)S(1)}, u32[]{:S(2)}, u32[]{:S(2)}) collective-permute-start(bf16[2,1280,128]{2,1,0:T(8,128)(2,1)} %get-tuple-element.174), channel_id=1, source_target_pairs={{0,6},{1,7},{2,4},{3,5},{4,2},{5,3},{6,0},{7,1},{8,14},{9,15},{10,... | collective-permute-start | bytes 1966088 | tf_op jit(solution)/shard_map/ppermute | solution.py:229
  138.3 80.8 %collective-permute-start.15 = (bf16[2,1280,128]{2,1,0:T(8,128)(2,1)}, bf16[2,1280,128]{2,1,0:T(8,128)(2,1)S(1)}, u32[]{:S(2)}, u32[]{:S(2)}) collective-permute-start(bf16[2,1280,128]{2,1,0:T(8,128)(2,1)} %get-tuple-element.175), channel_id=1, source_target_pairs={{0,4},{1,5},{2,6},{3,7},{4,0},{5,1},{6,2},{7,3},{8,12},{9,13},{10,... | collective-permute-start | bytes 1966088 | tf_op jit(solution)/shard_map/ppermute | solution.py:229
  144.1 30.9 %collective-permute-start.60 = (bf16[2,256,128]{2,1,0:T(8,128)(2,1)}, bf16[2,256,128]{2,1,0:T(8,128)(2,1)S(1)}, u32[]{:S(2)}, u32[]{:S(2)}) collective-permute-start(bf16[2,256,128]{2,1,0:T(8,128)(2,1)} %get-tuple-element.271), channel_id=1, source_target_pairs={{0,5},{1,4},{2,7},{3,6},{4,1},{5,0},{6,3},{7,2},{8,13},{9,12},{10,... | collective-permute-start | bytes 393224 | tf_op jit(solution)/shard_map/ppermute | solution.py:229
  149.6 27.0 %collective-permute-start.61 = (bf16[2,256,128]{2,1,0:T(8,128)(2,1)S(1)}, bf16[2,256,128]{2,1,0:T(8,128)(2,1)S(1)}, u32[]{:S(2)}, u32[]{:S(2)}) collective-permute-start(bf16[2,256,128]{2,1,0:T(8,128)(2,1)S(1)} %copy-done.47), channel_id=1, source_target_pairs={{0,3},{1,2},{2,1},{3,0},{4,7},{5,6},{6,5},{7,4},{8,11},{9,10},{10,... | collective-permute-start | bytes 393224 | tf_op jit(solution)/shard_map/ppermute | solution.py:229
  150.7 27.4 %collective-permute-start.62 = (bf16[2,256,128]{2,1,0:T(8,128)(2,1)S(1)}, bf16[2,256,128]{2,1,0:T(8,128)(2,1)S(1)}, u32[]{:S(2)}, u32[]{:S(2)}) collective-permute-start(bf16[2,256,128]{2,1,0:T(8,128)(2,1)S(1)} %copy-done.46), channel_id=1, source_target_pairs={{0,1},{1,0},{2,3},{3,2},{4,5},{5,4},{6,7},{7,6},{8,9},{9,8},{10,11... | collective-permute-start | bytes 393224 | tf_op jit(solution)/shard_map/ppermute | solution.py:229
  178.1 41.1 %collective-permute-start.16 = (bf16[2,1280,128]{2,1,0:T(8,128)(2,1)S(1)}, bf16[2,1280,128]{2,1,0:T(8,128)(2,1)S(1)}, u32[]{:S(2)}, u32[]{:S(2)}) collective-permute-start(bf16[2,1280,128]{2,1,0:T(8,128)(2,1)S(1)} %copy-done.35), channel_id=1, source_target_pairs={{0,2},{1,3},{2,0},{3,1},{4,6},{5,7},{6,4},{7,5},{8,10},{9,11},{10,... | collective-permute-start | bytes 1966088 | tf_op jit(solution)/shard_map/ppermute | solution.py:229
  181.7 38.6 %collective-permute-start.17 = (bf16[2,1280,128]{2,1,0:T(8,128)(2,1)}, bf16[2,1280,128]{2,1,0:T(8,128)(2,1)S(1)}, u32[]{:S(2)}, u32[]{:S(2)}) collective-permute-start(bf16[2,1280,128]{2,1,0:T(8,128)(2,1)} %get-tuple-element.177), channel_id=1, source_target_pairs={{0,7},{1,6},{2,5},{3,4},{4,3},{5,2},{6,1},{7,0},{8,15},{9,14},{10,... | collective-permute-start | bytes 1966088 | tf_op jit(solution)/shard_map/ppermute | solution.py:229
  183.1 27.6 %collective-permute-start.44 = (bf16[2,192,128]{2,1,0:T(8,128)(2,1)}, bf16[2,192,128]{2,1,0:T(8,128)(2,1)S(1)}, u32[]{:S(2)}, u32[]{:S(2)}) collective-permute-start(bf16[2,192,128]{2,1,0:T(8,128)(2,1)} %get-tuple-element.254), channel_id=1, source_target_pairs={{0,2},{1,3},{2,0},{3,1},{4,6},{5,7},{6,4},{7,5},{8,10},{9,11},{10,... | collective-permute-start | bytes 294920 | tf_op jit(solution)/shard_map/ppermute | solution.py:229
  219.2 40.2 %collective-permute-start.49 = (bf16[2,768,128]{2,1,0:T(8,128)(2,1)}, bf16[2,768,128]{2,1,0:T(8,128)(2,1)S(1)}, u32[]{:S(2)}, u32[]{:S(2)}) collective-permute-start(bf16[2,768,128]{2,1,0:T(8,128)(2,1)} %get-tuple-element.260), channel_id=1, source_target_pairs={{0,6},{1,7},{2,4},{3,5},{4,2},{5,3},{6,0},{7,1},{8,14},{9,15},{10,... | collective-permute-start | bytes 1179656 | tf_op jit(solution)/shard_map/ppermute | solution.py:229
  220.2 40.4 %collective-permute-start.50 = (bf16[2,768,128]{2,1,0:T(8,128)(2,1)}, bf16[2,768,128]{2,1,0:T(8,128)(2,1)S(1)}, u32[]{:S(2)}, u32[]{:S(2)}) collective-permute-start(bf16[2,768,128]{2,1,0:T(8,128)(2,1)} %get-tuple-element.261), channel_id=1, source_target_pairs={{0,4},{1,5},{2,6},{3,7},{4,0},{5,1},{6,2},{7,3},{8,12},{9,13},{10,... | collective-permute-start | bytes 1179656 | tf_op jit(solution)/shard_map/ppermute | solution.py:229
  260.6 23.9 %collective-permute-start.55 = (bf16[2,768,128]{2,1,0:T(8,128)(2,1)}, bf16[2,768,128]{2,1,0:T(8,128)(2,1)}, u32[]{:S(2)}, u32[]{:S(2)}) collective-permute-start(bf16[2,768,128]{2,1,0:T(8,128)(2,1)} %get-tuple-element.266), channel_id=1, source_target_pairs={{0,1},{1,0},{2,3},{3,2},{4,5},{5,4},{6,7},{7,6},{8,9},{9,8},{10,11... | collective-permute-start | bytes 1179656 | tf_op jit(solution)/shard_map/ppermute | solution.py:229
  267.2 39.5 %collective-permute-start.37 = (bf16[2,64,128]{2,1,0:T(8,128)(2,1)}, bf16[2,64,128]{2,1,0:T(8,128)(2,1)S(1)}, u32[]{:S(2)}, u32[]{:S(2)}) collective-permute-start(bf16[2,64,128]{2,1,0:T(8,128)(2,1)} %get-tuple-element.246), channel_id=1, source_target_pairs={{0,2},{1,3},{2,0},{3,1},{4,6},{5,7},{6,4},{7,5},{8,10},{9,11},{10,... | collective-permute-start | bytes 98312 | tf_op jit(solution)/shard_map/ppermute | solution.py:229
  274.5 32.2 %collective-permute-start.38 = (bf16[2,64,128]{2,1,0:T(8,128)(2,1)}, bf16[2,64,128]{2,1,0:T(8,128)(2,1)S(1)}, u32[]{:S(2)}, u32[]{:S(2)}) collective-permute-start(bf16[2,64,128]{2,1,0:T(8,128)(2,1)} %get-tuple-element.247), channel_id=1, source_target_pairs={{0,7},{1,6},{2,5},{3,4},{4,3},{5,2},{6,1},{7,0},{8,15},{9,14},{10,... | collective-permute-start | bytes 98312 | tf_op jit(solution)/shard_map/ppermute | solution.py:229
  277.7 29.0 %collective-permute-start.39 = (bf16[2,64,128]{2,1,0:T(8,128)(2,1)}, bf16[2,64,128]{2,1,0:T(8,128)(2,1)S(1)}, u32[]{:S(2)}, u32[]{:S(2)}) collective-permute-start(bf16[2,64,128]{2,1,0:T(8,128)(2,1)} %get-tuple-element.248), channel_id=1, source_target_pairs={{0,5},{1,4},{2,7},{3,6},{4,1},{5,0},{6,3},{7,2},{8,13},{9,12},{10,... | collective-permute-start | bytes 98312 | tf_op jit(solution)/shard_map/ppermute | solution.py:229
  282.6 24.1 %collective-permute-start.40 = (bf16[2,64,128]{2,1,0:T(8,128)(2,1)}, bf16[2,64,128]{2,1,0:T(8,128)(2,1)S(1)}, u32[]{:S(2)}, u32[]{:S(2)}) collective-permute-start(bf16[2,64,128]{2,1,0:T(8,128)(2,1)} %get-tuple-element.249), channel_id=1, source_target_pairs={{0,3},{1,2},{2,1},{3,0},{4,7},{5,6},{6,5},{7,4},{8,11},{9,10},{10,... | collective-permute-start | bytes 98312 | tf_op jit(solution)/shard_map/ppermute | solution.py:229
  (89 other events, 1567.2 us)

commit v9 on v8

--- a/solution.py
+++ b/solution.py
@@ -15,7 +15,7 @@
 GROUP = 32
 WRAP = 256
 SMALL = 256
-CHUNKS = ((256, 512), (768, 1024), (1792, 1280), (3072, 768), (3840, 192), (4032, 64))
+CHUNKS = ((256, 512), (768, 1024), (1792, 1280), (3072, 640), (3712, 256), (3968, 128))
 BLOCK = 256
 ORDER = (6, 4, 2, 7, 5, 3, 1)
 VMEM_LIMIT = 56 * 1024 * 1024
@@ -49,9 +49,10 @@
 def pack(first, count, offsets, k_mine, v_mine):
     dim = k_mine.shape[2]
     pieces = len(offsets)
+    piece = pltpu.VMEM if first == CHUNKS[0][0] or count <= SMALL else jax.ShapeDtypeStruct
     return pl.pallas_call(
         functools.partial(pack_kernel, first, count, offsets),
-        out_shape=[jax.ShapeDtypeStruct((2, count, dim), jnp.bfloat16)] * pieces,
+        out_shape=[piece((2, count, dim), jnp.bfloat16)] * pieces,
         in_specs=[pl.BlockSpec(memory_space=pltpu.HBM)] * 2,
         out_specs=[pl.BlockSpec(memory_space=pltpu.VMEM)] * pieces,
         scratch_shapes=[pltpu.SemaphoreType.DMA((pieces, 2))],

time: 310 us -> 315 us (1.016)
  waiting for transfers between devices: 128 us -> 150 us
  starting transfers between devices: 75.5 us -> 58.9 us
    ppermute x63, waiting for transfers between devices: 128 us -> 150 us  [swap(): return lax.ppermute(value, 'sh', [(i, i ^ offset) for i in range(PEERS)])]
    ppermute x63, starting transfers between devices: 75.5 us -> 58.9 us  [swap(): return lax.ppermute(value, 'sh', [(i, i ^ offset) for i in range(PEERS)])]
    pallas_call x7, Pallas kernels: 20.6 us -> 16.8 us  [pack(): pl.pallas_call(functools.partial(pack_kernel, first, count, offsets), out...]
  transfers between devices with their start and end apart: 63 -> 63, of which waited for: 27 -> 26; matrix products, arithmetic and copies ran while one was open for 9% -> 9% of each run, Pallas kernels for 13% -> 12%
where the time goes in v9:
time: 315 us; the launch traced here: 313 us
  waiting for transfers between devices  150 us (48%)
  starting transfers between devices  58.9 us (19%)
  Pallas kernels  46.8 us (15%)
  matrix products  46.4 us (15%)
  local copies, waits for them, and re-layouts  4.72 us (1%)
    ppermute x63, waiting for transfers between devices, swap(): return lax.ppermute(value, 'sh', [(i, i ^ offset) for i in range(PEERS)])  150 us
    ppermute x63, starting transfers between devices, swap(): return lax.ppermute(value, 'sh', [(i, i ^ offset) for i in range(PEERS)])  58.9 us
    pallas_call x4, Pallas kernels, interleave(): pl.pallas_call(functools.partial(interleave_kernel, first, count, block,...  21.7 us
    pallas_call x7, Pallas kernels, pack(): pl.pallas_call(functools.partial(pack_kernel, first, count, offsets), out...  16.8 us
    dot_general x1, matrix products, per_device(): jnp.dot(attn_out, w_out, preferred_element_type=jnp.float32)  13.5 us
    dot_general x1, matrix products, per_device(): jnp.dot(normed, w_query, preferred_element_type=jnp.float32)  12.8 us
  transfers between devices with their start and end apart: 63, of which 26 were waited for; matrix products, arithmetic and copies ran while one was open for 9% of the time, Pallas kernels for 12%

profile of v9, /device:TPU:0, one launch (start us, length us, event | category | flops | bytes accessed | tf_op | source)
XLA Modules:
  0.0 313.1 jit_solution(14806389920911813892)
XLA Ops:
  3.2 4.0 %shard_map.114 = (bf16[2,1024,128]{2,1,0:T(8,128)(2,1)}, bf16[2,1024,128]{2,1,0:T(8,128)(2,1)}, bf16[2,1024,128]{2,1,0:T(8,128)(2,1)}, bf16[2,1024,128]{2,1,0:T(...) custom-call(bf16[8,4352,128]{2,1,0:T(8,128)(2,1)} %bitcast.76, ...), custom_call_target="tpu_custom_call" | custom-call | bytes 7340032 | tf_op jit(solution)/shard_map/pallas_call | solution.py:53
  8.6 4.6 %fusion.14 = f32[1,1024]{1,0:T(1,128)S(1)} fusion(bf16[4096,1024]{1,0:T(8,128)(2,1)} %param.15, f32[1,4096]{1,0:T(1,128)S(1)} %bitcast.89, bf16[1,4096]{1,0:T(2,128)(2,1)S(1)} %copy-done.3, f32[]{:T(128)S(6)} %rsqrt.4), kind=kOutput, calls=%fused_computation.28 | convolution fusion | flops 8404992 | bytes 8417284 | tf_op jit(solution)/shard_map/dot_general | solution.py:270
  14.6 4.6 %fusion.12 = f32[1,1024]{1,0:T(1,128)S(1)} fusion(bf16[4096,1024]{1,0:T(8,128)(2,1)} %param.16, f32[1,4096]{1,0:T(1,128)S(1)} %bitcast.90, bf16[1,4096]{1,0:T(2,128)(2,1)S(1)} %copy-done.3, f32[]{:T(128)S(6)} %rsqrt.4), kind=kOutput, calls=%fused_computation.26 | convolution fusion | flops 8404992 | bytes 8417284 | tf_op jit(solution)/shard_map/dot_general | solution.py:271
  19.8 12.8 %fusion.16 = f32[1,4096]{1,0:T(1,128)S(1)} fusion(bf16[4096,4096]{1,0:T(8,128)(2,1)} %param.14, f32[1,4096]{1,0:T(1,128)S(1)} %bitcast.91, bf16[1,4096]{1,0:T(2,128)(2,1)S(1)} %copy-done.3, f32[]{:T(128)S(6)} %rsqrt.4), kind=kOutput, calls=%fused_computation.30 | convolution fusion | flops 33570816 | bytes 33595396 | tf_op jit(solution)/shard_map/dot_general | solution.py:269
  50.1 6.0 %fusion.32 = (f32[8,4]{1,0:T(8,128)S(1)}, f32[8,4,4352]{2,1,0:T(4,128)S(1)}) fusion(bf16[8,4352,1,128]{3,1,2,0:T(8,128)(2,1)} %param.9, bf16[8,6,128]{2,1,0:T(8,128)(2,1)S(1)} %copy_select_fusion, pred[8,4352]{1,0:T(8,128)(4,1)S(1)} %fusion.7), kind=kOutput, calls=%fused_computation.91 | convolution fusion | flops 36069344 | bytes 9513088 | tf_op jit(solution)/shard_map/bgd,bsd->bgs/dot_general | solution.py:288
  56.5 5.0 %fusion.3 = bf16[1,8,4,128]{3,2,1,0:T(4,128)(2,1)S(1)} fusion(f32[8,4,4352]{2,1,0:T(4,128)S(1)} %get-tuple-element.312, f32[8,4]{1,0:T(8,128)S(1)} %get-tuple-element.288, f32[8,4]{1,0:T(8,128)S(1)} %multiply_maximum_fusion, f32[8,128]{1,0:T(8,128)S(1)} %bitcast.93, f32[8,4]{1,0:T(8,128)S(1)} %get-tuple-element.287, bf16[8,4352,1,128]{3,1,2,0:T(8,128)(2,1)} %param.10), kind=kOutput, calls=%fused_computation.8 | convolution fusion | flops 36081664 | bytes 9482624 | tf_op jit(solution)/shard_map/bgs,bsd->bgd/dot_general | solution.py:298
  69.6 3.6 %collective-permute-done.12 = bf16[1,512]{1,0:T(2,128)(2,1)S(1)} collective-permute-done((bf16[1,512]{1,0:T(2,128)(2,1)S(1)}, bf16[1,512]{1,0:T(2,128)(2,1)S(1)}, u32[]{:S(2)}, u32[]{:S(2)}) %collective-permute-start.12) | collective-permute-done | bytes 1056 | tf_op jit(solution)/shard_map/ppermute | solution.py:230
  73.2 3.9 %collective-permute-done.13 = bf16[1,512]{1,0:T(2,128)(2,1)S(1)} collective-permute-done((bf16[1,512]{1,0:T(2,128)(2,1)S(1)}, bf16[1,512]{1,0:T(2,128)(2,1)S(1)}, u32[]{:S(2)}, u32[]{:S(2)}) %collective-permute-start.13) | collective-permute-done | bytes 1056 | tf_op jit(solution)/shard_map/ppermute | solution.py:230
  99.2 3.3 %collective-permute-done.31.refs_5_ = bf16[2,512,128]{2,1,0:T(8,128)(2,1)} collective-permute-done((bf16[2,512,128]{2,1,0:T(8,128)(2,1)S(1)}, bf16[2,512,128]{2,1,0:T(8,128)(2,1)}, u32[]{:S(2)}, u32[]{:S(2)}) %collective-permute-start.31) | collective-permute-done | bytes 262176 | tf_op jit(solution)/shard_map/ppermute | solution.py:230
  103.7 3.7 %collective-permute-done.32.refs_6_ = bf16[2,512,128]{2,1,0:T(8,128)(2,1)S(1)} collective-permute-done((bf16[2,512,128]{2,1,0:T(8,128)(2,1)S(1)}, bf16[2,512,128]{2,1,0:T(8,128)(2,1)S(1)}, u32[]{:S(2)}, u32[]{:S(2)}) %collective-permute-start.32) | collective-permute-done | bytes 262176 | tf_op jit(solution)/shard_map/ppermute | solution.py:230
  111.7 4.5 %shard_map.115 = (bf16[2,1280,128]{2,1,0:T(8,128)(2,1)}, bf16[2,1280,128]{2,1,0:T(8,128)(2,1)}, bf16[2,1280,128]{2,1,0:T(8,128)(2,1)}, bf16[2,1280,128]{2,1,0:T(...) custom-call(bf16[8,4352,128]{2,1,0:T(8,128)(2,1)} %bitcast.79, ...), custom_call_target="tpu_custom_call" | custom-call | bytes 9175040 | tf_op jit(solution)/shard_map/pallas_call | solution.py:53
  116.2 31.8 %collective-permute-done.28.refs_2_ = bf16[2,512,128]{2,1,0:T(8,128)(2,1)} collective-permute-done((bf16[2,512,128]{2,1,0:T(8,128)(2,1)S(1)}, bf16[2,512,128]{2,1,0:T(8,128)(2,1)}, u32[]{:S(2)}, u32[]{:S(2)}) %collective-permute-start.28) | collective-permute-done | bytes 262176 | tf_op jit(solution)/shard_map/ppermute | solution.py:230
  153.4 37.1 %collective-permute-done.25.refs_6_ = bf16[2,1024,128]{2,1,0:T(8,128)(2,1)S(1)} collective-permute-done((bf16[2,1024,128]{2,1,0:T(8,128)(2,1)S(1)}, bf16[2,1024,128]{2,1,0:T(8,128)(2,1)S(1)}, u32[]{:S(2)}, u32[]{:S(2)}) %collective-permute-start.25) | collective-permute-done | bytes 524320 | tf_op jit(solution)/shard_map/ppermute | solution.py:230
  196.1 4.7 %shard_map.116 = (bf16[32768,128]{1,0:T(8,128)(2,1)}, bf16[32768,128]{1,0:T(8,128)(2,1)}) custom-call(s32[1]{0:T(128)} %dynamic_slice.51.len_ref, f32[3,8,128]{2,1,0:T(8,128)} %maximum_maximum_fusion.new_ref, bf16[8,4352,128]{2,1,0:T(8,128)(2,1)} %bitcast.80, bf16[8,4352,128]{2,1,0:T(8,128)(2,1)} %bitcast.67, ...), custom_call_target="tpu_custom_call" | custom-call | flops 4194304 | bytes 4194304 | tf_op jit(solution)/shard_map/pallas_call | solution.py:165
  200.9 5.4 %shard_map.117 = (bf16[32768,128]{1,0:T(8,128)(2,1)}, bf16[32768,128]{1,0:T(8,128)(2,1)}) custom-call(s32[1]{0:T(128)} %dynamic_slice.51.len_ref, f32[3,8,128]{2,1,0:T(8,128)} %maximum_maximum_fusion.new_ref, bf16[8,4352,128]{2,1,0:T(8,128)(2,1)} %bitcast.81, bf16[8,4352,128]{2,1,0:T(8,128)(2,1)} %bitcast.68, ...), custom_call_target="tpu_custom_call", output_to_operand_aliasing={{0}: (11, {}), {1}: (12, {})} | custom-call | flops 8388608 | bytes 8388608 | tf_op jit(solution)/shard_map/pallas_call | solution.py:165
  206.3 3.2 %shard_map.118 = (bf16[2,640,128]{2,1,0:T(8,128)(2,1)}, bf16[2,640,128]{2,1,0:T(8,128)(2,1)}, bf16[2,640,128]{2,1,0:T(8,128)(2,1)}, bf16[2,640,128]{2,1,0:T(8,12...) custom-call(bf16[8,4352,128]{2,1,0:T(8,128)(2,1)} %bitcast.82, ...), custom_call_target="tpu_custom_call" | custom-call | bytes 4587520 | tf_op jit(solution)/shard_map/pallas_call | solution.py:53
  211.8 9.6 %collective-permute-done.17.refs_5_ = bf16[2,1280,128]{2,1,0:T(8,128)(2,1)S(1)} collective-permute-done((bf16[2,1280,128]{2,1,0:T(8,128)(2,1)}, bf16[2,1280,128]{2,1,0:T(8,128)(2,1)S(1)}, u32[]{:S(2)}, u32[]{:S(2)}) %collective-permute-start.17) | collective-permute-done | bytes 655392 | tf_op jit(solution)/shard_map/ppermute | solution.py:230
  223.9 11.5 %collective-permute-done.19.refs_7_ = bf16[2,1280,128]{2,1,0:T(8,128)(2,1)S(1)} collective-permute-done((bf16[2,1280,128]{2,1,0:T(8,128)(2,1)}, bf16[2,1280,128]{2,1,0:T(8,128)(2,1)S(1)}, u32[]{:S(2)}, u32[]{:S(2)}) %collective-permute-start.19) | collective-permute-done | bytes 655392 | tf_op jit(solution)/shard_map/ppermute | solution.py:230
  242.1 8.8 %collective-permute-done.45.refs_3_ = bf16[2,256,128]{2,1,0:T(8,128)(2,1)S(1)} collective-permute-done((bf16[2,256,128]{2,1,0:T(8,128)(2,1)S(1)}, bf16[2,256,128]{2,1,0:T(8,128)(2,1)S(1)}, u32[]{:S(2)}, u32[]{:S(2)}) %collective-permute-start.45) | collective-permute-done | bytes 131104 | tf_op jit(solution)/shard_map/ppermute | solution.py:230
  252.4 6.7 %shard_map.120 = (bf16[32768,128]{1,0:T(8,128)(2,1)}, bf16[32768,128]{1,0:T(8,128)(2,1)}) custom-call(s32[1]{0:T(128)} %dynamic_slice.51.len_ref, f32[3,8,128]{2,1,0:T(8,128)} %maximum_maximum_fusion.new_ref, bf16[8,4352,128]{2,1,0:T(8,128)(2,1)} %bitcast.84, bf16[8,4352,128]{2,1,0:T(8,128)(2,1)} %bitcast.71, ...), custom_call_target="tpu_custom_call", output_to_operand_aliasing={{0}: (11, {}), {1}: (12, {})} | custom-call | flops 10485760 | bytes 10485760 | tf_op jit(solution)/shard_map/pallas_call | solution.py:165
  270.3 4.5 %collective-permute-done.51.refs_4_ = bf16[2,640,128]{2,1,0:T(8,128)(2,1)} collective-permute-done((bf16[2,640,128]{2,1,0:T(8,128)(2,1)}, bf16[2,640,128]{2,1,0:T(8,128)(2,1)}, u32[]{:S(2)}, u32[]{:S(2)}) %collective-permute-start.51) | collective-permute-done | bytes 327712 | tf_op jit(solution)/shard_map/ppermute | solution.py:230
  275.2 4.6 %collective-permute-done.52.refs_5_ = bf16[2,640,128]{2,1,0:T(8,128)(2,1)} collective-permute-done((bf16[2,640,128]{2,1,0:T(8,128)(2,1)}, bf16[2,640,128]{2,1,0:T(8,128)(2,1)}, u32[]{:S(2)}, u32[]{:S(2)}) %collective-permute-start.52) | collective-permute-done | bytes 327712 | tf_op jit(solution)/shard_map/ppermute | solution.py:230
  289.0 13.5 %fusion.1 = bf16[1,4096]{1,0:T(2,128)(2,1)} fusion(bf16[4096,1]{0,1:T(2,128)(2,1)S(1)} %bitcast.94, bf16[4096,4096]{1,0:T(8,128)(2,1)} %param.17, bf16[1,4096]{1,0:T(2,128)(2,1)S(1)} %copy-done.3), kind=kOutput, calls=%fused_computation.5 | convolution fusion | flops 33566720 | bytes 33579008 | tf_op jit(solution)/shard_map/dot_general | solution.py:318
  304.5 4.8 %shard_map.124 = (bf16[32768,128]{1,0:T(8,128)(2,1)}, bf16[32768,128]{1,0:T(8,128)(2,1)}) custom-call(s32[1]{0:T(128)} %dynamic_slice.51.len_ref, f32[3,8,128]{2,1,0:T(8,128)} %maximum_maximum_fusion.new_ref, bf16[8,4352,128]{2,1,0:T(8,128)(2,1)} %bitcast.86, bf16[8,4352,128]{2,1,0:T(8,128)(2,1)} %bitcast.73, ...), custom_call_target="tpu_custom_call", output_to_operand_aliasing={{0}: (11, {}), {1}: (12, {})} | custom-call | flops 5242880 | bytes 5242880 | tf_op jit(solution)/shard_map/pallas_call | solution.py:165
  (276 shorter events, 107.7 us)
Async XLA Ops:
  44.1 41.5 %collective-permute-start.56 = (bf16[2,256,128]{2,1,0:T(8,128)(2,1)}, bf16[2,256,128]{2,1,0:T(8,128)(2,1)S(1)}, u32[]{:S(2)}, u32[]{:S(2)}) collective-permute-start(bf16[2,256,128]{2,1,0:T(8,128)(2,1)} %get-tuple-element.267), channel_id=1, source_target_pairs={{0,6},{1,7},{2,4},{3,5},{4,2},{5,3},{6,0},{7,1},{8,14},{9,15},{10,... | collective-permute-start | bytes 393224 | tf_op jit(solution)/shard_map/ppermute | solution.py:230
  46.7 40.0 %collective-permute-start.57 = (bf16[2,256,128]{2,1,0:T(8,128)(2,1)}, bf16[2,256,128]{2,1,0:T(8,128)(2,1)S(1)}, u32[]{:S(2)}, u32[]{:S(2)}) collective-permute-start(bf16[2,256,128]{2,1,0:T(8,128)(2,1)} %get-tuple-element.268), channel_id=1, source_target_pairs={{0,4},{1,5},{2,6},{3,7},{4,0},{5,1},{6,2},{7,3},{8,12},{9,13},{10,... | collective-permute-start | bytes 393224 | tf_op jit(solution)/shard_map/ppermute | solution.py:230
  47.2 39.7 %collective-permute-start.58 = (bf16[2,256,128]{2,1,0:T(8,128)(2,1)}, bf16[2,256,128]{2,1,0:T(8,128)(2,1)S(1)}, u32[]{:S(2)}, u32[]{:S(2)}) collective-permute-start(bf16[2,256,128]{2,1,0:T(8,128)(2,1)} %get-tuple-element.269), channel_id=1, source_target_pairs={{0,2},{1,3},{2,0},{3,1},{4,6},{5,7},{6,4},{7,5},{8,10},{9,11},{10,... | collective-permute-start | bytes 393224 | tf_op jit(solution)/shard_map/ppermute | solution.py:230
  47.6 40.5 %collective-permute-start.59 = (bf16[2,256,128]{2,1,0:T(8,128)(2,1)}, bf16[2,256,128]{2,1,0:T(8,128)(2,1)S(1)}, u32[]{:S(2)}, u32[]{:S(2)}) collective-permute-start(bf16[2,256,128]{2,1,0:T(8,128)(2,1)} %get-tuple-element.270), channel_id=1, source_target_pairs={{0,7},{1,6},{2,5},{3,4},{4,3},{5,2},{6,1},{7,0},{8,15},{9,14},{10,... | collective-permute-start | bytes 393224 | tf_op jit(solution)/shard_map/ppermute | solution.py:230
  97.7 51.9 %collective-permute-start.21 = (bf16[2,1024,128]{2,1,0:T(8,128)(2,1)S(1)}, bf16[2,1024,128]{2,1,0:T(8,128)(2,1)S(1)}, u32[]{:S(2)}, u32[]{:S(2)}) collective-permute-start(bf16[2,1024,128]{2,1,0:T(8,128)(2,1)S(1)} %copy-done.52), channel_id=1, source_target_pairs={{0,6},{1,7},{2,4},{3,5},{4,2},{5,3},{6,0},{7,1},{8,14},{9,15},{10,... | collective-permute-start | bytes 1572872 | tf_op jit(solution)/shard_map/ppermute | solution.py:230
  102.6 48.3 %collective-permute-start.22 = (bf16[2,1024,128]{2,1,0:T(8,128)(2,1)}, bf16[2,1024,128]{2,1,0:T(8,128)(2,1)S(1)}, u32[]{:S(2)}, u32[]{:S(2)}) collective-permute-start(bf16[2,1024,128]{2,1,0:T(8,128)(2,1)} %get-tuple-element.182), channel_id=1, source_target_pairs={{0,4},{1,5},{2,6},{3,7},{4,0},{5,1},{6,2},{7,3},{8,12},{9,13},{10,... | collective-permute-start | bytes 1572872 | tf_op jit(solution)/shard_map/ppermute | solution.py:230
  107.4 43.6 %collective-permute-start.23 = (bf16[2,1024,128]{2,1,0:T(8,128)(2,1)}, bf16[2,1024,128]{2,1,0:T(8,128)(2,1)S(1)}, u32[]{:S(2)}, u32[]{:S(2)}) collective-permute-start(bf16[2,1024,128]{2,1,0:T(8,128)(2,1)} %get-tuple-element.183), channel_id=1, source_target_pairs={{0,2},{1,3},{2,0},{3,1},{4,6},{5,7},{6,4},{7,5},{8,10},{9,11},{10,... | collective-permute-start | bytes 1572872 | tf_op jit(solution)/shard_map/ppermute | solution.py:230
  108.4 44.2 %collective-permute-start.24 = (bf16[2,1024,128]{2,1,0:T(8,128)(2,1)S(1)}, bf16[2,1024,128]{2,1,0:T(8,128)(2,1)S(1)}, u32[]{:S(2)}, u32[]{:S(2)}) collective-permute-start(bf16[2,1024,128]{2,1,0:T(8,128)(2,1)S(1)} %copy-done.51), channel_id=1, source_target_pairs={{0,7},{1,6},{2,5},{3,4},{4,3},{5,2},{6,1},{7,0},{8,15},{9,14},{10,... | collective-permute-start | bytes 1572872 | tf_op jit(solution)/shard_map/ppermute | solution.py:230
  110.3 37.8 %collective-permute-start.28 = (bf16[2,512,128]{2,1,0:T(8,128)(2,1)S(1)}, bf16[2,512,128]{2,1,0:T(8,128)(2,1)}, u32[]{:S(2)}, u32[]{:S(2)}) collective-permute-start(bf16[2,512,128]{2,1,0:T(8,128)(2,1)S(1)} %shard_map.112), channel_id=1, source_target_pairs={{0,6},{1,7},{2,4},{3,5},{4,2},{5,3},{6,0},{7,1},{8,14},{9,15},{10,... | collective-permute-start | bytes 786440 | tf_op jit(solution)/shard_map/ppermute | solution.py:230
  148.1 45.7 %collective-permute-start.14 = (bf16[2,1280,128]{2,1,0:T(8,128)(2,1)}, bf16[2,1280,128]{2,1,0:T(8,128)(2,1)S(1)}, u32[]{:S(2)}, u32[]{:S(2)}) collective-permute-start(bf16[2,1280,128]{2,1,0:T(8,128)(2,1)} %get-tuple-element.174), channel_id=1, source_target_pairs={{0,6},{1,7},{2,4},{3,5},{4,2},{5,3},{6,0},{7,1},{8,14},{9,15},{10,... | collective-permute-start | bytes 1966088 | tf_op jit(solution)/shard_map/ppermute | solution.py:230
  149.5 45.0 %collective-permute-start.15 = (bf16[2,1280,128]{2,1,0:T(8,128)(2,1)}, bf16[2,1280,128]{2,1,0:T(8,128)(2,1)S(1)}, u32[]{:S(2)}, u32[]{:S(2)}) collective-permute-start(bf16[2,1280,128]{2,1,0:T(8,128)(2,1)} %get-tuple-element.175), channel_id=1, source_target_pairs={{0,4},{1,5},{2,6},{3,7},{4,0},{5,1},{6,2},{7,3},{8,12},{9,13},{10,... | collective-permute-start | bytes 1966088 | tf_op jit(solution)/shard_map/ppermute | solution.py:230
  150.9 39.6 %collective-permute-start.25 = (bf16[2,1024,128]{2,1,0:T(8,128)(2,1)S(1)}, bf16[2,1024,128]{2,1,0:T(8,128)(2,1)S(1)}, u32[]{:S(2)}, u32[]{:S(2)}) collective-permute-start(bf16[2,1024,128]{2,1,0:T(8,128)(2,1)S(1)} %copy-done.50), channel_id=1, source_target_pairs={{0,5},{1,4},{2,7},{3,6},{4,1},{5,0},{6,3},{7,2},{8,13},{9,12},{10,... | collective-permute-start | bytes 1572872 | tf_op jit(solution)/shard_map/ppermute | solution.py:230
  151.0 40.9 %collective-permute-start.26 = (bf16[2,1024,128]{2,1,0:T(8,128)(2,1)S(1)}, bf16[2,1024,128]{2,1,0:T(8,128)(2,1)}, u32[]{:S(2)}, u32[]{:S(2)}) collective-permute-start(bf16[2,1024,128]{2,1,0:T(8,128)(2,1)S(1)} %copy-done.49), channel_id=1, source_target_pairs={{0,3},{1,2},{2,1},{3,0},{4,7},{5,6},{6,5},{7,4},{8,11},{9,10},{10,... | collective-permute-start | bytes 1572872 | tf_op jit(solution)/shard_map/ppermute | solution.py:230
  152.6 40.0 %collective-permute-start.27 = (bf16[2,1024,128]{2,1,0:T(8,128)(2,1)S(1)}, bf16[2,1024,128]{2,1,0:T(8,128)(2,1)}, u32[]{:S(2)}, u32[]{:S(2)}) collective-permute-start(bf16[2,1024,128]{2,1,0:T(8,128)(2,1)S(1)} %copy-done.48), channel_id=1, source_target_pairs={{0,1},{1,0},{2,3},{3,2},{4,5},{5,4},{6,7},{7,6},{8,9},{9,8},{10,11... | collective-permute-start | bytes 1572872 | tf_op jit(solution)/shard_map/ppermute | solution.py:230
  191.9 29.5 %collective-permute-start.17 = (bf16[2,1280,128]{2,1,0:T(8,128)(2,1)}, bf16[2,1280,128]{2,1,0:T(8,128)(2,1)S(1)}, u32[]{:S(2)}, u32[]{:S(2)}) collective-permute-start(bf16[2,1280,128]{2,1,0:T(8,128)(2,1)} %get-tuple-element.177), channel_id=1, source_target_pairs={{0,7},{1,6},{2,5},{3,4},{4,3},{5,2},{6,1},{7,0},{8,15},{9,14},{10,... | collective-permute-start | bytes 1966088 | tf_op jit(solution)/shard_map/ppermute | solution.py:230
  192.6 30.4 %collective-permute-start.18 = (bf16[2,1280,128]{2,1,0:T(8,128)(2,1)}, bf16[2,1280,128]{2,1,0:T(8,128)(2,1)S(1)}, u32[]{:S(2)}, u32[]{:S(2)}) collective-permute-start(bf16[2,1280,128]{2,1,0:T(8,128)(2,1)} %get-tuple-element.178), channel_id=1, source_target_pairs={{0,5},{1,4},{2,7},{3,6},{4,1},{5,0},{6,3},{7,2},{8,13},{9,12},{10,... | collective-permute-start | bytes 1966088 | tf_op jit(solution)/shard_map/ppermute | solution.py:230
  193.8 41.7 %collective-permute-start.19 = (bf16[2,1280,128]{2,1,0:T(8,128)(2,1)}, bf16[2,1280,128]{2,1,0:T(8,128)(2,1)S(1)}, u32[]{:S(2)}, u32[]{:S(2)}) collective-permute-start(bf16[2,1280,128]{2,1,0:T(8,128)(2,1)} %get-tuple-element.179), channel_id=1, source_target_pairs={{0,3},{1,2},{2,1},{3,0},{4,7},{5,6},{6,5},{7,4},{8,11},{9,10},{10,... | collective-permute-start | bytes 1966088 | tf_op jit(solution)/shard_map/ppermute | solution.py:230
  194.6 42.1 %collective-permute-start.20 = (bf16[2,1280,128]{2,1,0:T(8,128)(2,1)}, bf16[2,1280,128]{2,1,0:T(8,128)(2,1)S(1)}, u32[]{:S(2)}, u32[]{:S(2)}) collective-permute-start(bf16[2,1280,128]{2,1,0:T(8,128)(2,1)} %get-tuple-element.180), channel_id=1, source_target_pairs={{0,1},{1,0},{2,3},{3,2},{4,5},{5,4},{6,7},{7,6},{8,9},{9,8},{10,11... | collective-permute-start | bytes 1966088 | tf_op jit(solution)/shard_map/ppermute | solution.py:230
  211.0 28.9 %collective-permute-start.42 = (bf16[2,256,128]{2,1,0:T(8,128)(2,1)S(1)}, bf16[2,256,128]{2,1,0:T(8,128)(2,1)S(1)}, u32[]{:S(2)}, u32[]{:S(2)}) collective-permute-start(bf16[2,256,128]{2,1,0:T(8,128)(2,1)S(1)} %get-tuple-element.252), channel_id=1, source_target_pairs={{0,6},{1,7},{2,4},{3,5},{4,2},{5,3},{6,0},{7,1},{8,14},{9,15},{10,... | collective-permute-start | bytes 393224 | tf_op jit(solution)/shard_map/ppermute | solution.py:230
  235.5 33.4 %collective-permute-start.49 = (bf16[2,640,128]{2,1,0:T(8,128)(2,1)S(1)}, bf16[2,640,128]{2,1,0:T(8,128)(2,1)S(1)}, u32[]{:S(2)}, u32[]{:S(2)}) collective-permute-start(bf16[2,640,128]{2,1,0:T(8,128)(2,1)S(1)} %copy-done.54), channel_id=1, source_target_pairs={{0,6},{1,7},{2,4},{3,5},{4,2},{5,3},{6,0},{7,1},{8,14},{9,15},{10,... | collective-permute-start | bytes 983048 | tf_op jit(solution)/shard_map/ppermute | solution.py:230
  236.7 32.7 %collective-permute-start.50 = (bf16[2,640,128]{2,1,0:T(8,128)(2,1)S(1)}, bf16[2,640,128]{2,1,0:T(8,128)(2,1)S(1)}, u32[]{:S(2)}, u32[]{:S(2)}) collective-permute-start(bf16[2,640,128]{2,1,0:T(8,128)(2,1)S(1)} %copy-done.53), channel_id=1, source_target_pairs={{0,4},{1,5},{2,6},{3,7},{4,0},{5,1},{6,2},{7,3},{8,12},{9,13},{10,... | collective-permute-start | bytes 983048 | tf_op jit(solution)/shard_map/ppermute | solution.py:230
  274.8 36.7 %collective-permute-start.37 = (bf16[2,128,128]{2,1,0:T(8,128)(2,1)S(1)}, bf16[2,128,128]{2,1,0:T(8,128)(2,1)S(1)}, u32[]{:S(2)}, u32[]{:S(2)}) collective-permute-start(bf16[2,128,128]{2,1,0:T(8,128)(2,1)S(1)} %get-tuple-element.246), channel_id=1, source_target_pairs={{0,2},{1,3},{2,0},{3,1},{4,6},{5,7},{6,4},{7,5},{8,10},{9,11},{10,... | collective-permute-start | bytes 196616 | tf_op jit(solution)/shard_map/ppermute | solution.py:230
  279.8 31.8 %collective-permute-start.38 = (bf16[2,128,128]{2,1,0:T(8,128)(2,1)S(1)}, bf16[2,128,128]{2,1,0:T(8,128)(2,1)S(1)}, u32[]{:S(2)}, u32[]{:S(2)}) collective-permute-start(bf16[2,128,128]{2,1,0:T(8,128)(2,1)S(1)} %get-tuple-element.247), channel_id=1, source_target_pairs={{0,7},{1,6},{2,5},{3,4},{4,3},{5,2},{6,1},{7,0},{8,15},{9,14},{10,... | collective-permute-start | bytes 196616 | tf_op jit(solution)/shard_map/ppermute | solution.py:230
  284.4 27.1 %collective-permute-start.39 = (bf16[2,128,128]{2,1,0:T(8,128)(2,1)S(1)}, bf16[2,128,128]{2,1,0:T(8,128)(2,1)S(1)}, u32[]{:S(2)}, u32[]{:S(2)}) collective-permute-start(bf16[2,128,128]{2,1,0:T(8,128)(2,1)S(1)} %get-tuple-element.248), channel_id=1, source_target_pairs={{0,5},{1,4},{2,7},{3,6},{4,1},{5,0},{6,3},{7,2},{8,13},{9,12},{10,... | collective-permute-start | bytes 196616 | tf_op jit(solution)/shard_map/ppermute | solution.py:230
  (97 other events, 1823.6 us)
